TPU v7x, 64 devices: a 2x2x8 block of a 4x4x8 slice. The times are simulated.
64 devices in a mesh: rep: 8 (over x, y, core), dp: 8 (over z).
Axes of the slice: x: 2, y: 2, z: 8, core: 2. Of those that a mesh axis runs over, the one named last changes fastest.
The devices are a block of a 4x4x8 slice.
Arguments:
- x: bfloat16 [64, 2048, 512], P(('rep', 'dp')), parts along dimension 0
- dy: bfloat16 [64, 2048, 512], P(('rep', 'dp')), parts along dimension 0
- w_gate: bfloat16 [2, 512, 2560], replicated
- w_up: bfloat16 [2, 512, 2560], replicated
- w_down: bfloat16 [2, 2560, 512], replicated
- m_w_gate: float32 [2, 512, 2560], replicated
- m_w_up: float32 [2, 512, 2560], replicated
- m_w_down: float32 [2, 2560, 512], replicated
- v_w_gate: float32 [2, 512, 2560], replicated
- v_w_up: float32 [2, 512, 2560], replicated
- v_w_down: float32 [2, 2560, 512], replicated
Outputs:
- output 1: bfloat16 [16, 512, 2560], P('rep'), parts along dimension 0
- output 2: bfloat16 [16, 512, 2560], P('rep'), parts along dimension 0
- output 3: bfloat16 [16, 2560, 512], P('rep'), parts along dimension 0
- output 4: float32 [16, 512, 2560], P('rep'), parts along dimension 0
- output 5: float32 [16, 512, 2560], P('rep'), parts along dimension 0
- output 6: float32 [16, 2560, 512], P('rep'), parts along dimension 0
- output 7: float32 [16, 512, 2560], P('rep'), parts along dimension 0
- output 8: float32 [16, 512, 2560], P('rep'), parts along dimension 0
- output 9: float32 [16, 2560, 512], P('rep'), parts along dimension 0
There are 8 independent parts. A program takes and returns all parts, laid end to end along the dimension named above; an argument that names none is the same for every part.
All inputs are finite; a program needn't handle non-finite values.
Results may differ from a plain program's by a relative error of at most 0.022.
Values are sent between devices in bfloat16 or wider.
A program may use at most 768 MiB of HBM per device.

v0:
```python
import jax
import jax.numpy as jnp
from jax import lax
from jax.sharding import PartitionSpec as P

NAMES = ("w_gate", "w_up", "w_down")


def matmul(a, w):
    return jnp.dot(a, w, preferred_element_type=jnp.float32).astype(jnp.bfloat16)


def normed(h):
    wide = h.astype(jnp.float32)
    scale = lax.rsqrt(jnp.mean(wide**2, -1, keepdims=True) + 1e-6)
    return (wide * scale).astype(jnp.bfloat16)


def layer(h, w):
    a = normed(h)
    gate = jnp.dot(a, w["w_gate"], preferred_element_type=jnp.float32)
    up = jnp.dot(a, w["w_up"], preferred_element_type=jnp.float32)
    return h + matmul((jax.nn.silu(gate) * up).astype(jnp.bfloat16), w["w_down"])


def adamw(w, m, v, g):
    m = 0.9 * m + 0.1 * g
    v = 0.95 * v + 0.05 * g * g
    step = m * lax.rsqrt(v + 1e-8) + 0.1 * w
    return (w - 0.02 * step).astype(jnp.bfloat16), m, v


def clipped(gradients, sum_of_squares, count):
    factor = jnp.minimum(1.0, 0.5 * lax.rsqrt(sum_of_squares / count + 1e-30))
    return [g * factor for g in gradients]


def solution(mesh):
    def step(x, dy, *arrays):
        weights, m, v = (arrays[i : i + 3] for i in (0, 3, 6))
        layers = weights[0].shape[0]
        h, kept = x[0], []
        for number in range(layers):
            kept.append(h)
            h = layer(h, {name: w[number] for name, w in zip(NAMES, weights, strict=True)})
        by_h, summed = dy[0], [None] * layers
        for number in reversed(range(layers)):
            _, back = jax.vjp(lambda w, h: layer(h, w), {name: w[number] for name, w in zip(NAMES, weights, strict=True)}, kept[number])
            by_w, by_h = back(by_h)
            summed[number] = [lax.psum(by_w[name], "dp") for name in NAMES]
        gradients = [jnp.stack([summed[number][i] for number in range(layers)]).astype(jnp.float32) for i in range(3)]
        gradients = clipped(gradients, sum(jnp.sum(g * g) for g in gradients), sum(g.size for g in gradients))
        new = [adamw(w.astype(jnp.float32), m, v, g) for w, m, v, g in zip(weights, m, v, gradients, strict=True)]
        return tuple(one[which] for which in range(3) for one in new)

    return jax.shard_map(
        step,
        mesh=mesh,
        in_specs=(P(("rep", "dp"), None, None),) * 2 + (P(None, None, None),) * 9,
        out_specs=(P("rep", None, None),) * 9,
        check_vma=False,
    )
```

profile of v0, /device:TPU:21, one launch (start us, length us, event | category | flops | bytes accessed | tf_op | source)
XLA Modules:
  0.0 637.9 jit_solution(2410316653829392069)
XLA Ops:
  7.2 0.1 all-reduce.3.cloned.1.call-start
  7.3 2.9 copy.20
  10.2 0.0 copy-start.3
  10.2 0.5 fusion.42
  10.7 4.2 copy.21
  14.8 10.4 %convolution_convert_fusion.1 = bf16[2048,2560]{1,0:T(8,128)(2,1)} fusion(bf16[2,2560,512]{2,1,0:T(8,128)(2,1)} %param.15, bf16[1,2048,512]{2,1,0:T(8,128)(2,1)} %param.12), kind=kOutput, calls=%fused_computation.41 | convolution fusion | flops 5373952000 | bytes 15204352 | tf_op jit(solution)/shard_map/transpose(jvp())/dot_general | solution.py:10
  25.2 11.6 %fusion.70 = f32[2048,2560]{1,0:T(8,128)} fusion(bf16[2,512,2560]{2,1,0:T(8,128)(2,1)} %param.13, bf16[1,2048,512]{2,1,0:T(8,128)(2,1)S(1)} %copy-done.6, f32[2048]{0:T(1024)S(1)} %add_rsqrt_fusion), kind=kOutput, calls=%fused_computation.106 | convolution fusion | flops 5371854848 | bytes 25698304 | tf_op jit(solution)/shard_map/dot_general | solution.py:21
  36.9 18.9 %multiply_convert_fusion.1 = (bf16[2048,2560]{1,0:T(8,128)(2,1)}, f32[2048,2560]{1,0:T(8,128)}) fusion(f32[2048,2560]{1,0:T(8,128)} %fusion.70, bf16[2,512,2560]{2,1,0:T(8,128)(2,1)} %param.14, bf16[1,2048,512]{2,1,0:T(8,128)(2,1)} %param.11, f32[2048]{0:T(1024)S(1)} %add_rsqrt_fusion), kind=kOutput, calls=%fused_computation.17 | convolution fusion | flops 5403312128 | bytes 57155584 | tf_op jit(solution)/shard_map/dot_general | solution.py:22
  55.8 9.3 %fusion.46 = (f32[2048]{0:T(1024)S(1)}, bf16[2048,512]{0,1:T(8,128)(2,1)S(1)}) fusion(bf16[2048,2560]{1,0:T(8,128)(2,1)} %get-tuple-element.24, bf16[2,2560,512]{2,1,0:T(8,128)(2,1)} %param.15, bf16[1,2048,512]{1,2,0:T(8,128)(2,1)S(1)} %copy.20), kind=kOutput, calls=%fused_computation.82 | convolution fusion | flops 5373949952 | bytes 17309696 | tf_op jit(solution)/shard_map/dot_general | solution.py:10
  65.1 0.6 copy-done.10
  65.7 0.7 copy-done.8
  66.4 11.8 %fusion.59 = f32[2048,2560]{1,0:T(8,128)} fusion(bf16[2,512,2560]{2,1,0:T(8,128)(2,1)} %param.14, bf16[2048,512]{0,1:T(8,128)(2,1)S(1)} %get-tuple-element.27, f32[2048]{0:T(1024)S(1)} %fusion.99), kind=kOutput, calls=%fused_computation.95 | convolution fusion | flops 5371854848 | bytes 25698304 | tf_op jit(solution)/shard_map/jvp()/dot_general | solution.py:22
  78.3 29.3 %fusion.2 = (bf16[2048,2560]{1,0:T(8,128)(2,1)}, f32[2048,2560]{1,0:T(8,128)}) fusion(f32[2048,2560]{1,0:T(8,128)} %fusion.59, bf16[2048,2560]{1,0:T(8,128)(2,1)} %convolution_convert_fusion.1, bf16[2,512,2560]{2,1,0:T(8,128)(2,1)} %param.13, bf16[2048,512]{0,1:T(8,128)(2,1)} %copy-done.8, f32[2048]{0:T(1024)S(1)} %fusion.99), kind=kOutput, calls=%fused_computation.8 | convolution fusion | flops 5434769408 | bytes 67641344 | tf_op jit(solution)/shard_map/jvp()/dot_general | solution.py:21
  107.6 15.3 %fusion.58 = bf16[2048,512]{0,1:T(8,128)(2,1)} fusion(bf16[2048,2560]{1,0:T(8,128)(2,1)} %convolution_convert_fusion.1, bf16[2,512,2560]{2,1,0:T(8,128)(2,1)} %param.14, f32[2048,2560]{1,0:T(8,128)} %get-tuple-element.29), kind=kOutput, calls=%fused_computation.92 | convolution fusion | flops 5401214976 | bytes 36175872 | tf_op jit(solution)/shard_map/transpose(jvp())/dot_general | solution.py:22
  122.9 18.0 %fusion.56 = bf16[1,2560,512]{2,1,0:T(8,128)(2,1)} fusion(f32[2048,2560]{1,0:T(8,128)} %fusion.59, bf16[1,2048,512]{2,1,0:T(8,128)(2,1)S(1)} %copy-done.7, f32[2048,2560]{1,0:T(8,128)} %get-tuple-element.29), kind=kOutput, calls=%fused_computation.91 | convolution fusion | flops 5401477120 | bytes 46661632 | tf_op jit(solution)/shard_map/transpose(jvp())/dot_general | solution.py:10
  140.9 11.6 %fusion.48 = (f32[2048]{0:T(1024)S(1)}, bf16[2048,512]{0,1:T(8,128)(2,1)S(1)}) fusion(bf16[2048,512]{0,1:T(8,128)(2,1)} %copy-done.8, bf16[2048,512]{0,1:T(8,128)(2,1)} %fusion.58, bf16[2048,2560]{1,0:T(8,128)(2,1)} %get-tuple-element.28, bf16[2,512,2560]{2,1,0:T(8,128)(2,1)} %param.13), kind=kOutput, calls=%fused_computation.84 | convolution fusion | flops 5373949952 | bytes 19406848 | tf_op jit(solution)/shard_map/transpose(jvp())/dot_general | solution.py:21
  152.6 0.0 slice-start
  152.6 1.4 fusion.88
  154.0 0.0 slice-start.1
  154.0 7.0 %fusion.50 = bf16[1,2560,512]{2,1,0:T(8,128)(2,1)} fusion(bf16[2048,2560]{1,0:T(8,128)(2,1)S(1)} %copy-done.14, bf16[2048,512]{0,1:T(8,128)(2,1)S(1)} %fusion.88), kind=kOutput, calls=%fused_computation.87 | convolution fusion | flops 5370019840 | bytes 15204352 | tf_op jit(solution)/shard_map/transpose(jvp())/dot_general | solution.py:10
  161.0 8.5 %convolution_convert_fusion = bf16[2048,2560]{1,0:T(8,128)(2,1)} fusion(bf16[2048,512]{0,1:T(8,128)(2,1)S(1)} %fusion.88, bf16[2,2560,512]{2,1,0:T(8,128)(2,1)S(1)} %bitcast.75), kind=kOutput, calls=%fused_computation.40 | convolution fusion | flops 5373952000 | bytes 15204352 | tf_op jit(solution)/shard_map/transpose(jvp())/dot_general | solution.py:10
  169.5 14.6 %fusion.55 = bf16[1,512,2560]{2,1,0:T(8,128)(2,1)} fusion(bf16[2048,2560]{1,0:T(8,128)(2,1)} %convolution_convert_fusion.1, bf16[2048,512]{0,1:T(8,128)(2,1)S(1)} %copy-done.9, f32[2048]{0:T(1024)S(1)} %fusion.99, f32[2048,2560]{1,0:T(8,128)} %get-tuple-element.29), kind=kOutput, calls=%fused_computation.90 | convolution fusion | flops 5404622848 | bytes 36184064 | tf_op jit(solution)/shard_map/transpose(jvp())/dot_general | solution.py:22
  184.0 11.0 %fusion.49 = bf16[1,512,2560]{2,1,0:T(8,128)(2,1)} fusion(bf16[2048,2560]{1,0:T(8,128)(2,1)} %get-tuple-element.28, bf16[2048,512]{0,1:T(8,128)(2,1)S(1)} %copy-done.9, f32[2048]{0:T(1024)S(1)} %fusion.99), kind=kOutput, calls=%fused_computation.86 | convolution fusion | flops 5371854848 | bytes 15212544 | tf_op jit(solution)/shard_map/transpose(jvp())/dot_general | solution.py:21
  195.0 14.8 %fusion.51 = bf16[1,512,2560]{2,1,0:T(8,128)(2,1)} fusion(bf16[2048,2560]{1,0:T(8,128)(2,1)} %convolution_convert_fusion, f32[2048,2560]{1,0:T(8,128)} %fusion.70, bf16[1,2048,512]{1,2,0:T(8,128)(2,1)S(1)} %copy-done.4, f32[2048]{0:T(1024)S(1)} %copy-done.13), kind=kOutput, calls=%fused_computation.88 | convolution fusion | flops 5404622848 | bytes 36184064 | tf_op jit(solution)/shard_map/transpose(jvp())/dot_general | solution.py:22
  209.8 21.2 %fusion.52 = bf16[1,512,2560]{2,1,0:T(8,128)(2,1)} fusion(f32[2048,2560]{1,0:T(8,128)} %fusion.70, f32[2048,2560]{1,0:T(8,128)} %get-tuple-element.25, bf16[2048,2560]{1,0:T(8,128)(2,1)} %convolution_convert_fusion, bf16[1,2048,512]{1,2,0:T(8,128)(2,1)S(1)} %copy-done.4, f32[2048]{0:T(1024)S(1)} %copy-done.13), kind=kOutput, calls=%fused_computation.89 | convolution fusion | flops 5430837248 | bytes 57155584 | tf_op jit(solution)/shard_map/transpose(jvp())/dot_general | solution.py:21
  231.0 0.1 all-reduce.3.cloned.1.call-update
  231.1 324.1 %all-reduce.3.cloned.1.call-done = (bf16[1,512,2560]{2,1,0:T(8,128)(2,1)}, bf16[1,512,2560]{2,1,0:T(8,128)(2,1)}, bf16[1,512,2560]{2,1,0:T(8,128)(2,1)}, bf16[1,...) async-done(((bf16[1,512,2560]{2,1,0:T(8,128)(2,1)}, bf16[1,512,2560]{2,1,0:T(8,128)(2,1)}, bf16[1,512,2560]{2,1,0:T(8,128)(2,1)}, ...) | async-done | bytes 15728656 | tf_op jit(solution)/shard_map/psum | solution.py:50
  555.3 6.0 fusion.24
  561.2 5.8 fusion.23
  567.1 3.3 fusion.22
  572.4 21.3 %fusion.30 = (bf16[2,2560,512]{2,1,0:T(8,128)(2,1)}, f32[2,2560,512]{2,1,0:T(8,128)}, f32[2,2560,512]{2,1,0:T(8,128)}) fusion(bf16[2,2560,512]{2,1,0:T(8,128)(2,1)} %param.15, f32[]{:T(128)S(6)} %min_shard_map.3, bf16[1,2560,512]{2,1,0:T(8,128)(2,1)S(1)} %copy-done, bf16[1,2560,512]{2,1,0:T(8,128)(2,1)} %get-tuple-element.14, f32[2,2560,512]{2,1,0:T(8,128)} %param.21, ...), kind=kLoop, calls=%fused_computation.56 | loop fusion | flops 52428800 | bytes 57671684 | tf_op jit(solution)/shard_map/convert_element_type | solution.py:30
  593.7 36.8 %fusion.21 = (bf16[2,512,2560]{2,1,0:T(8,128)(2,1)}, f32[2,512,2560]{2,1,0:T(8,128)}, f32[2,512,2560]{2,1,0:T(8,128)}, bf16[2,512,2560]{2,1,0:T(8,128)(2,1)}, f3...) fusion(bf16[2,512,2560]{2,1,0:T(8,128)(2,1)} %param.13, f32[]{:T(128)S(6)} %min_shard_map.3, ...), kind=kLoop, calls=%fused_computation.47 | loop fusion | flops 104857600 | bytes 115343360 | tf_op jit(solution)/shard_map/convert_element_type | solution.py:30
  (33 shorter events, 0.1 us)
Async XLA Ops:
  7.2 548.1 %all-reduce.3.cloned.1.call-start = ((), (), s32[]{:S(2)}) async-start(), calls=%async_computation | async-start | bytes 31457280 | tf_op jit(solution)/shard_map/psum | solution.py:50
  10.2 45.6 %copy-start.3 = (bf16[1,2048,512]{1,2,0:T(8,128)(2,1)}, bf16[1,2048,512]{1,2,0:T(8,128)(2,1)S(1)}, u32[]{:S(2)}) copy-start(bf16[1,2048,512]{1,2,0:T(8,128)(2,1)S(1)} %copy.20) | copy-start | bytes 6291460
  10.7 26.2 %copy-start.12 = (f32[2048]{0:T(1024)}, f32[2048]{0:T(1024)S(1)}, u32[]{:S(2)}) copy-start(f32[2048]{0:T(1024)S(1)} %add_rsqrt_fusion) | copy-start | bytes 24580
  14.8 10.4 %copy-start.6 = (bf16[1,2048,512]{2,1,0:T(8,128)(2,1)S(1)}, bf16[1,2048,512]{2,1,0:T(8,128)(2,1)}, u32[]{:S(2)}) copy-start(bf16[1,2048,512]{2,1,0:T(8,128)(2,1)} %param.11) | copy-start | bytes 6291460
  65.1 0.6 copy-start.10
  65.1 1.3 copy-start.8
  107.6 15.3 %copy-start.7 = (bf16[1,2048,512]{2,1,0:T(8,128)(2,1)S(1)}, bf16[1,2048,512]{2,1,0:T(8,128)(2,1)}, u32[]{:S(2)}) copy-start(bf16[1,2048,512]{2,1,0:T(8,128)(2,1)} %param.12) | copy-start | bytes 6291460
  140.9 11.6 %copy-start.11 = (f32[2048]{0:T(1024)S(1)}, f32[2048]{0:T(1024)}, u32[]{:S(2)}) copy-start(f32[2048]{0:T(1024)} %copy-done.10) | copy-start | bytes 24580
  140.9 11.6 %copy-start.5 = (bf16[1,2048,512]{1,2,0:T(8,128)(2,1)S(1)}, bf16[1,2048,512]{1,2,0:T(8,128)(2,1)}, u32[]{:S(2)}) copy-start(bf16[1,2048,512]{1,2,0:T(8,128)(2,1)} %copy.21) | copy-start | bytes 6291460
  140.9 11.6 %copy-start.9 = (bf16[2048,512]{0,1:T(8,128)(2,1)S(1)}, bf16[2048,512]{0,1:T(8,128)(2,1)}, u32[]{:S(2)}) copy-start(bf16[2048,512]{0,1:T(8,128)(2,1)} %copy-done.8) | copy-start | bytes 6291460
  140.9 13.0 %copy-start.14 = (bf16[2048,2560]{1,0:T(8,128)(2,1)S(1)}, bf16[2048,2560]{1,0:T(8,128)(2,1)}, u32[]{:S(2)}) copy-start(bf16[2048,2560]{1,0:T(8,128)(2,1)} %get-tuple-element.24) | copy-start | bytes 31457284
  152.6 8.4 %slice-start = ((s8[5242880]{0:T(1024)(128)(4,1)}), s8[4194304]{0:T(1024)(128)(4,1)S(1)}, s32[]{:S(2)}) async-start(s8[5242880]{0:T(1024)(128)(4,1)} %bitcast.74), calls=%async_computation.1 | async-start | bytes 8388608
  154.0 7.0 %slice-start.1 = ((s8[5242880]{0:T(1024)(128)(4,1)}), s8[1048576]{0:T(1024)(128)(4,1)S(1)}, s32[]{:S(2)}) async-start(s8[5242880]{0:T(1024)(128)(4,1)} %bitcast.74), calls=%async_computation.2 | async-start | bytes 2097152
  184.0 11.0 %copy-start.4 = (bf16[1,2048,512]{1,2,0:T(8,128)(2,1)S(1)}, bf16[1,2048,512]{1,2,0:T(8,128)(2,1)}, u32[]{:S(2)}) copy-start(bf16[1,2048,512]{1,2,0:T(8,128)(2,1)} %copy-done.3) | copy-start | bytes 6291460
  184.0 11.0 %copy-start.13 = (f32[2048]{0:T(1024)S(1)}, f32[2048]{0:T(1024)}, u32[]{:S(2)}) copy-start(f32[2048]{0:T(1024)} %copy-done.12) | copy-start | bytes 24580
  555.2 11.8 %copy-start.1 = (bf16[1,512,2560]{2,1,0:T(8,128)(2,1)S(1)}, bf16[1,512,2560]{2,1,0:T(8,128)(2,1)}, u32[]{:S(2)}) copy-start(bf16[1,512,2560]{2,1,0:T(8,128)(2,1)} %get-tuple-element.9) | copy-start | bytes 7864324
  555.2 11.8 %copy-start.2 = (bf16[1,512,2560]{2,1,0:T(8,128)(2,1)S(1)}, bf16[1,512,2560]{2,1,0:T(8,128)(2,1)}, u32[]{:S(2)}) copy-start(bf16[1,512,2560]{2,1,0:T(8,128)(2,1)} %get-tuple-element.10) | copy-start | bytes 7864324
  555.3 17.1 %copy-start = (bf16[1,2560,512]{2,1,0:T(8,128)(2,1)S(1)}, bf16[1,2560,512]{2,1,0:T(8,128)(2,1)}, u32[]{:S(2)}) copy-start(bf16[1,2560,512]{2,1,0:T(8,128)(2,1)} %get-tuple-element.13) | copy-start | bytes 7864324
Sparse Core Ops, SparseCore 0:
  231.2 323.9 all-reduce.2
where the time goes:
time: 647 us; the launch traced here: 638 us
  waiting for transfers between devices  324 us (50%)
  matrix products  213 us (33%)
  other arithmetic  75.1 us (12%)
  between operations  16.8 us (3%)
  local copies, waits for them, and re-layouts  8.48 us (1%)
    psum x1, waiting for transfers between devices, step(): summed[number] = [lax.psum(by_w[name], 'dp') for name in NAMES]  324 us
    dot_general x5, matrix products, layer(): gate = jnp.dot(a, w['w_gate'], preferred_element_type=jnp.float32)  84.7 us
    dot_general x5, matrix products, layer(): up = jnp.dot(a, w['w_up'], preferred_element_type=jnp.float32)  75.4 us
    convert_element_type x2, other arithmetic, adamw(): return ((w - 0.02 * step).astype(jnp.bfloat16), m, v)  58.2 us
    dot_general x5, matrix products, matmul(): jnp.dot(a, w, preferred_element_type=jnp.float32).astype(jnp.bfloat16)  53.1 us
    reduce_sum x3, other arithmetic, step(): jnp.sum(g * g)  15.1 us
  transfers between devices with their start and end apart: 1, of which 1 were waited for; matrix products, arithmetic and copies ran while one was open for 0% of the time, Pallas kernels for 0%

commit v1 on v0

v1 whole, which is shorter than its diff:
```python
import functools

import jax
import jax.numpy as jnp
from jax import lax
from jax.experimental import pallas as pl
from jax.experimental.pallas import tpu as pltpu
from jax.sharding import PartitionSpec as P

f32, bf16 = jnp.float32, jnp.bfloat16
MESH = pl.DeviceIdType.MESH
FC = 256
SLOTS = 4
HELD = 7
EARLY = 3
TILE = 1024


def dot(a, b):
    return jnp.dot(a, b, preferred_element_type=f32)


def dot_nt(a, b):
    return lax.dot_general(a, b, (((1,), (1,)), ((), ())), preferred_element_type=f32)


def sigmoid(x):
    return 0.5 * jnp.tanh(0.5 * x) + 0.5


def loop(n, body):
    lax.fori_loop(0, n, lambda i, c: (body(i), c)[1], 0)


def train_kernel(n, rounds, x, dy, wg_h, wu_h, wd_h, G, L0, L1, sq_out, A0, A1, AT, H, DY, DYT, ACC, HID, DGU, WGU, WD, PART, RECV, SQ, SQA,
                 in_sem, w_sem, rs_s, rs_r, ag_s, ag_r, own_sem, sq_s, sq_r):
    _, tokens, d = x.shape
    layers, _, ff = wg_h.shape
    chunks = ff // FC
    units = layers * chunks
    last = (L0, L1)
    rows_p, rows_d = d // (2 * n), FC // (2 * n)
    me, rep = lax.axis_index("dp"), lax.axis_index("rep")
    to = (lax.rem(me + 1, n), lax.rem(me + n - 1, n))
    sign = (-1, 1)
    step_rows = tokens // 4

    bar = pltpu.get_barrier_semaphore()
    for k in range(1, n):
        pl.semaphore_signal(bar, inc=1, device_id=(rep, lax.rem(me + k, n)), device_id_type=MESH)

    def w_copies(i):
        slot = lax.rem(i, SLOTS)
        ly = jnp.where(i // chunks == 1, layers - 1, 0)
        c = pl.ds(pl.multiple_of(lax.rem(i, chunks) * FC, FC), FC)
        return (
            pltpu.make_async_copy(wg_h.at[ly, :, c], WGU.at[slot, :, 0:FC], w_sem.at[slot, 0]),
            pltpu.make_async_copy(wu_h.at[ly, :, c], WGU.at[slot, :, FC : 2 * FC], w_sem.at[slot, 1]),
            pltpu.make_async_copy(wd_h.at[ly, c, :], WD.at[slot], w_sem.at[slot, 2]),
        )

    def w_start(i):
        for c in w_copies(i):
            c.start()

    def w_wait(i):
        for c in w_copies(i):
            c.wait()

    x_in = pltpu.make_async_copy(x.at[0], H, in_sem.at[0])
    dy_in = pltpu.make_async_copy(dy.at[0], DY, in_sem.at[1])
    x_in.start()
    w_start(0)
    w_start(1)
    dy_in.start()

    def rows(t):
        return pl.ds(pl.multiple_of(t * step_rows, step_rows), step_rows)

    def scale_of(w):
        return lax.rsqrt(jnp.mean(w * w, -1, keepdims=True) + 1e-6)

    x_in.wait()

    def norm_x(t):
        w = H[rows(t), :].astype(f32)
        A0[rows(t), :] = (w * scale_of(w)).astype(bf16)

    loop(4, norm_x)
    ACC[...] = jnp.zeros_like(ACC)

    def forward(i):
        w_wait(2 * i)
        w_wait(2 * i + 1)
        w_start(2 * i + 2)
        w_start(2 * i + 3)
        total = None
        for k in range(2):
            slot = lax.rem(2 * i + k, SLOTS)
            gu = dot(A0[...], WGU[slot])
            g, u = gu[:, :FC], gu[:, FC:]
            part = dot((g * sigmoid(g) * u).astype(bf16), WD[slot])
            total = part if total is None else total + part
        ACC[...] += total

    loop(chunks // 2, forward)
    dy_in.wait()

    def between(t):
        r = rows(t)
        h = (H[r, :].astype(f32) + ACC[r, :].astype(bf16).astype(f32)).astype(bf16)
        H[r, :] = h
        w = h.astype(f32)
        a = (w * scale_of(w)).astype(bf16)
        A1[r, :] = a
        AT[:, r] = a.T
        DYT[:, r] = DY[r, :].T
        ACC[r, :] = jnp.zeros((step_rows, d), f32)

    loop(4, between)
    pl.semaphore_wait(bar, n - 1)

    def piece(s, h):
        return 2 * lax.rem(me + sign[h] * (1 + s) + 2 * n, n) + h

    def rs_copy(u, s, h):
        return pltpu.make_async_remote_copy(PART.at[u, piece(s, h)], RECV.at[u, s, h], rs_s.at[u, s, h], rs_r.at[u, s, h],
                                            device_id=(rep, to[h]), device_id_type=MESH)

    def rs_take(u, s, h):
        rs_copy(u, s, h).wait_recv()
        p = piece(s + 1, h)
        total = (PART[u, p].astype(f32) + RECV[u, s, h].astype(f32)).astype(bf16)
        PART[u, p] = total
        return total

    def rs_event(u, s):
        @pl.when(s < n - 1)
        def _():
            for h in (0, 1):
                rs_take(u, s - 1, h)
            for h in (0, 1):
                rs_copy(u, s, h).start()

        @pl.when(s == n - 1)
        def _():
            for h in (0, 1):
                g = rs_take(u, n - 2, h).astype(f32)
                SQ[...] += g * g
                own_copy(u, h).start()

    def own_copy(u, h):
        return pltpu.make_async_copy(PART.at[u, 2 * me + h], G.at[h, 0, u], own_sem.at[u, h])

    def done(u, i):
        return jnp.where(i <= EARLY, 2 * (i - u) + 1, (i - u) + 1 + jnp.maximum(EARLY - u, 0))

    def events(i, second, lo, hi):
        def one(q):
            u = i - hi + q
            s = done(u, i - 1) + second

            @pl.when((u >= 0) & (u < units) & (s < n) & (s < done(u, i)))
            def _():
                rs_event(u, s)

        loop(hi - lo + 1, one)

    def backward(ly, A, i):
        w_wait(i + chunks)

        @pl.when(i + 2 < units)
        def _():
            w_start(i + chunks + 2)

        slot = lax.rem(i + chunks, SLOTS)
        wgu, wd = WGU.at[slot], WD.at[slot]

        def tile(t):
            r = pl.ds(pl.multiple_of(t * TILE, TILE), TILE)
            gu = dot(A[r, :], wgu[...])
            g, u = gu[:, :FC], gu[:, FC:]
            by_hid = dot_nt(DY[r, :], wd[...]).astype(bf16).astype(f32)
            sg = sigmoid(g)
            sl = g * sg
            HID[r, :] = (sl * u).astype(bf16)
            DGU[r, FC : 2 * FC] = (by_hid * sl).astype(bf16)
            DGU[r, 0:FC] = (by_hid * u * (sg + sl * (1 - sg))).astype(bf16)

        loop(tokens // TILE, tile)
        events(i, 0, 4, 7)
        wdt = dot(DYT[...], HID[...]).astype(bf16).T
        for k in range(d // FC):
            PART[i, :, 2 * rows_p + k * rows_d : 2 * rows_p + (k + 1) * rows_d] = wdt[:, k * FC : (k + 1) * FC].reshape(2 * n, rows_d, FC)
        events(i, 0, 1, 3)
        gw = dot(AT[...], DGU[...]).astype(bf16)
        PART[i, :, 0:rows_p] = gw[:, :FC].reshape(2 * n, rows_p, FC)
        PART[i, :, rows_p : 2 * rows_p] = gw[:, FC:].reshape(2 * n, rows_p, FC)

        for h in (0, 1):
            rs_copy(i, 0, h).start()
        if ly:
            ACC[...] += dot_nt(DGU[...], wgu[...])
            events(i, 1, 1, 3)

    SQ[...] = jnp.zeros_like(SQ)
    loop(chunks, functools.partial(backward, 1, A1))

    def by_input(t):
        r = rows(t)
        w, da = H[r, :].astype(f32), ACC[r, :].astype(bf16).astype(f32)
        s = scale_of(w)
        along = jnp.sum(da * w, -1, keepdims=True) * (s * s * s) * (1.0 / d)
        by_h = (DY[r, :].astype(f32) + (da * s - w * along).astype(bf16).astype(f32)).astype(bf16)
        DY[r, :] = by_h
        DYT[:, r] = by_h.T
        AT[:, r] = A0[r, :].T

    loop(4, by_input)
    loop(chunks, lambda i: backward(0, A0, i + chunks))

    def ag_copy(u, j, h, dst):
        src = PART.at[u, 2 * me + h] if isinstance(j, int) and j == 0 else G.at[h, j, u]
        return pltpu.make_async_remote_copy(src, dst, ag_s.at[u, j, h], ag_r.at[u, j, h], device_id=(rep, to[h]), device_id_type=MESH)

    per = -(-units // (n - 1))

    def drain(i):
        def one(q):
            u = units + i - n + 1 + q
            s = n - 1 - q

            @pl.when(u < units)
            def _():
                rs_event(u, s)

        loop(n - 1, one)

        def first(k):
            u = i * per + k

            @pl.when(u < units)
            def _():
                for h in (0, 1):
                    ag_copy(u, 0, h, G.at[h, 1, u]).start()

        loop(per, first)

    loop(n - 1, drain)

    lanes = SQA.shape[-1]
    q = SQ[...]
    q = sum(q[:, k * lanes : (k + 1) * lanes] for k in range(FC // lanes))
    SQA[me] = q.reshape(-1, 8, lanes).sum(0)

    def sq_copy(k, slot):
        return pltpu.make_async_remote_copy(SQA.at[me], SQA.at[me], sq_s.at[k], sq_r.at[k], device_id=(rep, lax.rem(me + k, n)), device_id_type=MESH)

    for k in range(1, n):
        sq_copy(k, None).start()

    def gather(t):
        j, u = t // units, lax.rem(t, units)
        for h in (0, 1):
            ag_copy(u, j, h, G.at[h, j + 1, u]).wait_recv()
            ag_copy(u, j + 1, h, G.at[h, j + 2, u]).start()

    loop((rounds - 2) * units, gather)

    def gather_last(u):
        for h in (0, 1):
            ag_copy(u, rounds - 2, h, G.at[h, rounds - 1, u]).wait_recv()
            ag_copy(u, rounds - 1, h, last[h].at[u]).start()

    loop(units, gather_last)

    def sq_from(k):
        src = lax.rem(me + n - k, n)
        return pltpu.make_async_remote_copy(SQA.at[src], SQA.at[src], sq_s.at[k], sq_r.at[k], device_id=(rep, lax.rem(me + k, n)), device_id_type=MESH)

    for k in range(1, n):
        sq_from(k).wait_recv()
    total = SQA[0]
    for k in range(1, n):
        total = total + SQA[k]
    sq_out[...] = jnp.broadcast_to(jnp.sum(total, keepdims=True), sq_out.shape)

    def finish(u):
        for h in (0, 1):
            ag_copy(u, rounds - 1, h, last[h].at[u]).wait_recv()
            own_copy(u, h).wait()

        def sends(s):
            for h in (0, 1):
                rs_copy(u, s, h).wait_send()

        loop(n - 1, sends)

        def sends2(j):
            for h in (0, 1):
                ag_copy(u, j, h, G.at[h, 1, u]).wait_send()

        loop(rounds, sends2)

    loop(units, finish)
    for k in range(1, n):
        sq_copy(k, None).wait_send()


def train(n, rounds, x, dy, w_gate, w_up, w_down):
    _, tokens, d = x.shape
    layers, _, ff = w_gate.shape
    units, rows = layers * ff // FC, 3 * d // (2 * n)
    part = (rows, FC)
    any_ = pl.BlockSpec(memory_space=pl.ANY)
    got = jax.ShapeDtypeStruct((units,) + part, bf16)
    act = pltpu.VMEM((tokens, d), bf16)
    act_t = pltpu.VMEM((d, tokens), bf16)
    dma = pltpu.SemaphoreType.DMA
    return pl.pallas_call(
        functools.partial(train_kernel, n, rounds),
        name="train",
        out_shape=(jax.ShapeDtypeStruct((2, rounds, units) + part, bf16), got, got, jax.ShapeDtypeStruct((8, 128), f32)),
        in_specs=[any_] * 5,
        out_specs=(any_, any_, any_, pl.BlockSpec(memory_space=pltpu.VMEM)),
        scratch_shapes=[
            act, act, act_t, act, act, act_t,
            pltpu.VMEM((tokens, d), f32),
            pltpu.VMEM((tokens, FC), bf16),
            pltpu.VMEM((tokens, 2 * FC), bf16),
            pltpu.VMEM((SLOTS, d, 2 * FC), bf16),
            pltpu.VMEM((SLOTS, FC, d), bf16),
            pltpu.VMEM((units, 2 * n) + part, bf16),
            pltpu.VMEM((units, n - 1, 2) + part, bf16),
            pltpu.VMEM(part, f32),
            pltpu.VMEM((n, 8, 128), f32),
            dma((2,)), dma((SLOTS, 3)),
            dma((units, n - 1, 2)), dma((units, n - 1, 2)),
            dma((units, rounds, 2)), dma((units, rounds, 2)),
            dma((units, 2)), dma((n,)), dma((n,)),
        ],
        compiler_params=pltpu.CompilerParams(collective_id=0, has_side_effects=True, vmem_limit_bytes=67043328),
        cost_estimate=pl.CostEstimate(flops=17 * 2 * tokens * d * ff, bytes_accessed=8 * units * n * rows * FC, transcendentals=0),
    )(x, dy, w_gate, w_up, w_down)


def adam_kernel(n_src, count, source, aliased, index, sq, *refs):
    gs, refs = refs[:n_src], refs[n_src:]
    w, m, v = refs[0:3], refs[3:6], refs[6:9]
    outs = refs[9 + (9 if aliased else 0) :]
    i = pl.program_id(0)
    factor = jnp.minimum(1.0, 0.5 * lax.rsqrt(sq[0:1, 0:1] / count + 1e-30))

    def update(g, k, at):
        g = g.astype(f32) * factor
        new_m = 0.9 * m[k][at] + 0.1 * g
        new_v = 0.95 * v[k][at] + 0.05 * g * g
        old = w[k][at].astype(f32)
        outs[k][at] = (old - 0.02 * (new_m * lax.rsqrt(new_v + 1e-8) + 0.1 * old)).astype(bf16)
        outs[3 + k][at] = new_m
        outs[6 + k][at] = new_v

    def run(g):
        rows_p, rows_d, d = w[0].shape[2], w[2].shape[3], w[2].shape[4]
        for c in range(w[2].shape[1]):
            cols = slice(c * FC, (c + 1) * FC)
            for k in range(2):
                update(g[c, k * rows_p : (k + 1) * rows_p], k, (0, 0, slice(None), cols))
            for k in range(d // FC):
                at = 2 * rows_p + k * rows_d
                update(g[c, at : at + rows_d], 2, (0, c, 0, slice(None), slice(k * FC, (k + 1) * FC)))

    if n_src == 1:
        run(gs[0].at[0, 0] if len(gs[0].shape) == 5 else gs[0])
    else:
        for k in range(n_src):
            pl.when(source(i) == k)(functools.partial(run, gs[k]))


def adam(views, prev, sq, gs, pieces, count, held=None):
    w, m, v = views
    layers, parts, rows_p, ff = w[0].shape
    _, chunks, _, rows_d, d = w[2].shape
    steps = 2 * (held[1] if held else 1)

    wide = pl.BlockSpec((1, 1, rows_p, ff), lambda i, ly, index: (ly, index[i], 0, 0))
    tall = pl.BlockSpec((1, chunks, 1, rows_d, d), lambda i, ly, index: (ly, 0, index[i], 0, 0))
    blocks = [wide, wide, tall]
    rows = gs[0].shape[-2]
    if held:
        g_specs = [pl.BlockSpec((1, 1, chunks, rows, FC), lambda i, ly, index: (lax.rem(i, 2), held[0] + i // 2, layers - 1 - ly, 0, 0))]
    else:
        g_specs = [
            pl.BlockSpec((chunks, rows, FC), lambda i, ly, index: (jnp.where(i == 0, layers - 1 - ly, 0), 0, 0)),
            pl.BlockSpec((chunks, rows, FC), lambda i, ly, index: (jnp.where(i == 1, layers - 1 - ly, layers - 1), 0, 0)),
        ]
    args = [*gs, *w, *m, *v]
    specs = g_specs + blocks * 3
    aliases = {}
    if prev is not None:
        aliases = {2 + len(args) + k: k for k in range(9)}
        args += list(prev)
        specs += [pl.BlockSpec(memory_space=pl.ANY)] * 9
    outs = [jax.ShapeDtypeStruct(a.shape, a.dtype) for a in (*w, *m, *v)]
    moved = 2 * steps * sum(a.size * a.dtype.itemsize for a in (*w, *m, *v)) // parts
    return pl.pallas_call(
        functools.partial(adam_kernel, len(gs), count, lambda i: i, prev is not None),
        name="adam",
        grid_spec=pltpu.PrefetchScalarGridSpec(
            num_scalar_prefetch=1,
            grid=(steps, layers),
            in_specs=[pl.BlockSpec((8, 128), lambda i, ly, index: (0, 0))] + specs,
            out_specs=blocks * 3,
        ),
        out_shape=outs,
        input_output_aliases=aliases,
        compiler_params=pltpu.CompilerParams(vmem_limit_bytes=40 << 20),
        cost_estimate=pl.CostEstimate(flops=30 * moved, bytes_accessed=moved, transcendentals=0),
    )(pieces, sq, *args)


def solution(mesh):
    n = mesh.shape["dp"]

    def step(x, dy, *arrays):
        w = arrays[0:3]
        layers, d, ff = w[0].shape
        count = 3 * w[0].size
        rounds = HELD
        G, *got, sq = train(n, rounds, x, dy, *w)

        def view(a):
            a = list(a)
            for k in range(2):
                a[k] = a[k].reshape(layers, 2 * n, d // (2 * n), ff)
            a[2] = a[2].reshape(layers, ff // FC, 2 * n, FC // (2 * n), d)
            return a

        views = tuple(view(arrays[k : k + 3]) for k in (0, 3, 6))
        me = lax.axis_index("dp")

        def pieces(first, number):
            j = first + jnp.arange(number)
            return jnp.stack([2 * ((me - j + n) % n), 2 * ((me + j) % n) + 1], 1).reshape(-1).astype(jnp.int32)

        right, left = [(k, (k + 1) % n) for k in range(n)], [(k, (k - 1) % n) for k in range(n)]
        out = adam(views, None, sq, [G], pieces(0, rounds), count, (0, rounds))
        for j in range(rounds, n):
            out = adam(views, out, sq, got, pieces(j, 1), count)
            if j < n - 1:
                got = [lax.ppermute(got[0], "dp", right), lax.ppermute(got[1], "dp", left)]
        return tuple(o.reshape(a.shape) for o, a in zip(out, arrays, strict=True))

    return jax.shard_map(
        step,
        mesh=mesh,
        in_specs=(P(("rep", "dp"), None, None),) * 2 + (P(None, None, None),) * 9,
        out_specs=(P("rep", None, None),) * 9,
        check_vma=False,
    )
```

time: 647 us -> 439 us (0.68); the launches traced: 638 us -> 437 us
  Pallas kernels: 0 us -> 428 us
  waiting for transfers between devices: 324 us -> 0 us
  matrix products: 213 us -> 0 us
  other arithmetic: 75.1 us -> 0.62 us
  between operations: 16.8 us -> 0.88 us
    pallas_call x0 -> x3, Pallas kernels: none -> 428 us  [the longest x1 362 us: train(): pl.pallas_call(functools.partial(train_kernel, n, rounds), name='train',...]
    psum x1 -> x0, waiting for transfers between devices: 324 us -> none  [step(): summed[number] = [lax.psum(by_w[name], 'dp') for name in NAMES]]
    dot_general x15 -> x0, matrix products: 213 us -> none  [the longest x5 84.7 us: layer(): gate = jnp.dot(a, w['w_gate'], preferred_element_type=jnp.float32)]
    convert_element_type x2 -> x0, other arithmetic: 58.2 us -> none  [adamw(): return ((w - 0.02 * step).astype(jnp.bfloat16), m, v)]
    reduce_sum x4 -> x0, other arithmetic: 15.6 us -> none  [the longest x3 15.1 us: step(): jnp.sum(g * g)]
  transfers between devices with their start and end apart: 1 -> 0, of which waited for: 1 -> 0; matrix products, arithmetic and copies ran while one was open for 0% -> 0% of each run, Pallas kernels for 0% -> 0%
where the time goes in v1:
time: 439 us; the launch traced here: 437 us
  Pallas kernels  428 us (97%)
  local copies, waits for them, and re-layouts  7 us (2%)
    pallas_call x1, Pallas kernels, train(): pl.pallas_call(functools.partial(train_kernel, n, rounds), name='train',...  362 us
    pallas_call x2, Pallas kernels, adam(): pl.pallas_call(functools.partial(adam_kernel, len(gs), count, lambda i: i...  66.7 us

profile of v1, /device:TPU:21, one launch (start us, length us, event | category | flops | bytes accessed | tf_op | source)
XLA Modules:
  0.0 436.7 jit_solution(14187784611721693801)
XLA Ops:
  0.7 0.6 add_bitcast_fusion.index
  1.3 0.1 copy.29
  1.4 0.6 reshape.188.index
  2.0 361.5 %train.1 = (bf16[2,7,20,96,256]{4,3,2,1,0:T(8,128)(2,1)}, bf16[20,96,256]{2,1,0:T(8,128)(2,1)}, bf16[20,96,256]{2,1,0:T(8,128)(2,1)}, f32[8,128]{1,0:T(8,128)}) custom-call(bf16[1,2048,512]{2,1,0:T(8,128)(2,1)} %x.1, bf16[1,2048,512]{2,1,0:T(8,128)(2,1)} %dy.1, bf16[2,512,2560]{2,1,0:T(8,128)(2,1)} %wg_h.1, bf16[2,512,2560]{2,1,0:T(8,128)(2,1)} %wu_h.1, ...), custom_call_target="tpu_custom_call" | custom-call | flops 91268055040 | bytes 31457280 | tf_op jit(solution)/shard_map/train/pallas_call | solution.py:320
  363.5 0.0 copy-start
  363.5 2.5 copy-done
  366.0 0.0 copy-start.1
  366.0 2.5 copy-done.1
  368.5 0.0 copy-start.4
  368.5 0.7 copy-done.4
  369.2 0.0 copy-start.5
  369.2 0.7 copy-done.5
  369.8 0.0 copy-start.2
  369.9 0.0 copy-start.3
  369.9 0.0 copy-start.6
  369.9 57.5 %adam.2 = (bf16[2,16,32,2560]{3,2,1,0:T(8,128)(2,1)}, bf16[2,16,32,2560]{3,2,1,0:T(8,128)(2,1)}, bf16[2,10,16,16,512]{4,3,2,1,0:T(8,128)(2,1)}, f32[2,16,32,2560...) custom-call(s32[14]{0:T(128)S(1)} %copy-done.5, ...), custom_call_target="tpu_custom_call" | custom-call | flops 4128768000 | bytes 137625600 | tf_op jit(solution)/shard_map/adam/pallas_call | solution.py:406
  427.3 0.0 copy-done.2
  427.3 0.0 copy-done.3
  427.4 0.0 copy-done.6
  427.4 9.2 %adam.3 = (bf16[2,16,32,2560]{3,2,1,0:T(8,128)(2,1)}, bf16[2,16,32,2560]{3,2,1,0:T(8,128)(2,1)}, bf16[2,10,16,16,512]{4,3,2,1,0:T(8,128)(2,1)}, f32[2,16,32,2560...) custom-call(s32[2]{0:T(128)S(1)} %copy-done.6, ...), custom_call_target="tpu_custom_call", output_to_operand_aliasing={{0}: (13, {}), {1}: (14, {}), {2}: (15, {}), {3}: (16, {}),... | custom-call | flops 589824000 | bytes 19660800 | tf_op jit(solution)/shard_map/adam/pallas_call | solution.py:406
  (2 shorter events, 0.0 us)
Async XLA Ops:
  363.5 2.5 copy-start
  366.0 2.5 copy-start.1
  368.5 0.7 copy-start.4
  369.2 0.7 copy-start.5
  369.8 57.5 %copy-start.2 = (bf16[20,96,256]{2,1,0:T(8,128)(2,1)S(1)}, bf16[20,96,256]{2,1,0:T(8,128)(2,1)}, u32[]{:S(2)}) copy-start(bf16[20,96,256]{2,1,0:T(8,128)(2,1)} %get-tuple-element.32.refs_0_) | copy-start | bytes 2949124
  369.9 57.5 %copy-start.3 = (bf16[20,96,256]{2,1,0:T(8,128)(2,1)S(1)}, bf16[20,96,256]{2,1,0:T(8,128)(2,1)}, u32[]{:S(2)}) copy-start(bf16[20,96,256]{2,1,0:T(8,128)(2,1)} %get-tuple-element.33.refs_1_) | copy-start | bytes 2949124
  369.9 57.5 %copy-start.6 = (s32[2]{0:T(128)S(1)}, s32[2]{0:T(128)}, u32[]{:S(2)}) copy-start(s32[2]{0:T(128)} %add_bitcast_fusion.index) | copy-start | bytes 28

commit v2 on v1

--- a/solution.py
+++ b/solution.py
@@ -7,11 +7,12 @@
 from jax.experimental.pallas import tpu as pltpu
 from jax.sharding import PartitionSpec as P
 
+
 f32, bf16 = jnp.float32, jnp.bfloat16
 MESH = pl.DeviceIdType.MESH
 FC = 256
 SLOTS = 4
-HELD = 7
+HELD = 4
 EARLY = 3
 TILE = 1024
 
@@ -253,11 +254,11 @@
     q = sum(q[:, k * lanes : (k + 1) * lanes] for k in range(FC // lanes))
     SQA[me] = q.reshape(-1, 8, lanes).sum(0)
 
-    def sq_copy(k, slot):
+    def sq_copy(k):
         return pltpu.make_async_remote_copy(SQA.at[me], SQA.at[me], sq_s.at[k], sq_r.at[k], device_id=(rep, lax.rem(me + k, n)), device_id_type=MESH)
 
     for k in range(1, n):
-        sq_copy(k, None).start()
+        sq_copy(k).start()
 
     def gather(t):
         j, u = t // units, lax.rem(t, units)
@@ -304,7 +305,7 @@
 
     loop(units, finish)
     for k in range(1, n):
-        sq_copy(k, None).wait_send()
+        sq_copy(k).wait_send()
 
 
 def train(n, rounds, x, dy, w_gate, w_up, w_down):
@@ -344,7 +345,7 @@
     )(x, dy, w_gate, w_up, w_down)
 
 
-def adam_kernel(n_src, count, source, aliased, index, sq, *refs):
+def adam_kernel(n_src, count, sources, aliased, index, sq, *refs):
     gs, refs = refs[:n_src], refs[n_src:]
     w, m, v = refs[0:3], refs[3:6], refs[6:9]
     outs = refs[9 + (9 if aliased else 0) :]
@@ -362,40 +363,53 @@
 
     def run(g):
         rows_p, rows_d, d = w[0].shape[2], w[2].shape[3], w[2].shape[4]
-        for c in range(w[2].shape[1]):
-            cols = slice(c * FC, (c + 1) * FC)
+
+        def chunk(c):
+            cols = pl.ds(pl.multiple_of(c * FC, FC), FC)
             for k in range(2):
                 update(g[c, k * rows_p : (k + 1) * rows_p], k, (0, 0, slice(None), cols))
             for k in range(d // FC):
                 at = 2 * rows_p + k * rows_d
                 update(g[c, at : at + rows_d], 2, (0, c, 0, slice(None), slice(k * FC, (k + 1) * FC)))
 
-    if n_src == 1:
-        run(gs[0].at[0, 0] if len(gs[0].shape) == 5 else gs[0])
-    else:
-        for k in range(n_src):
-            pl.when(source(i) == k)(functools.partial(run, gs[k]))
-
-
-def adam(views, prev, sq, gs, pieces, count, held=None):
+        loop(w[2].shape[1], chunk)
+
+    for k in range(n_src):
+        g = gs[k].at[0, 0] if len(gs[k].shape) == 5 else gs[k]
+        mine = [sources.index(s) for s in sources if s[0] == k]
+        pl.when((i >= mine[0]) & (i <= mine[-1]))(functools.partial(run, g))
+
+
+def adam(views, prev, sq, gs, sources, me, n, count):
     w, m, v = views
     layers, parts, rows_p, ff = w[0].shape
     _, chunks, _, rows_d, d = w[2].shape
-    steps = 2 * (held[1] if held else 1)
+    steps = len(sources)
+    index = jnp.stack([2 * ((me + (2 * h - 1) * j + n) % n) + h for _, h, j in sources]).astype(jnp.int32)
 
     wide = pl.BlockSpec((1, 1, rows_p, ff), lambda i, ly, index: (ly, index[i], 0, 0))
     tall = pl.BlockSpec((1, chunks, 1, rows_d, d), lambda i, ly, index: (ly, 0, index[i], 0, 0))
     blocks = [wide, wide, tall]
-    rows = gs[0].shape[-2]
-    if held:
-        g_specs = [pl.BlockSpec((1, 1, chunks, rows, FC), lambda i, ly, index: (lax.rem(i, 2), held[0] + i // 2, layers - 1 - ly, 0, 0))]
-    else:
-        g_specs = [
-            pl.BlockSpec((chunks, rows, FC), lambda i, ly, index: (jnp.where(i == 0, layers - 1 - ly, 0), 0, 0)),
-            pl.BlockSpec((chunks, rows, FC), lambda i, ly, index: (jnp.where(i == 1, layers - 1 - ly, layers - 1), 0, 0)),
-        ]
+
+    def g_spec(k):
+        mine = [t for t in range(steps) if sources[t][0] == k]
+        lo, hi = mine[0], mine[-1]
+
+        def place(i, ly):
+            return jnp.clip(i, lo, hi), jnp.where(i < lo, layers - 1, jnp.where(i > hi, 0, layers - 1 - ly))
+
+        if len(gs[k].shape) == 3:
+            return pl.BlockSpec((chunks, gs[k].shape[1], FC), lambda i, ly, index: (place(i, ly)[1], 0, 0))
+
+        def held(i, ly, index):
+            t, at = place(i, ly)
+            _, _, j = sources[lo]
+            return lax.rem(t - lo, 2), j + (t - lo) // 2, at, 0, 0
+
+        return pl.BlockSpec((1, 1, chunks, gs[k].shape[3], FC), held)
+
     args = [*gs, *w, *m, *v]
-    specs = g_specs + blocks * 3
+    specs = [g_spec(k) for k in range(len(gs))] + blocks * 3
     aliases = {}
     if prev is not None:
         aliases = {2 + len(args) + k: k for k in range(9)}
@@ -404,7 +418,7 @@
     outs = [jax.ShapeDtypeStruct(a.shape, a.dtype) for a in (*w, *m, *v)]
     moved = 2 * steps * sum(a.size * a.dtype.itemsize for a in (*w, *m, *v)) // parts
     return pl.pallas_call(
-        functools.partial(adam_kernel, len(gs), count, lambda i: i, prev is not None),
+        functools.partial(adam_kernel, len(gs), count, sources, prev is not None),
         name="adam",
         grid_spec=pltpu.PrefetchScalarGridSpec(
             num_scalar_prefetch=1,
@@ -414,9 +428,9 @@
         ),
         out_shape=outs,
         input_output_aliases=aliases,
-        compiler_params=pltpu.CompilerParams(vmem_limit_bytes=40 << 20),
+        compiler_params=pltpu.CompilerParams(vmem_limit_bytes=67043328),
         cost_estimate=pl.CostEstimate(flops=30 * moved, bytes_accessed=moved, transcendentals=0),
-    )(pieces, sq, *args)
+    )(index, sq, *args)
 
 
 def solution(mesh):
@@ -424,9 +438,13 @@
 
     def step(x, dy, *arrays):
         w = arrays[0:3]
-        layers, d, ff = w[0].shape
         count = 3 * w[0].size
         rounds = HELD
+        return whole(n, rounds, count, x, dy, arrays)
+
+    def whole(n, rounds, count, x, dy, arrays):
+        w = arrays[0:3]
+        layers, d, ff = w[0].shape
         G, *got, sq = train(n, rounds, x, dy, *w)
 
         def view(a):
@@ -438,17 +456,24 @@
 
         views = tuple(view(arrays[k : k + 3]) for k in (0, 3, 6))
         me = lax.axis_index("dp")
-
-        def pieces(first, number):
-            j = first + jnp.arange(number)
-            return jnp.stack([2 * ((me - j + n) % n), 2 * ((me + j) % n) + 1], 1).reshape(-1).astype(jnp.int32)
-
         right, left = [(k, (k + 1) % n) for k in range(n)], [(k, (k - 1) % n) for k in range(n)]
-        out = adam(views, None, sq, [G], pieces(0, rounds), count, (0, rounds))
-        for j in range(rounds, n):
-            out = adam(views, out, sq, got, pieces(j, 1), count)
-            if j < n - 1:
-                got = [lax.ppermute(got[0], "dp", right), lax.ppermute(got[1], "dp", left)]
+
+        out, hops = None, n - 1 - rounds
+        first = rounds - 1
+        for k in range(hops + 1):
+            came = got
+            if k < hops:
+                r = lax.ppermute(came[0], "dp", right)
+                got = [r, lax.ppermute(came[1], "dp", left)]
+            if k == 0:
+                gs, sources = [G], [(0, h, j) for j in range(first) for h in (0, 1)]
+                late = came
+            else:
+                gs, sources = list(came), [(0, 0, rounds + k), (1, 1, rounds + k)]
+            if k == min(1, hops):
+                gs += [*late, G]
+                sources += [(2, 0, rounds), (3, 1, rounds), (4, 0, first), (4, 1, first)]
+            out = adam(views, out, sq, gs, sources, me, n, count)
         return tuple(o.reshape(a.shape) for o, a in zip(out, arrays, strict=True))
 
     return jax.shard_map(

time: 439 us -> 428 us (0.975)
  Pallas kernels: 428 us -> 373 us
  waiting for transfers between devices: 0 us -> 36.6 us
  starting transfers between devices: 0 us -> 8.11 us
  local copies, waits for them, and re-layouts: 7 us -> 2.16 us
    pallas_call x1, Pallas kernels: 362 us -> 297 us  [train(): pl.pallas_call(functools.partial(train_kernel, n, rounds), name='train',...]
    ppermute x0 -> x6, waiting for transfers between devices: none -> 36.6 us  [the longest x3 36.6 us: whole(): r = lax.ppermute(came[0], 'dp', right)]
    pallas_call x2 -> x4, Pallas kernels: 66.7 us -> 76.9 us  [adam(): pl.pallas_call(functools.partial(adam_kernel, len(gs), count, sources, pr...]
    ppermute x0 -> x6, starting transfers between devices: none -> 8.11 us  [the longest x3 7.99 us: whole(): got = [r, lax.ppermute(came[1], 'dp', left)]]
    unnamed x14 -> x4, local copies, waits for them, and re-layouts: 6.31 us -> 0.94 us
  transfers between devices with their start and end apart: 0 -> 6, of which waited for: 0 -> 2; matrix products, arithmetic and copies ran while one was open for 0% -> 1% of each run, Pallas kernels for 0% -> 16%
where the time goes in v2:
time: 428 us; the launch traced here: 422 us
  Pallas kernels  373 us (87%)
  waiting for transfers between devices  36.6 us (9%)
  starting transfers between devices  8.11 us (2%)
    pallas_call x1, Pallas kernels, train(): pl.pallas_call(functools.partial(train_kernel, n, rounds), name='train',...  297 us
    pallas_call x4, Pallas kernels, adam(): pl.pallas_call(functools.partial(adam_kernel, len(gs), count, sources, pr...  76.9 us
    ppermute x3, waiting for transfers between devices, whole(): r = lax.ppermute(came[0], 'dp', right)  36.6 us
  transfers between devices with their start and end apart: 6, of which 2 were waited for; matrix products, arithmetic and copies ran while one was open for 1% of the time, Pallas kernels for 16%

profile of v2, /device:TPU:21, one launch (start us, length us, event | category | flops | bytes accessed | tf_op | source)
XLA Modules:
  0.0 422.3 jit_solution(16680049455752874198)
XLA Ops:
  0.6 296.5 %train.1 = (bf16[2,4,20,96,256]{4,3,2,1,0:T(8,128)(2,1)}, bf16[20,96,256]{2,1,0:T(8,128)(2,1)}, bf16[20,96,256]{2,1,0:T(8,128)(2,1)}, f32[8,128]{1,0:T(8,128)}) custom-call(bf16[1,2048,512]{2,1,0:T(8,128)(2,1)} %x.1, bf16[1,2048,512]{2,1,0:T(8,128)(2,1)} %dy.1, bf16[2,512,2560]{2,1,0:T(8,128)(2,1)} %wg_h.1, bf16[2,512,2560]{2,1,0:T(8,128)(2,1)} %wu_h.1, ...), custom_call_target="tpu_custom_call" | custom-call | flops 91268055040 | bytes 31457280 | tf_op jit(solution)/shard_map/train/pallas_call | solution.py:321
  297.2 0.1 collective-permute-start
  297.3 2.7 collective-permute-start.3
  299.9 18.8 %collective-permute-done.refs_0_ = bf16[20,96,256]{2,1,0:T(8,128)(2,1)S(1)} collective-permute-done((bf16[20,96,256]{2,1,0:T(8,128)(2,1)}, bf16[20,96,256]{2,1,0:T(8,128)(2,1)S(1)}, u32[]{:S(2)}, u32[]{:S(2)}) %collective-permute-start) | collective-permute-done | bytes 983072 | tf_op jit(solution)/shard_map/ppermute | solution.py:466
  318.7 0.0 copy-start
  318.7 0.9 copy-done
  319.7 0.0 collective-permute-start.1
  319.7 0.0 collective-permute-done.3.refs_1_
  319.7 0.0 copy-start.1
  319.7 2.7 collective-permute-start.4
  322.4 17.8 %collective-permute-done.1.refs_0_ = bf16[20,96,256]{2,1,0:T(8,128)(2,1)} collective-permute-done((bf16[20,96,256]{2,1,0:T(8,128)(2,1)S(1)}, bf16[20,96,256]{2,1,0:T(8,128)(2,1)}, u32[]{:S(2)}, u32[]{:S(2)}) %collective-permute-start.1) | collective-permute-done | bytes 983072 | tf_op jit(solution)/shard_map/ppermute | solution.py:466
  340.2 0.0 copy-done.1
  340.2 0.0 collective-permute-start.2
  340.2 0.0 collective-permute-done.4.refs_1_
  340.2 2.7 collective-permute-start.5
  342.9 0.6 stack.79.index
  343.5 0.6 stack.72.index
  344.1 0.6 pad_add_fusion.1.index
  344.7 0.6 pad_add_fusion.index
  345.2 28.9 %adam.4 = (bf16[2,16,32,2560]{3,2,1,0:T(8,128)(2,1)}, bf16[2,16,32,2560]{3,2,1,0:T(8,128)(2,1)}, bf16[2,10,16,16,512]{4,3,2,1,0:T(8,128)(2,1)}, f32[2,16,32,2560...) custom-call(s32[6]{0:T(128)} %stack.79.index, ...), custom_call_target="tpu_custom_call" | custom-call | flops 1769472000 | bytes 58982400 | tf_op jit(solution)/shard_map/adam/pallas_call | solution.py:420
  374.1 26.4 %adam.5 = (bf16[2,16,32,2560]{3,2,1,0:T(8,128)(2,1)}, bf16[2,16,32,2560]{3,2,1,0:T(8,128)(2,1)}, bf16[2,10,16,16,512]{4,3,2,1,0:T(8,128)(2,1)}, f32[2,16,32,2560...) custom-call(s32[6]{0:T(128)} %stack.72.index, ...), custom_call_target="tpu_custom_call", output_to_operand_aliasing={{0}: (16, {}), {1}: (17, {}), {2}: (18, {}), {3}: (19, {}),... | custom-call | flops 1769472000 | bytes 58982400 | tf_op jit(solution)/shard_map/adam/pallas_call | solution.py:420
  400.5 10.8 %adam.6 = (bf16[2,16,32,2560]{3,2,1,0:T(8,128)(2,1)}, bf16[2,16,32,2560]{3,2,1,0:T(8,128)(2,1)}, bf16[2,10,16,16,512]{4,3,2,1,0:T(8,128)(2,1)}, f32[2,16,32,2560...) custom-call(s32[2]{0:T(128)} %pad_add_fusion.1.index, ...), custom_call_target="tpu_custom_call", output_to_operand_aliasing={{0}: (13, {}), {1}: (14, {}), {2}: (15, {}), {3}: (16, {}),... | custom-call | flops 589824000 | bytes 19660800 | tf_op jit(solution)/shard_map/adam/pallas_call | solution.py:420
  411.3 0.0 collective-permute-done.2.refs_0_
  411.3 0.0 collective-permute-done.5.refs_1_
  411.4 10.8 %adam.7 = (bf16[2,16,32,2560]{3,2,1,0:T(8,128)(2,1)}, bf16[2,16,32,2560]{3,2,1,0:T(8,128)(2,1)}, bf16[2,10,16,16,512]{4,3,2,1,0:T(8,128)(2,1)}, f32[2,16,32,2560...) custom-call(s32[2]{0:T(128)} %pad_add_fusion.index, ...), custom_call_target="tpu_custom_call", output_to_operand_aliasing={{0}: (13, {}), {1}: (14, {}), {2}: (15, {}), {3}: (16, {}),... | custom-call | flops 589824000 | bytes 19660800 | tf_op jit(solution)/shard_map/adam/pallas_call | solution.py:420
Async XLA Ops:
  297.2 21.6 %collective-permute-start = (bf16[20,96,256]{2,1,0:T(8,128)(2,1)}, bf16[20,96,256]{2,1,0:T(8,128)(2,1)S(1)}, u32[]{:S(2)}, u32[]{:S(2)}) collective-permute-start(bf16[20,96,256]{2,1,0:T(8,128)(2,1)} %get-tuple-element.50.refs_2_), channel_id=1, source_target_pairs={{0,1},{1,2},{2,3},{3,4},{4,5},{5,6},{6,7},{7,0},{8,9},{9,10},{10,1... | collective-permute-start | bytes 2949128 | tf_op jit(solution)/shard_map/ppermute | solution.py:466
  297.3 22.4 %collective-permute-start.3 = (bf16[20,96,256]{2,1,0:T(8,128)(2,1)}, bf16[20,96,256]{2,1,0:T(8,128)(2,1)S(1)}, u32[]{:S(2)}, u32[]{:S(2)}) collective-permute-start(bf16[20,96,256]{2,1,0:T(8,128)(2,1)} %get-tuple-element.51.refs_3_), channel_id=1, source_target_pairs={{0,7},{1,0},{2,1},{3,2},{4,3},{5,4},{6,5},{7,6},{8,15},{9,8},{10,9... | collective-permute-start | bytes 2949128 | tf_op jit(solution)/shard_map/ppermute | solution.py:467
  318.7 0.9 copy-start
  319.7 20.5 %collective-permute-start.1 = (bf16[20,96,256]{2,1,0:T(8,128)(2,1)S(1)}, bf16[20,96,256]{2,1,0:T(8,128)(2,1)}, u32[]{:S(2)}, u32[]{:S(2)}) collective-permute-start(bf16[20,96,256]{2,1,0:T(8,128)(2,1)S(1)} %collective-permute-done.refs_0_), channel_id=1, source_target_pairs={{0,1},{1,2},{2,3},{3,4},{4,5},{5,6},{6,7},{7,0},{8,9},{9,10},{10,1... | collective-permute-start | bytes 2949128 | tf_op jit(solution)/shard_map/ppermute | solution.py:466
  319.7 20.5 %copy-start.1 = (bf16[20,96,256]{2,1,0:T(8,128)(2,1)}, bf16[20,96,256]{2,1,0:T(8,128)(2,1)S(1)}, u32[]{:S(2)}) copy-start(bf16[20,96,256]{2,1,0:T(8,128)(2,1)S(1)} %collective-permute-done.3.refs_1_) | copy-start | bytes 2949124
  319.7 20.5 %collective-permute-start.4 = (bf16[20,96,256]{2,1,0:T(8,128)(2,1)S(1)}, bf16[20,96,256]{2,1,0:T(8,128)(2,1)}, u32[]{:S(2)}, u32[]{:S(2)}) collective-permute-start(bf16[20,96,256]{2,1,0:T(8,128)(2,1)S(1)} %collective-permute-done.3.refs_1_), channel_id=1, source_target_pairs={{0,7},{1,0},{2,1},{3,2},{4,3},{5,4},{6,5},{7,6},{8,15},{9,8},{10,9... | collective-permute-start | bytes 2949128 | tf_op jit(solution)/shard_map/ppermute | solution.py:467
  340.2 71.1 %collective-permute-start.2 = (bf16[20,96,256]{2,1,0:T(8,128)(2,1)}, bf16[20,96,256]{2,1,0:T(8,128)(2,1)}, u32[]{:S(2)}, u32[]{:S(2)}) collective-permute-start(bf16[20,96,256]{2,1,0:T(8,128)(2,1)} %collective-permute-done.1.refs_0_), channel_id=1, source_target_pairs={{0,1},{1,2},{2,3},{3,4},{4,5},{5,6},{6,7},{7,0},{8,9},{9,10},{10,1... | collective-permute-start | bytes 2949128 | tf_op jit(solution)/shard_map/ppermute | solution.py:466
  340.2 71.1 %collective-permute-start.5 = (bf16[20,96,256]{2,1,0:T(8,128)(2,1)}, bf16[20,96,256]{2,1,0:T(8,128)(2,1)}, u32[]{:S(2)}, u32[]{:S(2)}) collective-permute-start(bf16[20,96,256]{2,1,0:T(8,128)(2,1)} %collective-permute-done.4.refs_1_), channel_id=1, source_target_pairs={{0,7},{1,0},{2,1},{3,2},{4,3},{5,4},{6,5},{7,6},{8,15},{9,8},{10,9... | collective-permute-start | bytes 2949128 | tf_op jit(solution)/shard_map/ppermute | solution.py:467

commit v3 on v2

v3 whole, which is shorter than its diff:
```python
import functools

import jax
import jax.numpy as jnp
from jax import lax
from jax.experimental import pallas as pl
from jax.experimental.pallas import tpu as pltpu
from jax.sharding import PartitionSpec as P


f32, bf16 = jnp.float32, jnp.bfloat16
MESH = pl.DeviceIdType.MESH
FC = 256
SLOTS = 4
HELD = 4
DEPTH = 6
TILE = 1024


def dot(a, b):
    return jnp.dot(a, b, preferred_element_type=f32)


def dot_nt(a, b):
    return lax.dot_general(a, b, (((1,), (1,)), ((), ())), preferred_element_type=f32)


def sigmoid(x):
    return 0.5 * jnp.tanh(0.5 * x) + 0.5


def loop(n, body):
    lax.fori_loop(0, n, lambda i, c: (body(i), c)[1], 0)


def train_kernel(n, rounds, x, dy, wg_h, wu_h, wd_h, G, L0, L1, sq_out, A0, A1, AT, H, DY, DYT, ACC, HID, DGU, WGU, WD, PART, RECV, SQ, SQA,
                 in_sem, w_sem, rs_s, rs_r, ag_s, ag_r, own_sem, sq_sem):
    _, tokens, d = x.shape
    layers, _, ff = wg_h.shape
    chunks = ff // FC
    units = layers * chunks
    last = (L0, L1)
    rows_p, rows_d = d // (2 * n), FC // (2 * n)
    me, rep = lax.axis_index("dp"), lax.axis_index("rep")
    to = (lax.rem(me + 1, n), lax.rem(me + n - 1, n))
    sign = (-1, 1)
    step_rows = tokens // 4

    bar = pltpu.get_barrier_semaphore()
    for k in range(1, n):
        pl.semaphore_signal(bar, inc=1, device_id=(rep, lax.rem(me + k, n)), device_id_type=MESH)

    def w_copies(i):
        slot = lax.rem(i, SLOTS)
        ly = jnp.where(i // chunks == 1, layers - 1, 0)
        c = pl.ds(pl.multiple_of(lax.rem(i, chunks) * FC, FC), FC)
        half = lax.rem(slot, 2)
        first = i < chunks
        at = jnp.where(first, half, 2 * half) * FC
        gap = jnp.where(first, 2, 1) * FC
        return (
            pltpu.make_async_copy(wg_h.at[ly, :, c], WGU.at[slot // 2, :, pl.ds(pl.multiple_of(at, FC), FC)], w_sem.at[slot, 0]),
            pltpu.make_async_copy(wu_h.at[ly, :, c], WGU.at[slot // 2, :, pl.ds(pl.multiple_of(at + gap, FC), FC)], w_sem.at[slot, 1]),
            pltpu.make_async_copy(wd_h.at[ly, c, :], WD.at[slot], w_sem.at[slot, 2]),
        )

    def w_start(i):
        for c in w_copies(i):
            c.start()

    def w_wait(i):
        for c in w_copies(i):
            c.wait()

    x_in = pltpu.make_async_copy(x.at[0], H, in_sem.at[0])
    dy_in = pltpu.make_async_copy(dy.at[0], DY, in_sem.at[1])
    x_in.start()
    w_start(0)
    w_start(1)
    dy_in.start()

    def rows(t):
        return pl.ds(pl.multiple_of(t * step_rows, step_rows), step_rows)

    def scale_of(w):
        return lax.rsqrt(jnp.mean(w * w, -1, keepdims=True) + 1e-6)

    x_in.wait()

    def norm_x(t):
        w = H[rows(t), :].astype(f32)
        A0[rows(t), :] = (w * scale_of(w)).astype(bf16)

    loop(4, norm_x)
    ACC[...] = jnp.zeros_like(ACC)

    def forward(i):
        w_wait(2 * i)
        w_wait(2 * i + 1)
        w_start(2 * i + 2)
        w_start(2 * i + 3)
        pair = lax.rem(i, SLOTS // 2)
        a = A0[...]
        g = dot(a, WGU[pair, :, 0 : 2 * FC])
        u = dot(a, WGU[pair, :, 2 * FC : 4 * FC])
        ACC[...] += dot((g * sigmoid(g) * u).astype(bf16), WD[pl.ds(2 * pair, 2)].reshape(2 * FC, d))

    loop(chunks // 2, forward)
    dy_in.wait()

    def between(t):
        r = rows(t)
        h = (H[r, :].astype(f32) + ACC[r, :].astype(bf16).astype(f32)).astype(bf16)
        H[r, :] = h
        w = h.astype(f32)
        a = (w * scale_of(w)).astype(bf16)
        A1[r, :] = a
        AT[:, r] = a.T
        DYT[:, r] = DY[r, :].T
        ACC[r, :] = jnp.zeros((step_rows, d), f32)

    loop(4, between)
    pl.semaphore_wait(bar, n - 1)

    def piece(s, h):
        return 2 * lax.rem(me + sign[h] * (1 + s) + 2 * n, n) + h

    def rs_copy(u, s, h):
        return pltpu.make_async_remote_copy(PART.at[u, piece(s, h)], RECV.at[u, s, h], rs_s.at[u], rs_r.at[u, s],
                                            device_id=(rep, to[h]), device_id_type=MESH)

    def whole(ref, sem):
        return pltpu.make_async_copy(ref, ref, sem)

    def rs_take(u, s, h):
        p = piece(s + 1, h)
        total = (PART[u, p].astype(f32) + RECV[u, s, h].astype(f32)).astype(bf16)
        PART[u, p] = total
        return total

    def rs_event(u, s):
        whole(RECV.at[u, s - 1], rs_r.at[u, s - 1]).wait()

        @pl.when(s < n - 1)
        def _():
            for h in (0, 1):
                rs_take(u, s - 1, h)
            for h in (0, 1):
                rs_copy(u, s, h).start()

        @pl.when(s == n - 1)
        def _():
            for h in (0, 1):
                g = rs_take(u, n - 2, h).astype(f32)
                SQ[...] += g * g
                own_copy(u, h).start()

    def own_copy(u, h):
        return pltpu.make_async_copy(PART.at[u, 2 * me + h], G.at[h, 0, u], own_sem.at[0])

    def events(i, back, number):
        def one(q):
            s = back - q

            @pl.when(i >= s)
            def _():
                rs_event(i - s, s)

        loop(number, one)

    def backward(ly, A, i):
        w_wait(i + chunks)

        @pl.when(i + 2 < units)
        def _():
            w_start(i + chunks + 2)

        slot = lax.rem(i + chunks, SLOTS)
        wgu = WGU.at[slot // 2, :, pl.ds(pl.multiple_of(lax.rem(slot, 2) * 2 * FC, 2 * FC), 2 * FC)]
        wd = WD.at[slot]

        def tile(t):
            r = pl.ds(pl.multiple_of(t * TILE, TILE), TILE)
            gu = dot(A[r, :], wgu[...])
            g, u = gu[:, :FC], gu[:, FC:]
            by_hid = dot_nt(DY[r, :], wd[...]).astype(bf16).astype(f32)
            sg = sigmoid(g)
            sl = g * sg
            HID[r, :] = (sl * u).astype(bf16)
            DGU[r, FC : 2 * FC] = (by_hid * sl).astype(bf16)
            DGU[r, 0:FC] = (by_hid * u * (sg + sl * (1 - sg))).astype(bf16)
            events(i, jnp.where(t == 0, n - 1, (n - 2) // 2), jnp.where(t == 0, n // 2, (n - 2) // 2 - 1))

        loop(tokens // TILE, tile)
        wdt = dot(DYT[...], HID[...]).astype(bf16).T
        for k in range(d // FC):
            PART[i, :, 2 * rows_p + k * rows_d : 2 * rows_p + (k + 1) * rows_d] = wdt[:, k * FC : (k + 1) * FC].reshape(2 * n, rows_d, FC)
        events(i, 1, 1)
        gw = dot(AT[...], DGU[...]).astype(bf16)
        PART[i, :, 0:rows_p] = gw[:, :FC].reshape(2 * n, rows_p, FC)
        PART[i, :, rows_p : 2 * rows_p] = gw[:, FC:].reshape(2 * n, rows_p, FC)

        for h in (0, 1):
            rs_copy(i, 0, h).start()
        if ly:
            ACC[...] += dot_nt(DGU[...], wgu[...])

    SQ[...] = jnp.zeros_like(SQ)
    loop(chunks, functools.partial(backward, 1, A1))

    def by_input(t):
        r = rows(t)
        w, da = H[r, :].astype(f32), ACC[r, :].astype(bf16).astype(f32)
        s = scale_of(w)
        along = jnp.sum(da * w, -1, keepdims=True) * (s * s * s) * (1.0 / d)
        by_h = (DY[r, :].astype(f32) + (da * s - w * along).astype(bf16).astype(f32)).astype(bf16)
        DY[r, :] = by_h
        DYT[:, r] = by_h.T
        AT[:, r] = A0[r, :].T

    loop(4, by_input)
    loop(chunks, lambda i: backward(0, A0, i + chunks))

    def ag_copy(u, j, h, dst):
        src = PART.at[u, 2 * me + h] if isinstance(j, int) and j == 0 else G.at[h, j, u]
        return pltpu.make_async_remote_copy(src, dst, ag_s.at[u], ag_r.at[u, j], device_id=(rep, to[h]), device_id_type=MESH)

    per = -(-units // (n - 1))

    def drain(i):
        def one(q):
            u = units + i - n + 1 + q
            s = n - 1 - q

            @pl.when(u < units)
            def _():
                rs_event(u, s)

        loop(n - 1, one)

        def first(k):
            u = i * per + k

            @pl.when(u < units)
            def _():
                for h in (0, 1):
                    ag_copy(u, 0, h, G.at[h, 1, u]).start()

        loop(per, first)

    loop(n - 1, drain)

    lanes = SQA.shape[-1]
    q = SQ[...]
    q = sum(q[:, k * lanes : (k + 1) * lanes] for k in range(FC // lanes))
    SQA[me] = q.reshape(-1, 8, lanes).sum(0)

    def sq_copy(k):
        return pltpu.make_async_remote_copy(SQA.at[me], SQA.at[me], sq_sem.at[0], sq_sem.at[1], device_id=(rep, lax.rem(me + k, n)), device_id_type=MESH)

    for k in range(1, n):
        sq_copy(k).start()

    def gather(t):
        j, u = t // units, lax.rem(t, units)
        whole(RECV.at[u, 0], ag_r.at[u, j]).wait()
        for h in (0, 1):
            ag_copy(u, j + 1, h, G.at[h, j + 2, u]).start()

    loop((rounds - 2) * units, gather)

    def gather_last(u):
        whole(RECV.at[u, 0], ag_r.at[u, rounds - 2]).wait()
        for h in (0, 1):
            ag_copy(u, rounds - 1, h, last[h].at[u]).start()

    loop(units, gather_last)

    whole(SQA.at[1:n], sq_sem.at[1]).wait()
    total = SQA[0]
    for k in range(1, n):
        total = total + SQA[k]
    sq_out[...] = jnp.broadcast_to(jnp.sum(total, keepdims=True), sq_out.shape)

    def finish(u):
        whole(RECV.at[u, 0], ag_r.at[u, rounds - 1]).wait()
        whole(RECV.at[u], rs_s.at[u]).wait()
        whole(RECV.at[u, 0:rounds], ag_s.at[u]).wait()

    loop(units, finish)
    whole(RECV.at[:, 0], own_sem.at[0]).wait()
    whole(SQA.at[1:n], sq_sem.at[0]).wait()


def train(n, rounds, x, dy, w_gate, w_up, w_down):
    _, tokens, d = x.shape
    layers, _, ff = w_gate.shape
    units, rows = layers * ff // FC, 3 * d // (2 * n)
    part = (rows, FC)
    any_ = pl.BlockSpec(memory_space=pl.ANY)
    got = jax.ShapeDtypeStruct((units,) + part, bf16)
    act = pltpu.VMEM((tokens, d), bf16)
    act_t = pltpu.VMEM((d, tokens), bf16)
    dma = pltpu.SemaphoreType.DMA
    return pl.pallas_call(
        functools.partial(train_kernel, n, rounds),
        name="train",
        out_shape=(jax.ShapeDtypeStruct((2, rounds, units) + part, bf16), got, got, jax.ShapeDtypeStruct((8, 128), f32)),
        in_specs=[any_] * 5,
        out_specs=(any_, any_, any_, pl.BlockSpec(memory_space=pltpu.VMEM)),
        scratch_shapes=[
            act, act, act_t, act, act, act_t,
            pltpu.VMEM((tokens, d), f32),
            pltpu.VMEM((tokens, FC), bf16),
            pltpu.VMEM((tokens, 2 * FC), bf16),
            pltpu.VMEM((SLOTS // 2, d, 4 * FC), bf16),
            pltpu.VMEM((SLOTS, FC, d), bf16),
            pltpu.VMEM((units, 2 * n) + part, bf16),
            pltpu.VMEM((units, n - 1, 2) + part, bf16),
            pltpu.VMEM(part, f32),
            pltpu.VMEM((n, 8, 128), f32),
            dma((2,)), dma((SLOTS, 3)),
            dma((units,)), dma((units, n - 1)), dma((units,)), dma((units, rounds)), dma((1,)), dma((2,)),
        ],
        compiler_params=pltpu.CompilerParams(collective_id=0, has_side_effects=True, vmem_limit_bytes=67043328),
        cost_estimate=pl.CostEstimate(flops=17 * 2 * tokens * d * ff, bytes_accessed=8 * units * n * rows * FC, transcendentals=0),
    )(x, dy, w_gate, w_up, w_down)


def adam_kernel(n, count, sources, n_src, aliased, sq, *refs):
    gs, w, m, v = refs[:n_src], refs[n_src : n_src + 3], refs[n_src + 3 : n_src + 6], refs[n_src + 6 : n_src + 9]
    refs = refs[n_src + 9 + (9 if aliased else 0) :]
    outs, g_in, wide, tall, in_sem, out_sem = refs[:9], refs[9], refs[10:13], refs[13:16], refs[16], refs[17]
    layers, _, rows_p, _ = w[0].shape
    _, chunks, _, rows_d, d = w[2].shape
    depth = g_in.shape[0]
    steps = layers * len(sources)
    me = lax.axis_index("dp")
    _, h0, j0 = sources[0]

    def place(k):
        t = 2 * j0 + h0 + k // layers
        h, j = lax.rem(t, 2), t // 2
        return lax.rem(k, layers), 2 * lax.rem(me + (2 * h - 1) * j + n, n) + h

    def state(k, arrays, sem, out):
        ly, p = place(k)
        slot = lax.rem(k, depth)
        for q in range(3):
            for x in range(3):
                here = tall[q].at[slot] if x == 2 else wide[q].at[slot, x]
                there = arrays[3 * q + x].at[ly, :, p] if x == 2 else arrays[3 * q + x].at[ly, p]
                yield pltpu.make_async_copy(*((here, there) if out else (there, here)), sem.at[slot])

    def taken(k):
        return state(k, (*w, *m, *v), in_sem, False)

    def given(k):
        return state(k, outs, out_sem, True)

    def arrived(k, sem, times):
        slots = g_in.at[0:times]
        pltpu.make_async_copy(slots, slots, sem.at[lax.rem(k, depth)]).wait()

    def gradient(k, x, t):
        units = pl.ds((layers - 1 - lax.rem(k, layers)) * chunks, chunks)
        at = gs[x].at[units]
        if len(gs[x].shape) == 5:
            i = k // layers - t
            at = gs[x].at[lax.rem(i, 2), sources[t][2] + i // 2, units]
        slot = lax.rem(k, depth)
        return pltpu.make_async_copy(at, g_in.at[slot], in_sem.at[slot])

    spans = [[t for t, src in enumerate(sources) if src[0] == x] for x in range(n_src)]

    def start(k):
        for c in taken(k):
            c.start()
        for x, span in enumerate(spans):

            @pl.when((k >= layers * span[0]) & (k < layers * (span[-1] + 1)))
            def _():
                gradient(k, x, span[0]).start()

    loop(min(depth - 2, steps), start)
    factor = jnp.minimum(1.0, 0.5 * lax.rsqrt(sq[0:1, 0:1] / count + 1e-30))

    def update(g, rows):
        g = g.astype(f32) * factor
        w, m, v = rows
        new_m = 0.9 * m[...] + 0.1 * g
        new_v = 0.95 * v[...] + 0.05 * g * g
        old = w[...].astype(f32)
        m[...] = new_m
        v[...] = new_v
        w[...] = (old - 0.02 * (new_m * lax.rsqrt(new_v + 1e-8) + 0.1 * old)).astype(bf16)

    def step(k):
        slot = lax.rem(k, depth)
        arrived(k, in_sem, 6)

        def chunk(c):
            cols = pl.ds(pl.multiple_of(c * FC, FC), FC)
            for x in range(2):
                update(g_in[slot, c, x * rows_p : (x + 1) * rows_p], [a.at[slot, x, :, cols] for a in wide])
            for x in range(d // FC):
                at = 2 * rows_p + x * rows_d
                update(g_in[slot, c, at : at + rows_d], [a.at[slot, c, :, x * FC : (x + 1) * FC] for a in tall])

        loop(chunks, chunk)
        for c in given(k):
            c.start()

        @pl.when(k >= 2)
        def _():
            arrived(k - 2, out_sem, 5)

        @pl.when(k + depth - 2 < steps)
        def _():
            start(k + depth - 2)

    loop(steps, step)

    def finish(k):
        arrived(steps - 2 + k, out_sem, 5)

    loop(2, finish)


def adam(views, prev, sq, gs, sources, n, count):
    w, m, v = views
    _, parts, rows_p, ff = w[0].shape
    _, chunks, _, rows_d, d = w[2].shape
    any_ = pl.BlockSpec(memory_space=pl.ANY)
    args = [*gs, *w, *m, *v]
    aliases = {}
    if prev is not None:
        aliases = {1 + len(args) + k: k for k in range(9)}
        args += list(prev)
    moved = 2 * len(sources) * sum(a.size * a.dtype.itemsize for a in (*w, *m, *v)) // parts
    types = (bf16, f32, f32)
    return pl.pallas_call(
        functools.partial(adam_kernel, n, count, sources, len(gs), prev is not None),
        name="adam",
        in_specs=[pl.BlockSpec(memory_space=pltpu.VMEM)] + [any_] * len(args),
        out_specs=[any_] * 9,
        out_shape=[jax.ShapeDtypeStruct(a.shape, a.dtype) for a in (*w, *m, *v)],
        input_output_aliases=aliases,
        scratch_shapes=[pltpu.VMEM((DEPTH, chunks, gs[0].shape[-2], FC), bf16)]
        + [pltpu.VMEM((DEPTH, 2, rows_p, ff), t) for t in types]
        + [pltpu.VMEM((DEPTH, chunks, rows_d, d), t) for t in types]
        + [pltpu.SemaphoreType.DMA((DEPTH,)), pltpu.SemaphoreType.DMA((DEPTH,))],
        compiler_params=pltpu.CompilerParams(vmem_limit_bytes=67043328),
        cost_estimate=pl.CostEstimate(flops=30 * moved, bytes_accessed=moved, transcendentals=0),
    )(sq, *args)


def solution(mesh):
    n = mesh.shape["dp"]

    def step(x, dy, *arrays):
        w = arrays[0:3]
        count = 3 * w[0].size
        rounds = HELD
        return whole(n, rounds, count, x, dy, arrays)

    def whole(n, rounds, count, x, dy, arrays):
        w = arrays[0:3]
        layers, d, ff = w[0].shape
        G, *got, sq = train(n, rounds, x, dy, *w)

        def view(a):
            a = list(a)
            for k in range(2):
                a[k] = a[k].reshape(layers, 2 * n, d // (2 * n), ff)
            a[2] = a[2].reshape(layers, ff // FC, 2 * n, FC // (2 * n), d)
            return a

        views = tuple(view(arrays[k : k + 3]) for k in (0, 3, 6))
        right, left = [(k, (k + 1) % n) for k in range(n)], [(k, (k - 1) % n) for k in range(n)]

        out, hops = None, n - 1 - rounds
        first = rounds - 1
        for k in range(hops + 1):
            came = got
            if k < hops:
                r = lax.ppermute(came[0], "dp", right)
                got = [r, lax.ppermute(came[1], "dp", left)]
            if k == 0:
                gs, sources = [G], [(0, h, j) for j in range(first) for h in (0, 1)]
                late = came
            elif k == 1:
                gs = [G, *late, *came]
                sources = [(0, 0, first), (0, 1, first), (1, 0, rounds), (2, 1, rounds), (3, 0, rounds + 1), (4, 1, rounds + 1)]
            else:
                gs, sources = list(came), [(0, 0, rounds + k), (1, 1, rounds + k)]
            out = adam(views, out, sq, gs, sources, n, count)
        return tuple(o.reshape(a.shape) for o, a in zip(out, arrays, strict=True))

    return jax.shard_map(
        step,
        mesh=mesh,
        in_specs=(P(("rep", "dp"), None, None),) * 2 + (P(None, None, None),) * 9,
        out_specs=(P("rep", None, None),) * 9,
        check_vma=False,
    )
```

time: 428 us -> 405 us (0.946)
  Pallas kernels: 373 us -> 353 us
    pallas_call x4, Pallas kernels: 76.9 us -> 65.5 us  [adam(): pl.pallas_call(functools.partial(adam_kernel, n, count, sources, len(gs),...]
    pallas_call x1, Pallas kernels: 297 us -> 288 us  [train(): pl.pallas_call(functools.partial(train_kernel, n, rounds), name='train',...]
  transfers between devices with their start and end apart: 6 -> 6, of which waited for: 2 -> 2; matrix products, arithmetic and copies ran while one was open for 1% -> 0% of each run, Pallas kernels for 16% -> 14%
where the time goes in v3:
time: 405 us; the launch traced here: 401 us
  Pallas kernels  353 us (87%)
  waiting for transfers between devices  38.2 us (9%)
  starting transfers between devices  8.19 us (2%)
    pallas_call x1, Pallas kernels, train(): pl.pallas_call(functools.partial(train_kernel, n, rounds), name='train',...  288 us
    pallas_call x4, Pallas kernels, adam(): pl.pallas_call(functools.partial(adam_kernel, n, count, sources, len(gs),...  65.5 us
    ppermute x3, waiting for transfers between devices, whole(): r = lax.ppermute(came[0], 'dp', right)  38.2 us
  transfers between devices with their start and end apart: 6, of which 2 were waited for; matrix products, arithmetic and copies ran while one was open for 0% of the time, Pallas kernels for 14%

profile of v3, /device:TPU:21, one launch (start us, length us, event | category | flops | bytes accessed | tf_op | source)
XLA Modules:
  0.0 401.3 jit_solution(722876941688665318)
XLA Ops:
  0.6 287.6 %train.1 = (bf16[2,4,20,96,256]{4,3,2,1,0:T(8,128)(2,1)}, bf16[20,96,256]{2,1,0:T(8,128)(2,1)}, bf16[20,96,256]{2,1,0:T(8,128)(2,1)}, f32[8,128]{1,0:T(8,128)}) custom-call(bf16[1,2048,512]{2,1,0:T(8,128)(2,1)} %x.1, bf16[1,2048,512]{2,1,0:T(8,128)(2,1)} %dy.1, bf16[2,512,2560]{2,1,0:T(8,128)(2,1)} %wg_h.1, bf16[2,512,2560]{2,1,0:T(8,128)(2,1)} %wu_h.1, ...), custom_call_target="tpu_custom_call" | custom-call | flops 91268055040 | bytes 31457280 | tf_op jit(solution)/shard_map/train/pallas_call | solution.py:305
  288.2 1.5 collective-permute-start
  289.7 1.4 collective-permute-start.3
  291.0 19.6 %collective-permute-done.refs_3_ = bf16[20,96,256]{2,1,0:T(8,128)(2,1)S(1)} collective-permute-done((bf16[20,96,256]{2,1,0:T(8,128)(2,1)}, bf16[20,96,256]{2,1,0:T(8,128)(2,1)S(1)}, u32[]{:S(2)}, u32[]{:S(2)}) %collective-permute-start) | collective-permute-done | bytes 983072 | tf_op jit(solution)/shard_map/ppermute | solution.py:487
  310.6 0.0 copy-start
  310.6 0.9 copy-done
  311.5 0.8 collective-permute-start.1
  312.3 0.0 collective-permute-done.3.refs_4_
  312.3 0.0 copy-start.1
  312.3 1.9 collective-permute-start.4
  314.2 18.6 %collective-permute-done.1.refs_0_ = bf16[20,96,256]{2,1,0:T(8,128)(2,1)} collective-permute-done((bf16[20,96,256]{2,1,0:T(8,128)(2,1)S(1)}, bf16[20,96,256]{2,1,0:T(8,128)(2,1)}, u32[]{:S(2)}, u32[]{:S(2)}) %collective-permute-start.1) | collective-permute-done | bytes 983072 | tf_op jit(solution)/shard_map/ppermute | solution.py:487
  332.9 0.0 copy-done.1
  332.9 0.2 collective-permute-start.2
  333.1 0.0 collective-permute-done.4.refs_1_
  333.1 2.5 collective-permute-start.5
  335.6 23.2 %adam.4 = (bf16[2,16,32,2560]{3,2,1,0:T(8,128)(2,1)}, bf16[2,16,32,2560]{3,2,1,0:T(8,128)(2,1)}, bf16[2,10,16,16,512]{4,3,2,1,0:T(8,128)(2,1)}, f32[2,16,32,2560...) custom-call(f32[8,128]{1,0:T(8,128)} %get-tuple-element.49.sq, ...), custom_call_target="tpu_custom_call" | custom-call | flops 1769472000 | bytes 58982400 | tf_op jit(solution)/shard_map/adam/pallas_call | solution.py:442
  358.8 23.3 %adam.5 = (bf16[2,16,32,2560]{3,2,1,0:T(8,128)(2,1)}, bf16[2,16,32,2560]{3,2,1,0:T(8,128)(2,1)}, bf16[2,10,16,16,512]{4,3,2,1,0:T(8,128)(2,1)}, f32[2,16,32,2560...) custom-call(f32[8,128]{1,0:T(8,128)} %get-tuple-element.49.sq, ...), custom_call_target="tpu_custom_call", output_to_operand_aliasing={{0}: (15, {}), {1}: (16, {}), {2}: (17, {}), {3}: (18, {}),... | custom-call | flops 1769472000 | bytes 58982400 | tf_op jit(solution)/shard_map/adam/pallas_call | solution.py:442
  382.0 9.5 %adam.6 = (bf16[2,16,32,2560]{3,2,1,0:T(8,128)(2,1)}, bf16[2,16,32,2560]{3,2,1,0:T(8,128)(2,1)}, bf16[2,10,16,16,512]{4,3,2,1,0:T(8,128)(2,1)}, f32[2,16,32,2560...) custom-call(f32[8,128]{1,0:T(8,128)} %get-tuple-element.49.sq, ...), custom_call_target="tpu_custom_call", output_to_operand_aliasing={{0}: (12, {}), {1}: (13, {}), {2}: (14, {}), {3}: (15, {}),... | custom-call | flops 589824000 | bytes 19660800 | tf_op jit(solution)/shard_map/adam/pallas_call | solution.py:442
  391.6 0.0 collective-permute-done.2.refs_0_
  391.6 0.0 collective-permute-done.5.refs_1_
  391.6 9.5 %adam.7 = (bf16[2,16,32,2560]{3,2,1,0:T(8,128)(2,1)}, bf16[2,16,32,2560]{3,2,1,0:T(8,128)(2,1)}, bf16[2,10,16,16,512]{4,3,2,1,0:T(8,128)(2,1)}, f32[2,16,32,2560...) custom-call(f32[8,128]{1,0:T(8,128)} %get-tuple-element.49.sq, ...), custom_call_target="tpu_custom_call", output_to_operand_aliasing={{0}: (12, {}), {1}: (13, {}), {2}: (14, {}), {3}: (15, {}),... | custom-call | flops 589824000 | bytes 19660800 | tf_op jit(solution)/shard_map/adam/pallas_call | solution.py:442
Async XLA Ops:
  288.2 22.4 %collective-permute-start = (bf16[20,96,256]{2,1,0:T(8,128)(2,1)}, bf16[20,96,256]{2,1,0:T(8,128)(2,1)S(1)}, u32[]{:S(2)}, u32[]{:S(2)}) collective-permute-start(bf16[20,96,256]{2,1,0:T(8,128)(2,1)} %get-tuple-element.50.refs_1_), channel_id=1, source_target_pairs={{0,1},{1,2},{2,3},{3,4},{4,5},{5,6},{6,7},{7,0},{8,9},{9,10},{10,1... | collective-permute-start | bytes 2949128 | tf_op jit(solution)/shard_map/ppermute | solution.py:487
  289.7 22.6 %collective-permute-start.3 = (bf16[20,96,256]{2,1,0:T(8,128)(2,1)}, bf16[20,96,256]{2,1,0:T(8,128)(2,1)S(1)}, u32[]{:S(2)}, u32[]{:S(2)}) collective-permute-start(bf16[20,96,256]{2,1,0:T(8,128)(2,1)} %get-tuple-element.51.refs_2_), channel_id=1, source_target_pairs={{0,7},{1,0},{2,1},{3,2},{4,3},{5,4},{6,5},{7,6},{8,15},{9,8},{10,9... | collective-permute-start | bytes 2949128 | tf_op jit(solution)/shard_map/ppermute | solution.py:488
  310.6 0.9 copy-start
  311.5 21.3 %collective-permute-start.1 = (bf16[20,96,256]{2,1,0:T(8,128)(2,1)S(1)}, bf16[20,96,256]{2,1,0:T(8,128)(2,1)}, u32[]{:S(2)}, u32[]{:S(2)}) collective-permute-start(bf16[20,96,256]{2,1,0:T(8,128)(2,1)S(1)} %collective-permute-done.refs_3_), channel_id=1, source_target_pairs={{0,1},{1,2},{2,3},{3,4},{4,5},{5,6},{6,7},{7,0},{8,9},{9,10},{10,1... | collective-permute-start | bytes 2949128 | tf_op jit(solution)/shard_map/ppermute | solution.py:487
  312.3 20.5 %copy-start.1 = (bf16[20,96,256]{2,1,0:T(8,128)(2,1)}, bf16[20,96,256]{2,1,0:T(8,128)(2,1)S(1)}, u32[]{:S(2)}) copy-start(bf16[20,96,256]{2,1,0:T(8,128)(2,1)S(1)} %collective-permute-done.3.refs_4_) | copy-start | bytes 2949124
  312.3 20.7 %collective-permute-start.4 = (bf16[20,96,256]{2,1,0:T(8,128)(2,1)S(1)}, bf16[20,96,256]{2,1,0:T(8,128)(2,1)}, u32[]{:S(2)}, u32[]{:S(2)}) collective-permute-start(bf16[20,96,256]{2,1,0:T(8,128)(2,1)S(1)} %collective-permute-done.3.refs_4_), channel_id=1, source_target_pairs={{0,7},{1,0},{2,1},{3,2},{4,3},{5,4},{6,5},{7,6},{8,15},{9,8},{10,9... | collective-permute-start | bytes 2949128 | tf_op jit(solution)/shard_map/ppermute | solution.py:488
  332.9 58.7 %collective-permute-start.2 = (bf16[20,96,256]{2,1,0:T(8,128)(2,1)}, bf16[20,96,256]{2,1,0:T(8,128)(2,1)}, u32[]{:S(2)}, u32[]{:S(2)}) collective-permute-start(bf16[20,96,256]{2,1,0:T(8,128)(2,1)} %collective-permute-done.1.refs_0_), channel_id=1, source_target_pairs={{0,1},{1,2},{2,3},{3,4},{4,5},{5,6},{6,7},{7,0},{8,9},{9,10},{10,1... | collective-permute-start | bytes 2949128 | tf_op jit(solution)/shard_map/ppermute | solution.py:487
  333.1 58.5 %collective-permute-start.5 = (bf16[20,96,256]{2,1,0:T(8,128)(2,1)}, bf16[20,96,256]{2,1,0:T(8,128)(2,1)}, u32[]{:S(2)}, u32[]{:S(2)}) collective-permute-start(bf16[20,96,256]{2,1,0:T(8,128)(2,1)} %collective-permute-done.4.refs_1_), channel_id=1, source_target_pairs={{0,7},{1,0},{2,1},{3,2},{4,3},{5,4},{6,5},{7,6},{8,15},{9,8},{10,9... | collective-permute-start | bytes 2949128 | tf_op jit(solution)/shard_map/ppermute | solution.py:488

commit v4 on v3

--- a/solution.py
+++ b/solution.py
@@ -12,7 +12,8 @@
 MESH = pl.DeviceIdType.MESH
 FC = 256
 SLOTS = 4
-HELD = 4
+JOINT = 2
+HELD = 3
 DEPTH = 6
 TILE = 1024
 
@@ -72,22 +73,23 @@
         for c in w_copies(i):
             c.wait()
 
-    x_in = pltpu.make_async_copy(x.at[0], H, in_sem.at[0])
-    dy_in = pltpu.make_async_copy(dy.at[0], DY, in_sem.at[1])
-    x_in.start()
+    def rows(t):
+        return pl.ds(pl.multiple_of(t * step_rows, step_rows), step_rows)
+
+    def x_in(t):
+        return pltpu.make_async_copy(x.at[0, rows(t)], H.at[rows(t)], in_sem.at[t])
+
+    dy_in = pltpu.make_async_copy(dy.at[0], DY, in_sem.at[4])
+    loop(4, lambda t: x_in(t).start())
     w_start(0)
     w_start(1)
     dy_in.start()
 
-    def rows(t):
-        return pl.ds(pl.multiple_of(t * step_rows, step_rows), step_rows)
-
     def scale_of(w):
         return lax.rsqrt(jnp.mean(w * w, -1, keepdims=True) + 1e-6)
 
-    x_in.wait()
-
     def norm_x(t):
+        x_in(t).wait()
         w = H[rows(t), :].astype(f32)
         A0[rows(t), :] = (w * scale_of(w)).astype(bf16)
 
@@ -104,9 +106,11 @@
         g = dot(a, WGU[pair, :, 0 : 2 * FC])
         u = dot(a, WGU[pair, :, 2 * FC : 4 * FC])
         ACC[...] += dot((g * sigmoid(g) * u).astype(bf16), WD[pl.ds(2 * pair, 2)].reshape(2 * FC, d))
-
+        t = rows(lax.rem(i, 4))
+        DYT[:, t] = DY[t, :].T
+
+    dy_in.wait()
     loop(chunks // 2, forward)
-    dy_in.wait()
 
     def between(t):
         r = rows(t)
@@ -116,7 +120,6 @@
         a = (w * scale_of(w)).astype(bf16)
         A1[r, :] = a
         AT[:, r] = a.T
-        DYT[:, r] = DY[r, :].T
         ACC[r, :] = jnp.zeros((step_rows, d), f32)
 
     loop(4, between)
@@ -221,11 +224,16 @@
     loop(4, by_input)
     loop(chunks, lambda i: backward(0, A0, i + chunks))
 
-    def ag_copy(u, j, h, dst):
-        src = PART.at[u, 2 * me + h] if isinstance(j, int) and j == 0 else G.at[h, j, u]
-        return pltpu.make_async_remote_copy(src, dst, ag_s.at[u], ag_r.at[u, j], device_id=(rep, to[h]), device_id_type=MESH)
-
-    per = -(-units // (n - 1))
+    groups = units // JOINT
+
+    def ag_copy(g, j, h):
+        us = pl.ds(JOINT * g, JOINT)
+        src = PART.at[us, 2 * me + h] if isinstance(j, int) and j == 0 else G.at[h, j, us]
+        dst = last[h].at[us] if isinstance(j, int) and j == rounds - 1 else G.at[h, j + 1, us]
+        return pltpu.make_async_remote_copy(src, dst, ag_s.at[g], ag_r.at[g, j], device_id=(rep, to[h]), device_id_type=MESH)
+
+    def ag_wait(g, j):
+        whole(RECV.at[0:JOINT, 0], ag_r.at[g, j]).wait()
 
     def drain(i):
         def one(q):
@@ -239,14 +247,14 @@
         loop(n - 1, one)
 
         def first(k):
-            u = i * per + k
-
-            @pl.when(u < units)
+            g = groups * i // (n - 1) + k
+
+            @pl.when(g < groups * (i + 1) // (n - 1))
             def _():
                 for h in (0, 1):
-                    ag_copy(u, 0, h, G.at[h, 1, u]).start()
-
-        loop(per, first)
+                    ag_copy(g, 0, h).start()
+
+        loop(-(-groups // (n - 1)), first)
 
     loop(n - 1, drain)
 
@@ -262,20 +270,19 @@
         sq_copy(k).start()
 
     def gather(t):
-        j, u = t // units, lax.rem(t, units)
-        whole(RECV.at[u, 0], ag_r.at[u, j]).wait()
+        j, g = t // groups, lax.rem(t, groups)
+        ag_wait(g, j)
         for h in (0, 1):
-            ag_copy(u, j + 1, h, G.at[h, j + 2, u]).start()
-
-    loop((rounds - 2) * units, gather)
-
-    def gather_last(u):
-        whole(RECV.at[u, 0], ag_r.at[u, rounds - 2]).wait()
+            ag_copy(g, j + 1, h).start()
+
+    loop((rounds - 2) * groups, gather)
+
+    def gather_last(g):
+        ag_wait(g, rounds - 2)
         for h in (0, 1):
-            ag_copy(u, rounds - 1, h, last[h].at[u]).start()
-
-    loop(units, gather_last)
-
+            ag_copy(g, rounds - 1, h).start()
+
+    loop(groups, gather_last)
     whole(SQA.at[1:n], sq_sem.at[1]).wait()
     total = SQA[0]
     for k in range(1, n):
@@ -283,10 +290,13 @@
     sq_out[...] = jnp.broadcast_to(jnp.sum(total, keepdims=True), sq_out.shape)
 
     def finish(u):
-        whole(RECV.at[u, 0], ag_r.at[u, rounds - 1]).wait()
         whole(RECV.at[u], rs_s.at[u]).wait()
-        whole(RECV.at[u, 0:rounds], ag_s.at[u]).wait()
-
+
+    def finish_ag(g):
+        ag_wait(g, rounds - 1)
+        whole(RECV.at[0:JOINT, 0:rounds], ag_s.at[g]).wait()
+
+    loop(groups, finish_ag)
     loop(units, finish)
     whole(RECV.at[:, 0], own_sem.at[0]).wait()
     whole(SQA.at[1:n], sq_sem.at[0]).wait()
@@ -319,8 +329,8 @@
             pltpu.VMEM((units, n - 1, 2) + part, bf16),
             pltpu.VMEM(part, f32),
             pltpu.VMEM((n, 8, 128), f32),
-            dma((2,)), dma((SLOTS, 3)),
-            dma((units,)), dma((units, n - 1)), dma((units,)), dma((units, rounds)), dma((1,)), dma((2,)),
+            dma((5,)), dma((SLOTS, 3)),
+            dma((units,)), dma((units, n - 1)), dma((units // JOINT,)), dma((units // JOINT, rounds)), dma((1,)), dma((2,)),
         ],
         compiler_params=pltpu.CompilerParams(collective_id=0, has_side_effects=True, vmem_limit_bytes=67043328),
         cost_estimate=pl.CostEstimate(flops=17 * 2 * tokens * d * ff, bytes_accessed=8 * units * n * rows * FC, transcendentals=0),
@@ -366,8 +376,8 @@
         units = pl.ds((layers - 1 - lax.rem(k, layers)) * chunks, chunks)
         at = gs[x].at[units]
         if len(gs[x].shape) == 5:
-            i = k // layers - t
-            at = gs[x].at[lax.rem(i, 2), sources[t][2] + i // 2, units]
+            i = 2 * sources[t][2] + sources[t][1] + k // layers - t
+            at = gs[x].at[lax.rem(i, 2), i // 2, units]
         slot = lax.rem(k, depth)
         return pltpu.make_async_copy(at, g_in.at[slot], in_sem.at[slot])
 
@@ -480,20 +490,19 @@
         right, left = [(k, (k + 1) % n) for k in range(n)], [(k, (k - 1) % n) for k in range(n)]
 
         out, hops = None, n - 1 - rounds
-        first = rounds - 1
+        came, at = [got], 0
         for k in range(hops + 1):
-            came = got
             if k < hops:
-                r = lax.ppermute(came[0], "dp", right)
-                got = [r, lax.ppermute(came[1], "dp", left)]
-            if k == 0:
-                gs, sources = [G], [(0, h, j) for j in range(first) for h in (0, 1)]
-                late = came
-            elif k == 1:
-                gs = [G, *late, *came]
-                sources = [(0, 0, first), (0, 1, first), (1, 0, rounds), (2, 1, rounds), (3, 0, rounds + 1), (4, 1, rounds + 1)]
-            else:
-                gs, sources = list(came), [(0, 0, rounds + k), (1, 1, rounds + k)]
+                r = lax.ppermute(came[k][0], "dp", right)
+                came.append([r, lax.ppermute(came[k][1], "dp", left)])
+            gs, sources = [], []
+            for p in range(at, at + (-(-(2 * n - 2 - at) // (hops - k)) if k < hops else 2)):
+                j, h = p // 2, p % 2
+                g = G if j < rounds else came[j - rounds][h]
+                if not any(g is o for o in gs):
+                    gs.append(g)
+                sources.append((len(gs) - 1, h, j))
+            at += len(sources)
             out = adam(views, out, sq, gs, sources, n, count)
         return tuple(o.reshape(a.shape) for o, a in zip(out, arrays, strict=True))
 

time: 405 us -> 407 us (level)
  Pallas kernels: 353 us -> 332 us
  waiting for transfers between devices: 38.2 us -> 54.7 us
  starting transfers between devices: 8.19 us -> 12.3 us
    pallas_call x1, Pallas kernels: 288 us -> 265 us  [train(): pl.pallas_call(functools.partial(train_kernel, n, rounds), name='train',...]
    ppermute x6 -> x8, waiting for transfers between devices: 38.2 us -> 54.7 us  [the longest x4 54.7 us: whole(): r = lax.ppermute(came[k][0], 'dp', right)]
    ppermute x6 -> x8, starting transfers between devices: 8.19 us -> 12.3 us  [the longest x4 8.85 us: whole(): came.append([r, lax.ppermute(came[k][1], 'dp', left)])]
    pallas_call x4 -> x5, Pallas kernels: 65.5 us -> 67.8 us  [adam(): pl.pallas_call(functools.partial(adam_kernel, n, count, sources, len(gs),...]
  transfers between devices with their start and end apart: 6 -> 8, of which waited for: 2 -> 3; matrix products, arithmetic and copies ran while one was open for 0% -> 0% of each run, Pallas kernels for 14% -> 15%
where the time goes in v4:
time: 407 us; the launch traced here: 401 us
  Pallas kernels  332 us (82%)
  waiting for transfers between devices  54.7 us (13%)
  starting transfers between devices  12.3 us (3%)
    pallas_call x1, Pallas kernels, train(): pl.pallas_call(functools.partial(train_kernel, n, rounds), name='train',...  265 us
    pallas_call x5, Pallas kernels, adam(): pl.pallas_call(functools.partial(adam_kernel, n, count, sources, len(gs),...  67.8 us
    ppermute x4, waiting for transfers between devices, whole(): r = lax.ppermute(came[k][0], 'dp', right)  54.7 us
    ppermute x4, starting transfers between devices, whole(): came.append([r, lax.ppermute(came[k][1], 'dp', left)])  8.85 us
  transfers between devices with their start and end apart: 8, of which 3 were waited for; matrix products, arithmetic and copies ran while one was open for 0% of the time, Pallas kernels for 15%

profile of v4, /device:TPU:21, one launch (start us, length us, event | category | flops | bytes accessed | tf_op | source)
XLA Modules:
  0.0 401.4 jit_solution(5921697251996013565)
XLA Ops:
  0.6 264.6 %train.1 = (bf16[2,3,20,96,256]{4,3,2,1,0:T(8,128)(2,1)}, bf16[20,96,256]{2,1,0:T(8,128)(2,1)}, bf16[20,96,256]{2,1,0:T(8,128)(2,1)}, f32[8,128]{1,0:T(8,128)}) custom-call(bf16[1,2048,512]{2,1,0:T(8,128)(2,1)} %x.1, bf16[1,2048,512]{2,1,0:T(8,128)(2,1)} %dy.1, bf16[2,512,2560]{2,1,0:T(8,128)(2,1)} %wg_h.1, bf16[2,512,2560]{2,1,0:T(8,128)(2,1)} %wu_h.1, ...), custom_call_target="tpu_custom_call" | custom-call | flops 91268055040 | bytes 31457280 | tf_op jit(solution)/shard_map/train/pallas_call | solution.py:315
  265.3 2.3 collective-permute-start
  267.6 1.4 collective-permute-start.4
  268.9 19.5 %collective-permute-done.refs_0_ = bf16[20,96,256]{2,1,0:T(8,128)(2,1)S(1)} collective-permute-done((bf16[20,96,256]{2,1,0:T(8,128)(2,1)}, bf16[20,96,256]{2,1,0:T(8,128)(2,1)S(1)}, u32[]{:S(2)}, u32[]{:S(2)}) %collective-permute-start) | collective-permute-done | bytes 983072 | tf_op jit(solution)/shard_map/ppermute | solution.py:496
  288.4 0.0 copy-start.1
  288.4 0.8 collective-permute-start.1
  289.2 0.0 collective-permute-done.4.refs_1_
  289.2 0.0 copy-start.2
  289.2 1.9 collective-permute-start.5
  291.1 18.5 %collective-permute-done.1.refs_2_ = bf16[20,96,256]{2,1,0:T(8,128)(2,1)S(1)} collective-permute-done((bf16[20,96,256]{2,1,0:T(8,128)(2,1)S(1)}, bf16[20,96,256]{2,1,0:T(8,128)(2,1)S(1)}, u32[]{:S(2)}, u32[]{:S(2)}) %collective-permute-start.1) | collective-permute-done | bytes 983072 | tf_op jit(solution)/shard_map/ppermute | solution.py:496
  309.5 0.0 copy-start.3
  309.5 0.2 collective-permute-start.2
  309.8 0.0 collective-permute-done.5.refs_0_
  309.8 0.0 copy-start
  309.8 1.0 copy-done
  310.8 2.4 collective-permute-start.6
  313.2 16.8 %collective-permute-done.2.refs_1_ = bf16[20,96,256]{2,1,0:T(8,128)(2,1)} collective-permute-done((bf16[20,96,256]{2,1,0:T(8,128)(2,1)S(1)}, bf16[20,96,256]{2,1,0:T(8,128)(2,1)}, u32[]{:S(2)}, u32[]{:S(2)}) %collective-permute-start.2) | collective-permute-done | bytes 983072 | tf_op jit(solution)/shard_map/ppermute | solution.py:496
  330.0 0.1 collective-permute-start.3
  330.1 0.0 collective-permute-done.6.refs_2_
  330.1 0.0 copy-done.1
  330.1 3.2 collective-permute-start.7
  333.3 0.0 copy-done.2
  333.3 0.0 copy-done.3
  333.3 16.3 %adam.5 = (bf16[2,16,32,2560]{3,2,1,0:T(8,128)(2,1)}, bf16[2,16,32,2560]{3,2,1,0:T(8,128)(2,1)}, bf16[2,10,16,16,512]{4,3,2,1,0:T(8,128)(2,1)}, f32[2,16,32,2560...) custom-call(f32[8,128]{1,0:T(8,128)} %get-tuple-element.58.sq, ...), custom_call_target="tpu_custom_call" | custom-call | flops 1179648000 | bytes 39321600 | tf_op jit(solution)/shard_map/adam/pallas_call | solution.py:452
  349.7 16.4 %adam.6 = (bf16[2,16,32,2560]{3,2,1,0:T(8,128)(2,1)}, bf16[2,16,32,2560]{3,2,1,0:T(8,128)(2,1)}, bf16[2,10,16,16,512]{4,3,2,1,0:T(8,128)(2,1)}, f32[2,16,32,2560...) custom-call(f32[8,128]{1,0:T(8,128)} %get-tuple-element.58.sq, ...), custom_call_target="tpu_custom_call", output_to_operand_aliasing={{0}: (13, {}), {1}: (14, {}), {2}: (15, {}), {3}: (16, {}),... | custom-call | flops 1179648000 | bytes 39321600 | tf_op jit(solution)/shard_map/adam/pallas_call | solution.py:452
  366.1 12.8 %adam.7 = (bf16[2,16,32,2560]{3,2,1,0:T(8,128)(2,1)}, bf16[2,16,32,2560]{3,2,1,0:T(8,128)(2,1)}, bf16[2,10,16,16,512]{4,3,2,1,0:T(8,128)(2,1)}, f32[2,16,32,2560...) custom-call(f32[8,128]{1,0:T(8,128)} %get-tuple-element.58.sq, ...), custom_call_target="tpu_custom_call", output_to_operand_aliasing={{0}: (13, {}), {1}: (14, {}), {2}: (15, {}), {3}: (16, {}),... | custom-call | flops 884736000 | bytes 29491200 | tf_op jit(solution)/shard_map/adam/pallas_call | solution.py:452
  378.9 12.8 %adam.8 = (bf16[2,16,32,2560]{3,2,1,0:T(8,128)(2,1)}, bf16[2,16,32,2560]{3,2,1,0:T(8,128)(2,1)}, bf16[2,10,16,16,512]{4,3,2,1,0:T(8,128)(2,1)}, f32[2,16,32,2560...) custom-call(f32[8,128]{1,0:T(8,128)} %get-tuple-element.58.sq, ...), custom_call_target="tpu_custom_call", output_to_operand_aliasing={{0}: (13, {}), {1}: (14, {}), {2}: (15, {}), {3}: (16, {}),... | custom-call | flops 884736000 | bytes 29491200 | tf_op jit(solution)/shard_map/adam/pallas_call | solution.py:452
  391.7 0.0 collective-permute-done.3.refs_0_
  391.7 0.0 collective-permute-done.7.refs_1_
  391.7 9.5 %adam.9 = (bf16[2,16,32,2560]{3,2,1,0:T(8,128)(2,1)}, bf16[2,16,32,2560]{3,2,1,0:T(8,128)(2,1)}, bf16[2,10,16,16,512]{4,3,2,1,0:T(8,128)(2,1)}, f32[2,16,32,2560...) custom-call(f32[8,128]{1,0:T(8,128)} %get-tuple-element.58.sq, ...), custom_call_target="tpu_custom_call", output_to_operand_aliasing={{0}: (12, {}), {1}: (13, {}), {2}: (14, {}), {3}: (15, {}),... | custom-call | flops 589824000 | bytes 19660800 | tf_op jit(solution)/shard_map/adam/pallas_call | solution.py:452
Async XLA Ops:
  265.3 23.1 %collective-permute-start = (bf16[20,96,256]{2,1,0:T(8,128)(2,1)}, bf16[20,96,256]{2,1,0:T(8,128)(2,1)S(1)}, u32[]{:S(2)}, u32[]{:S(2)}) collective-permute-start(bf16[20,96,256]{2,1,0:T(8,128)(2,1)} %get-tuple-element.59.refs_1_), channel_id=1, source_target_pairs={{0,1},{1,2},{2,3},{3,4},{4,5},{5,6},{6,7},{7,0},{8,9},{9,10},{10,1... | collective-permute-start | bytes 2949128 | tf_op jit(solution)/shard_map/ppermute | solution.py:496
  267.6 21.6 %collective-permute-start.4 = (bf16[20,96,256]{2,1,0:T(8,128)(2,1)}, bf16[20,96,256]{2,1,0:T(8,128)(2,1)S(1)}, u32[]{:S(2)}, u32[]{:S(2)}) collective-permute-start(bf16[20,96,256]{2,1,0:T(8,128)(2,1)} %get-tuple-element.60.refs_2_), channel_id=1, source_target_pairs={{0,7},{1,0},{2,1},{3,2},{4,3},{5,4},{6,5},{7,6},{8,15},{9,8},{10,9... | collective-permute-start | bytes 2949128 | tf_op jit(solution)/shard_map/ppermute | solution.py:497
  288.4 41.7 %copy-start.1 = (bf16[20,96,256]{2,1,0:T(8,128)(2,1)}, bf16[20,96,256]{2,1,0:T(8,128)(2,1)S(1)}, u32[]{:S(2)}) copy-start(bf16[20,96,256]{2,1,0:T(8,128)(2,1)S(1)} %collective-permute-done.refs_0_) | copy-start | bytes 2949124
  288.4 21.2 %collective-permute-start.1 = (bf16[20,96,256]{2,1,0:T(8,128)(2,1)S(1)}, bf16[20,96,256]{2,1,0:T(8,128)(2,1)S(1)}, u32[]{:S(2)}, u32[]{:S(2)}) collective-permute-start(bf16[20,96,256]{2,1,0:T(8,128)(2,1)S(1)} %collective-permute-done.refs_0_), channel_id=1, source_target_pairs={{0,1},{1,2},{2,3},{3,4},{4,5},{5,6},{6,7},{7,0},{8,9},{9,10},{10,1... | collective-permute-start | bytes 2949128 | tf_op jit(solution)/shard_map/ppermute | solution.py:496
  289.2 44.1 %copy-start.2 = (bf16[20,96,256]{2,1,0:T(8,128)(2,1)}, bf16[20,96,256]{2,1,0:T(8,128)(2,1)S(1)}, u32[]{:S(2)}) copy-start(bf16[20,96,256]{2,1,0:T(8,128)(2,1)S(1)} %collective-permute-done.4.refs_1_) | copy-start | bytes 2949124
  289.2 20.6 %collective-permute-start.5 = (bf16[20,96,256]{2,1,0:T(8,128)(2,1)S(1)}, bf16[20,96,256]{2,1,0:T(8,128)(2,1)S(1)}, u32[]{:S(2)}, u32[]{:S(2)}) collective-permute-start(bf16[20,96,256]{2,1,0:T(8,128)(2,1)S(1)} %collective-permute-done.4.refs_1_), channel_id=1, source_target_pairs={{0,7},{1,0},{2,1},{3,2},{4,3},{5,4},{6,5},{7,6},{8,15},{9,8},{10,9... | collective-permute-start | bytes 2949128 | tf_op jit(solution)/shard_map/ppermute | solution.py:497
  309.5 23.8 %copy-start.3 = (bf16[20,96,256]{2,1,0:T(8,128)(2,1)}, bf16[20,96,256]{2,1,0:T(8,128)(2,1)S(1)}, u32[]{:S(2)}) copy-start(bf16[20,96,256]{2,1,0:T(8,128)(2,1)S(1)} %collective-permute-done.1.refs_2_) | copy-start | bytes 2949124
  309.5 20.4 %collective-permute-start.2 = (bf16[20,96,256]{2,1,0:T(8,128)(2,1)S(1)}, bf16[20,96,256]{2,1,0:T(8,128)(2,1)}, u32[]{:S(2)}, u32[]{:S(2)}) collective-permute-start(bf16[20,96,256]{2,1,0:T(8,128)(2,1)S(1)} %collective-permute-done.1.refs_2_), channel_id=1, source_target_pairs={{0,1},{1,2},{2,3},{3,4},{4,5},{5,6},{6,7},{7,0},{8,9},{9,10},{10,1... | collective-permute-start | bytes 2949128 | tf_op jit(solution)/shard_map/ppermute | solution.py:496
  309.8 1.0 copy-start
  310.8 19.3 %collective-permute-start.6 = (bf16[20,96,256]{2,1,0:T(8,128)(2,1)S(1)}, bf16[20,96,256]{2,1,0:T(8,128)(2,1)}, u32[]{:S(2)}, u32[]{:S(2)}) collective-permute-start(bf16[20,96,256]{2,1,0:T(8,128)(2,1)S(1)} %collective-permute-done.5.refs_0_), channel_id=1, source_target_pairs={{0,7},{1,0},{2,1},{3,2},{4,3},{5,4},{6,5},{7,6},{8,15},{9,8},{10,9... | collective-permute-start | bytes 2949128 | tf_op jit(solution)/shard_map/ppermute | solution.py:497
  330.0 61.7 %collective-permute-start.3 = (bf16[20,96,256]{2,1,0:T(8,128)(2,1)}, bf16[20,96,256]{2,1,0:T(8,128)(2,1)}, u32[]{:S(2)}, u32[]{:S(2)}) collective-permute-start(bf16[20,96,256]{2,1,0:T(8,128)(2,1)} %collective-permute-done.2.refs_1_), channel_id=1, source_target_pairs={{0,1},{1,2},{2,3},{3,4},{4,5},{5,6},{6,7},{7,0},{8,9},{9,10},{10,1... | collective-permute-start | bytes 2949128 | tf_op jit(solution)/shard_map/ppermute | solution.py:496
  330.1 61.6 %collective-permute-start.7 = (bf16[20,96,256]{2,1,0:T(8,128)(2,1)}, bf16[20,96,256]{2,1,0:T(8,128)(2,1)}, u32[]{:S(2)}, u32[]{:S(2)}) collective-permute-start(bf16[20,96,256]{2,1,0:T(8,128)(2,1)} %collective-permute-done.6.refs_2_), channel_id=1, source_target_pairs={{0,7},{1,0},{2,1},{3,2},{4,3},{5,4},{6,5},{7,6},{8,15},{9,8},{10,9... | collective-permute-start | bytes 2949128 | tf_op jit(solution)/shard_map/ppermute | solution.py:497

commit v5 on v4

--- a/solution.py
+++ b/solution.py
@@ -34,13 +34,13 @@
     lax.fori_loop(0, n, lambda i, c: (body(i), c)[1], 0)
 
 
-def train_kernel(n, rounds, x, dy, wg_h, wu_h, wd_h, G, L0, L1, sq_out, A0, A1, AT, H, DY, DYT, ACC, HID, DGU, WGU, WD, PART, RECV, SQ, SQA,
+def train_kernel(n, rounds, x, dy, wg_h, wu_h, wd_h, G, L00, L01, L10, L11, sq_out, A0, A1, AT, H, DY, DYT, ACC, HID, DGU, WGU, WD, PART, RECV, SQ, SQA,
                  in_sem, w_sem, rs_s, rs_r, ag_s, ag_r, own_sem, sq_sem):
     _, tokens, d = x.shape
     layers, _, ff = wg_h.shape
     chunks = ff // FC
     units = layers * chunks
-    last = (L0, L1)
+    last = ((L00, L01), (L10, L11))
     rows_p, rows_d = d // (2 * n), FC // (2 * n)
     me, rep = lax.axis_index("dp"), lax.axis_index("rep")
     to = (lax.rem(me + 1, n), lax.rem(me + n - 1, n))
@@ -226,10 +226,10 @@
 
     groups = units // JOINT
 
-    def ag_copy(g, j, h):
+    def ag_copy(g, j, h, part=None):
         us = pl.ds(JOINT * g, JOINT)
         src = PART.at[us, 2 * me + h] if isinstance(j, int) and j == 0 else G.at[h, j, us]
-        dst = last[h].at[us] if isinstance(j, int) and j == rounds - 1 else G.at[h, j + 1, us]
+        dst = G.at[h, j + 1, us] if part is None else last[part][h].at[pl.ds(JOINT * (g - part * groups // layers), JOINT)]
         return pltpu.make_async_remote_copy(src, dst, ag_s.at[g], ag_r.at[g, j], device_id=(rep, to[h]), device_id_type=MESH)
 
     def ag_wait(g, j):
@@ -277,12 +277,14 @@
 
     loop((rounds - 2) * groups, gather)
 
-    def gather_last(g):
+    def gather_last(part, g):
+        g = g + part * groups // layers
         ag_wait(g, rounds - 2)
         for h in (0, 1):
-            ag_copy(g, rounds - 1, h).start()
-
-    loop(groups, gather_last)
+            ag_copy(g, rounds - 1, h, part).start()
+
+    for part in range(layers):
+        loop(groups // layers, functools.partial(gather_last, part))
     whole(SQA.at[1:n], sq_sem.at[1]).wait()
     total = SQA[0]
     for k in range(1, n):
@@ -308,16 +310,16 @@
     units, rows = layers * ff // FC, 3 * d // (2 * n)
     part = (rows, FC)
     any_ = pl.BlockSpec(memory_space=pl.ANY)
-    got = jax.ShapeDtypeStruct((units,) + part, bf16)
+    got = jax.ShapeDtypeStruct((units // layers,) + part, bf16)
     act = pltpu.VMEM((tokens, d), bf16)
     act_t = pltpu.VMEM((d, tokens), bf16)
     dma = pltpu.SemaphoreType.DMA
     return pl.pallas_call(
         functools.partial(train_kernel, n, rounds),
         name="train",
-        out_shape=(jax.ShapeDtypeStruct((2, rounds, units) + part, bf16), got, got, jax.ShapeDtypeStruct((8, 128), f32)),
+        out_shape=(jax.ShapeDtypeStruct((2, rounds, units) + part, bf16), got, got, got, got, jax.ShapeDtypeStruct((8, 128), f32)),
         in_specs=[any_] * 5,
-        out_specs=(any_, any_, any_, pl.BlockSpec(memory_space=pltpu.VMEM)),
+        out_specs=(any_,) * 5 + (pl.BlockSpec(memory_space=pltpu.VMEM),),
         scratch_shapes=[
             act, act, act_t, act, act, act_t,
             pltpu.VMEM((tokens, d), f32),
@@ -337,24 +339,27 @@
     )(x, dy, w_gate, w_up, w_down)
 
 
-def adam_kernel(n, count, sources, n_src, aliased, sq, *refs):
+def adam_kernel(n, count, sources, spans, aliased, sq, *refs):
+    n_src = len(spans)
     gs, w, m, v = refs[:n_src], refs[n_src : n_src + 3], refs[n_src + 3 : n_src + 6], refs[n_src + 6 : n_src + 9]
     refs = refs[n_src + 9 + (9 if aliased else 0) :]
     outs, g_in, wide, tall, in_sem, out_sem = refs[:9], refs[9], refs[10:13], refs[13:16], refs[16], refs[17]
     layers, _, rows_p, _ = w[0].shape
     _, chunks, _, rows_d, d = w[2].shape
     depth = g_in.shape[0]
-    steps = layers * len(sources)
+    steps = len(sources)
     me = lax.axis_index("dp")
-    _, h0, j0 = sources[0]
+    h0, j0, b0 = sources[0]
+    each = 1 if steps == 1 or sources[1][2] == b0 else layers
 
     def place(k):
-        t = 2 * j0 + h0 + k // layers
+        t = 2 * j0 + h0 + k // each
         h, j = lax.rem(t, 2), t // 2
-        return lax.rem(k, layers), 2 * lax.rem(me + (2 * h - 1) * j + n, n) + h
+        return b0 + lax.rem(k, each), 2 * lax.rem(me + (2 * h - 1) * j + n, n) + h
 
     def state(k, arrays, sem, out):
-        ly, p = place(k)
+        back, p = place(k)
+        ly = layers - 1 - back
         slot = lax.rem(k, depth)
         for q in range(3):
             for x in range(3):
@@ -372,25 +377,22 @@
         slots = g_in.at[0:times]
         pltpu.make_async_copy(slots, slots, sem.at[lax.rem(k, depth)]).wait()
 
-    def gradient(k, x, t):
-        units = pl.ds((layers - 1 - lax.rem(k, layers)) * chunks, chunks)
-        at = gs[x].at[units]
-        if len(gs[x].shape) == 5:
-            i = 2 * sources[t][2] + sources[t][1] + k // layers - t
-            at = gs[x].at[lax.rem(i, 2), i // 2, units]
+    def gradient(k, x):
+        at = gs[x]
+        if len(at.shape) == 5:
+            t = 2 * j0 + h0 + k // each
+            at = at.at[lax.rem(t, 2), t // 2, pl.ds(place(k)[0] * chunks, chunks)]
         slot = lax.rem(k, depth)
         return pltpu.make_async_copy(at, g_in.at[slot], in_sem.at[slot])
-
-    spans = [[t for t, src in enumerate(sources) if src[0] == x] for x in range(n_src)]
 
     def start(k):
         for c in taken(k):
             c.start()
-        for x, span in enumerate(spans):
-
-            @pl.when((k >= layers * span[0]) & (k < layers * (span[-1] + 1)))
+        for x, (lo, hi) in enumerate(spans):
+
+            @pl.when((k >= lo) & (k <= hi))
             def _():
-                gradient(k, x, span[0]).start()
+                gradient(k, x).start()
 
     loop(min(depth - 2, steps), start)
     factor = jnp.minimum(1.0, 0.5 * lax.rsqrt(sq[0:1, 0:1] / count + 1e-30))
@@ -437,9 +439,17 @@
     loop(2, finish)
 
 
-def adam(views, prev, sq, gs, sources, n, count):
+def adam(views, prev, sq, steps, n, count):
+    gs, spans = [], []
+    for k, (g, *_) in enumerate(steps):
+        if gs and gs[-1] is g:
+            spans[-1][1] = k
+        else:
+            gs.append(g)
+            spans.append([k, k])
+    sources = [src[1:] for src in steps]
     w, m, v = views
-    _, parts, rows_p, ff = w[0].shape
+    layers, parts, rows_p, ff = w[0].shape
     _, chunks, _, rows_d, d = w[2].shape
     any_ = pl.BlockSpec(memory_space=pl.ANY)
     args = [*gs, *w, *m, *v]
@@ -447,10 +457,10 @@
     if prev is not None:
         aliases = {1 + len(args) + k: k for k in range(9)}
         args += list(prev)
-    moved = 2 * len(sources) * sum(a.size * a.dtype.itemsize for a in (*w, *m, *v)) // parts
+    moved = 2 * len(sources) * sum(a.size * a.dtype.itemsize for a in (*w, *m, *v)) // (parts * layers)
     types = (bf16, f32, f32)
     return pl.pallas_call(
-        functools.partial(adam_kernel, n, count, sources, len(gs), prev is not None),
+        functools.partial(adam_kernel, n, count, sources, spans, prev is not None),
         name="adam",
         in_specs=[pl.BlockSpec(memory_space=pltpu.VMEM)] + [any_] * len(args),
         out_specs=[any_] * 9,
@@ -490,20 +500,24 @@
         right, left = [(k, (k + 1) % n) for k in range(n)], [(k, (k - 1) % n) for k in range(n)]
 
         out, hops = None, n - 1 - rounds
-        came, at = [got], 0
-        for k in range(hops + 1):
-            if k < hops:
-                r = lax.ppermute(came[k][0], "dp", right)
-                came.append([r, lax.ppermute(came[k][1], "dp", left)])
-            gs, sources = [], []
-            for p in range(at, at + (-(-(2 * n - 2 - at) // (hops - k)) if k < hops else 2)):
-                j, h = p // 2, p % 2
-                g = G if j < rounds else came[j - rounds][h]
-                if not any(g is o for o in gs):
-                    gs.append(g)
-                sources.append((len(gs) - 1, h, j))
-            at += len(sources)
-            out = adam(views, out, sq, gs, sources, n, count)
+        came, at = [[got[2 * b : 2 * b + 2] for b in range(layers)]], 0
+
+        def steps_of(p, b):
+            j, h = p // 2, p % 2
+            return G if j < rounds else came[j - rounds][b][h], h, j, b
+
+        for k in range(hops):
+            came.append([])
+            for b in range(layers):
+                pair = []
+                for h, way in enumerate((right, left)):
+                    pair.append(lax.ppermute(came[k][b][h], "dp", way))
+                came[-1].append(pair)
+            more = -(-(2 * n - 2 - at) // (hops - k))
+            out = adam(views, out, sq, [steps_of(p, b) for p in range(at, at + more) for b in range(layers)], n, count)
+            at += more
+        for b in range(layers):
+            out = adam(views, out, sq, [steps_of(p, b) for p in range(at, 2 * n)], n, count)
         return tuple(o.reshape(a.shape) for o, a in zip(out, arrays, strict=True))
 
     return jax.shard_map(

time: 407 us -> 410 us (level)
  waiting for transfers between devices: 54.7 us -> 44 us
  starting transfers between devices: 12.3 us -> 22.5 us
    ppermute x8 -> x16, waiting for transfers between devices: 54.7 us -> 44 us  [whole(): pair.append(lax.ppermute(came[k][b][h], 'dp', way))]
    ppermute x8 -> x16, starting transfers between devices: 12.3 us -> 22.5 us  [whole(): pair.append(lax.ppermute(came[k][b][h], 'dp', way))]
    pallas_call x5 -> x6, Pallas kernels: 67.8 us -> 70.2 us  [adam(): pl.pallas_call(functools.partial(adam_kernel, n, count, sources, spans, p...]
  transfers between devices with their start and end apart: 8 -> 16, of which waited for: 3 -> 6; matrix products, arithmetic and copies ran while one was open for 0% -> 0% of each run, Pallas kernels for 15% -> 16%
where the time goes in v5:
time: 410 us; the launch traced here: 404 us
  Pallas kernels  335 us (82%)
  waiting for transfers between devices  44 us (11%)
  starting transfers between devices  22.5 us (5%)
    pallas_call x1, Pallas kernels, train(): pl.pallas_call(functools.partial(train_kernel, n, rounds), name='train',...  265 us
    pallas_call x6, Pallas kernels, adam(): pl.pallas_call(functools.partial(adam_kernel, n, count, sources, spans, p...  70.2 us
    ppermute x16, waiting for transfers between devices, whole(): pair.append(lax.ppermute(came[k][b][h], 'dp', way))  44 us
    ppermute x16, starting transfers between devices, whole(): pair.append(lax.ppermute(came[k][b][h], 'dp', way))  22.5 us
  transfers between devices with their start and end apart: 16, of which 6 were waited for; matrix products, arithmetic and copies ran while one was open for 0% of the time, Pallas kernels for 16%

profile of v5, /device:TPU:21, one launch (start us, length us, event | category | flops | bytes accessed | tf_op | source)
XLA Modules:
  0.0 404.0 jit_solution(2050730124850123436)
XLA Ops:
  0.6 264.8 %train.1 = (bf16[2,3,20,96,256]{4,3,2,1,0:T(8,128)(2,1)}, bf16[10,96,256]{2,1,0:T(8,128)(2,1)}, bf16[10,96,256]{2,1,0:T(8,128)(2,1)}, bf16[10,96,256]{2,1,0:T(8,...) custom-call(bf16[1,2048,512]{2,1,0:T(8,128)(2,1)} %x.1, bf16[1,2048,512]{2,1,0:T(8,128)(2,1)} %dy.1, ...), custom_call_target="tpu_custom_call" | custom-call | flops 91268055040 | bytes 31457280 | tf_op jit(solution)/shard_map/train/pallas_call | solution.py:317
  265.4 2.2 collective-permute-start.8
  267.7 1.4 collective-permute-start.12
  269.1 0.1 collective-permute-start
  269.1 2.6 collective-permute-start.4
  271.7 6.2 %collective-permute-done.8.refs_0_ = bf16[10,96,256]{2,1,0:T(8,128)(2,1)S(1)} collective-permute-done((bf16[10,96,256]{2,1,0:T(8,128)(2,1)}, bf16[10,96,256]{2,1,0:T(8,128)(2,1)S(1)}, u32[]{:S(2)}, u32[]{:S(2)}) %collective-permute-start.8) | collective-permute-done | bytes 491552 | tf_op jit(solution)/shard_map/ppermute | solution.py:514
  278.0 0.8 copy-done
  278.8 0.8 collective-permute-start.9
  279.6 1.9 collective-permute-start.13
  281.4 7.1 %collective-permute-done.refs_1_ = bf16[10,96,256]{2,1,0:T(8,128)(2,1)S(1)} collective-permute-done((bf16[10,96,256]{2,1,0:T(8,128)(2,1)}, bf16[10,96,256]{2,1,0:T(8,128)(2,1)S(1)}, u32[]{:S(2)}, u32[]{:S(2)}) %collective-permute-start) | collective-permute-done | bytes 491552 | tf_op jit(solution)/shard_map/ppermute | solution.py:514
  288.5 0.8 collective-permute-start.1
  289.3 1.9 collective-permute-start.5
  291.2 7.8 %collective-permute-done.9.refs_4_ = bf16[10,96,256]{2,1,0:T(8,128)(2,1)S(1)} collective-permute-done((bf16[10,96,256]{2,1,0:T(8,128)(2,1)S(1)}, bf16[10,96,256]{2,1,0:T(8,128)(2,1)S(1)}, u32[]{:S(2)}, u32[]{:S(2)}) %collective-permute-start.9) | collective-permute-done | bytes 491552 | tf_op jit(solution)/shard_map/ppermute | solution.py:514
  299.0 0.8 collective-permute-start.10
  299.9 0.8 copy-done.1
  300.6 1.9 collective-permute-start.14
  302.5 7.1 %collective-permute-done.1.refs_5_ = bf16[10,96,256]{2,1,0:T(8,128)(2,1)S(1)} collective-permute-done((bf16[10,96,256]{2,1,0:T(8,128)(2,1)S(1)}, bf16[10,96,256]{2,1,0:T(8,128)(2,1)S(1)}, u32[]{:S(2)}, u32[]{:S(2)}) %collective-permute-start.1) | collective-permute-done | bytes 491552 | tf_op jit(solution)/shard_map/ppermute | solution.py:514
  309.6 0.8 collective-permute-start.2
  310.4 1.9 collective-permute-start.6
  312.3 8.0 %collective-permute-done.10.refs_2_ = bf16[10,96,256]{2,1,0:T(8,128)(2,1)} collective-permute-done((bf16[10,96,256]{2,1,0:T(8,128)(2,1)S(1)}, bf16[10,96,256]{2,1,0:T(8,128)(2,1)}, u32[]{:S(2)}, u32[]{:S(2)}) %collective-permute-start.10) | collective-permute-done | bytes 491552 | tf_op jit(solution)/shard_map/ppermute | solution.py:514
  320.2 0.8 collective-permute-start.11
  321.0 0.0 collective-permute-done.14.refs_4_
  321.0 1.9 collective-permute-start.15
  322.9 7.8 %collective-permute-done.2.refs_3_ = bf16[10,96,256]{2,1,0:T(8,128)(2,1)} collective-permute-done((bf16[10,96,256]{2,1,0:T(8,128)(2,1)S(1)}, bf16[10,96,256]{2,1,0:T(8,128)(2,1)}, u32[]{:S(2)}, u32[]{:S(2)}) %collective-permute-start.2) | collective-permute-done | bytes 491552 | tf_op jit(solution)/shard_map/ppermute | solution.py:514
  330.7 0.8 collective-permute-start.3
  331.6 2.0 collective-permute-start.7
  333.5 16.3 %adam.6 = (bf16[2,16,32,2560]{3,2,1,0:T(8,128)(2,1)}, bf16[2,16,32,2560]{3,2,1,0:T(8,128)(2,1)}, bf16[2,10,16,16,512]{4,3,2,1,0:T(8,128)(2,1)}, f32[2,16,32,2560...) custom-call(f32[8,128]{1,0:T(8,128)} %get-tuple-element.69.sq, ...), custom_call_target="tpu_custom_call" | custom-call | flops 1179648000 | bytes 39321600 | tf_op jit(solution)/shard_map/adam/pallas_call | solution.py:462
  349.9 16.4 %adam.7 = (bf16[2,16,32,2560]{3,2,1,0:T(8,128)(2,1)}, bf16[2,16,32,2560]{3,2,1,0:T(8,128)(2,1)}, bf16[2,10,16,16,512]{4,3,2,1,0:T(8,128)(2,1)}, f32[2,16,32,2560...) custom-call(f32[8,128]{1,0:T(8,128)} %get-tuple-element.69.sq, ...), custom_call_target="tpu_custom_call", output_to_operand_aliasing={{0}: (15, {}), {1}: (16, {}), {2}: (17, {}), {3}: (18, {}),... | custom-call | flops 1179648000 | bytes 39321600 | tf_op jit(solution)/shard_map/adam/pallas_call | solution.py:462
  366.3 12.8 %adam.8 = (bf16[2,16,32,2560]{3,2,1,0:T(8,128)(2,1)}, bf16[2,16,32,2560]{3,2,1,0:T(8,128)(2,1)}, bf16[2,10,16,16,512]{4,3,2,1,0:T(8,128)(2,1)}, f32[2,16,32,2560...) custom-call(f32[8,128]{1,0:T(8,128)} %get-tuple-element.69.sq, ...), custom_call_target="tpu_custom_call", output_to_operand_aliasing={{0}: (16, {}), {1}: (17, {}), {2}: (18, {}), {3}: (19, {}),... | custom-call | flops 884736000 | bytes 29491200 | tf_op jit(solution)/shard_map/adam/pallas_call | solution.py:462
  379.1 12.8 %adam.9 = (bf16[2,16,32,2560]{3,2,1,0:T(8,128)(2,1)}, bf16[2,16,32,2560]{3,2,1,0:T(8,128)(2,1)}, bf16[2,10,16,16,512]{4,3,2,1,0:T(8,128)(2,1)}, f32[2,16,32,2560...) custom-call(f32[8,128]{1,0:T(8,128)} %get-tuple-element.69.sq, ...), custom_call_target="tpu_custom_call", output_to_operand_aliasing={{0}: (16, {}), {1}: (17, {}), {2}: (18, {}), {3}: (19, {}),... | custom-call | flops 884736000 | bytes 29491200 | tf_op jit(solution)/shard_map/adam/pallas_call | solution.py:462
  391.9 6.0 %adam.10 = (bf16[2,16,32,2560]{3,2,1,0:T(8,128)(2,1)}, bf16[2,16,32,2560]{3,2,1,0:T(8,128)(2,1)}, bf16[2,10,16,16,512]{4,3,2,1,0:T(8,128)(2,1)}, f32[2,16,32,256...) custom-call(f32[8,128]{1,0:T(8,128)} %get-tuple-element.69.sq, ...), custom_call_target="tpu_custom_call", output_to_operand_aliasing={{0}: (12, {}), {1}: (13, {}), {2}: (14, {}), {3}: (15, {}),... | custom-call | flops 294912000 | bytes 9830400 | tf_op jit(solution)/shard_map/adam/pallas_call | solution.py:462
  397.9 5.9 %adam.11 = (bf16[2,16,32,2560]{3,2,1,0:T(8,128)(2,1)}, bf16[2,16,32,2560]{3,2,1,0:T(8,128)(2,1)}, bf16[2,10,16,16,512]{4,3,2,1,0:T(8,128)(2,1)}, f32[2,16,32,256...) custom-call(f32[8,128]{1,0:T(8,128)} %get-tuple-element.69.sq, ...), custom_call_target="tpu_custom_call", output_to_operand_aliasing={{0}: (12, {}), {1}: (13, {}), {2}: (14, {}), {3}: (15, {}),... | custom-call | flops 294912000 | bytes 9830400 | tf_op jit(solution)/shard_map/adam/pallas_call | solution.py:462
  (23 shorter events, 0.0 us)
Async XLA Ops:
  265.4 12.6 %collective-permute-start.8 = (bf16[10,96,256]{2,1,0:T(8,128)(2,1)}, bf16[10,96,256]{2,1,0:T(8,128)(2,1)S(1)}, u32[]{:S(2)}, u32[]{:S(2)}) collective-permute-start(bf16[10,96,256]{2,1,0:T(8,128)(2,1)} %get-tuple-element.72.refs_1_), channel_id=1, source_target_pairs={{0,1},{1,2},{2,3},{3,4},{4,5},{5,6},{6,7},{7,0},{8,9},{9,10},{10,1... | collective-permute-start | bytes 1474568 | tf_op jit(solution)/shard_map/ppermute | solution.py:514
  267.7 11.9 %collective-permute-start.12 = (bf16[10,96,256]{2,1,0:T(8,128)(2,1)}, bf16[10,96,256]{2,1,0:T(8,128)(2,1)S(1)}, u32[]{:S(2)}, u32[]{:S(2)}) collective-permute-start(bf16[10,96,256]{2,1,0:T(8,128)(2,1)} %get-tuple-element.73.refs_3_), channel_id=1, source_target_pairs={{0,7},{1,0},{2,1},{3,2},{4,3},{5,4},{6,5},{7,6},{8,15},{9,8},{10,9... | collective-permute-start | bytes 1474568 | tf_op jit(solution)/shard_map/ppermute | solution.py:514
  269.1 19.5 %collective-permute-start = (bf16[10,96,256]{2,1,0:T(8,128)(2,1)}, bf16[10,96,256]{2,1,0:T(8,128)(2,1)S(1)}, u32[]{:S(2)}, u32[]{:S(2)}) collective-permute-start(bf16[10,96,256]{2,1,0:T(8,128)(2,1)} %get-tuple-element.70.refs_2_), channel_id=1, source_target_pairs={{0,1},{1,2},{2,3},{3,4},{4,5},{5,6},{6,7},{7,0},{8,9},{9,10},{10,1... | collective-permute-start | bytes 1474568 | tf_op jit(solution)/shard_map/ppermute | solution.py:514
  269.1 20.2 %collective-permute-start.4 = (bf16[10,96,256]{2,1,0:T(8,128)(2,1)}, bf16[10,96,256]{2,1,0:T(8,128)(2,1)S(1)}, u32[]{:S(2)}, u32[]{:S(2)}) collective-permute-start(bf16[10,96,256]{2,1,0:T(8,128)(2,1)} %get-tuple-element.71.refs_4_), channel_id=1, source_target_pairs={{0,7},{1,0},{2,1},{3,2},{4,3},{5,4},{6,5},{7,6},{8,15},{9,8},{10,9... | collective-permute-start | bytes 1474568 | tf_op jit(solution)/shard_map/ppermute | solution.py:514
  278.0 0.8 copy-start
  278.8 20.3 %collective-permute-start.9 = (bf16[10,96,256]{2,1,0:T(8,128)(2,1)S(1)}, bf16[10,96,256]{2,1,0:T(8,128)(2,1)S(1)}, u32[]{:S(2)}, u32[]{:S(2)}) collective-permute-start(bf16[10,96,256]{2,1,0:T(8,128)(2,1)S(1)} %collective-permute-done.8.refs_0_), channel_id=1, source_target_pairs={{0,1},{1,2},{2,3},{3,4},{4,5},{5,6},{6,7},{7,0},{8,9},{9,10},{10,1... | collective-permute-start | bytes 1474568 | tf_op jit(solution)/shard_map/ppermute | solution.py:514
  279.6 41.4 %copy-start.2 = (bf16[10,96,256]{2,1,0:T(8,128)(2,1)}, bf16[10,96,256]{2,1,0:T(8,128)(2,1)S(1)}, u32[]{:S(2)}) copy-start(bf16[10,96,256]{2,1,0:T(8,128)(2,1)S(1)} %collective-permute-done.12.refs_2_) | copy-start | bytes 1474564
  279.6 20.3 %collective-permute-start.13 = (bf16[10,96,256]{2,1,0:T(8,128)(2,1)S(1)}, bf16[10,96,256]{2,1,0:T(8,128)(2,1)S(1)}, u32[]{:S(2)}, u32[]{:S(2)}) collective-permute-start(bf16[10,96,256]{2,1,0:T(8,128)(2,1)S(1)} %collective-permute-done.12.refs_2_), channel_id=1, source_target_pairs={{0,7},{1,0},{2,1},{3,2},{4,3},{5,4},{6,5},{7,6},{8,15},{9,8},{10,9... | collective-permute-start | bytes 1474568 | tf_op jit(solution)/shard_map/ppermute | solution.py:514
  288.5 34.4 %copy-start.3 = (bf16[10,96,256]{2,1,0:T(8,128)(2,1)}, bf16[10,96,256]{2,1,0:T(8,128)(2,1)S(1)}, u32[]{:S(2)}) copy-start(bf16[10,96,256]{2,1,0:T(8,128)(2,1)S(1)} %collective-permute-done.refs_1_) | copy-start | bytes 1474564
  288.5 21.1 %collective-permute-start.1 = (bf16[10,96,256]{2,1,0:T(8,128)(2,1)S(1)}, bf16[10,96,256]{2,1,0:T(8,128)(2,1)S(1)}, u32[]{:S(2)}, u32[]{:S(2)}) collective-permute-start(bf16[10,96,256]{2,1,0:T(8,128)(2,1)S(1)} %collective-permute-done.refs_1_), channel_id=1, source_target_pairs={{0,1},{1,2},{2,3},{3,4},{4,5},{5,6},{6,7},{7,0},{8,9},{9,10},{10,1... | collective-permute-start | bytes 1474568 | tf_op jit(solution)/shard_map/ppermute | solution.py:514
  289.3 41.4 %copy-start.4 = (bf16[10,96,256]{2,1,0:T(8,128)(2,1)}, bf16[10,96,256]{2,1,0:T(8,128)(2,1)S(1)}, u32[]{:S(2)}) copy-start(bf16[10,96,256]{2,1,0:T(8,128)(2,1)S(1)} %collective-permute-done.4.refs_3_) | copy-start | bytes 1474564
  289.3 21.1 %collective-permute-start.5 = (bf16[10,96,256]{2,1,0:T(8,128)(2,1)S(1)}, bf16[10,96,256]{2,1,0:T(8,128)(2,1)S(1)}, u32[]{:S(2)}, u32[]{:S(2)}) collective-permute-start(bf16[10,96,256]{2,1,0:T(8,128)(2,1)S(1)} %collective-permute-done.4.refs_3_), channel_id=1, source_target_pairs={{0,7},{1,0},{2,1},{3,2},{4,3},{5,4},{6,5},{7,6},{8,15},{9,8},{10,9... | collective-permute-start | bytes 1474568 | tf_op jit(solution)/shard_map/ppermute | solution.py:514
  299.0 32.5 %copy-start.6 = (bf16[10,96,256]{2,1,0:T(8,128)(2,1)}, bf16[10,96,256]{2,1,0:T(8,128)(2,1)S(1)}, u32[]{:S(2)}) copy-start(bf16[10,96,256]{2,1,0:T(8,128)(2,1)S(1)} %collective-permute-done.9.refs_4_) | copy-start | bytes 1474564
  299.0 21.2 %collective-permute-start.10 = (bf16[10,96,256]{2,1,0:T(8,128)(2,1)S(1)}, bf16[10,96,256]{2,1,0:T(8,128)(2,1)}, u32[]{:S(2)}, u32[]{:S(2)}) collective-permute-start(bf16[10,96,256]{2,1,0:T(8,128)(2,1)S(1)} %collective-permute-done.9.refs_4_), channel_id=1, source_target_pairs={{0,1},{1,2},{2,3},{3,4},{4,5},{5,6},{6,7},{7,0},{8,9},{9,10},{10,1... | collective-permute-start | bytes 1474568 | tf_op jit(solution)/shard_map/ppermute | solution.py:514
  299.9 0.8 copy-start.1
  300.6 20.4 %collective-permute-start.14 = (bf16[10,96,256]{2,1,0:T(8,128)(2,1)S(1)}, bf16[10,96,256]{2,1,0:T(8,128)(2,1)}, u32[]{:S(2)}, u32[]{:S(2)}) collective-permute-start(bf16[10,96,256]{2,1,0:T(8,128)(2,1)S(1)} %collective-permute-done.13.refs_0_), channel_id=1, source_target_pairs={{0,7},{1,0},{2,1},{3,2},{4,3},{5,4},{6,5},{7,6},{8,15},{9,8},{10,9... | collective-permute-start | bytes 1474568 | tf_op jit(solution)/shard_map/ppermute | solution.py:514
  309.6 24.0 %copy-start.7 = (bf16[10,96,256]{2,1,0:T(8,128)(2,1)}, bf16[10,96,256]{2,1,0:T(8,128)(2,1)S(1)}, u32[]{:S(2)}) copy-start(bf16[10,96,256]{2,1,0:T(8,128)(2,1)S(1)} %collective-permute-done.1.refs_5_) | copy-start | bytes 1474564
  309.6 21.2 %collective-permute-start.2 = (bf16[10,96,256]{2,1,0:T(8,128)(2,1)S(1)}, bf16[10,96,256]{2,1,0:T(8,128)(2,1)}, u32[]{:S(2)}, u32[]{:S(2)}) collective-permute-start(bf16[10,96,256]{2,1,0:T(8,128)(2,1)S(1)} %collective-permute-done.1.refs_5_), channel_id=1, source_target_pairs={{0,1},{1,2},{2,3},{3,4},{4,5},{5,6},{6,7},{7,0},{8,9},{9,10},{10,1... | collective-permute-start | bytes 1474568 | tf_op jit(solution)/shard_map/ppermute | solution.py:514
  310.4 21.2 %copy-start.5 = (bf16[10,96,256]{2,1,0:T(8,128)(2,1)}, bf16[10,96,256]{2,1,0:T(8,128)(2,1)S(1)}, u32[]{:S(2)}) copy-start(bf16[10,96,256]{2,1,0:T(8,128)(2,1)S(1)} %collective-permute-done.5.refs_1_) | copy-start | bytes 1474564
  310.4 21.2 %collective-permute-start.6 = (bf16[10,96,256]{2,1,0:T(8,128)(2,1)S(1)}, bf16[10,96,256]{2,1,0:T(8,128)(2,1)}, u32[]{:S(2)}, u32[]{:S(2)}) collective-permute-start(bf16[10,96,256]{2,1,0:T(8,128)(2,1)S(1)} %collective-permute-done.5.refs_1_), channel_id=1, source_target_pairs={{0,7},{1,0},{2,1},{3,2},{4,3},{5,4},{6,5},{7,6},{8,15},{9,8},{10,9... | collective-permute-start | bytes 1474568 | tf_op jit(solution)/shard_map/ppermute | solution.py:514
  320.2 71.7 %collective-permute-start.11 = (bf16[10,96,256]{2,1,0:T(8,128)(2,1)}, bf16[10,96,256]{2,1,0:T(8,128)(2,1)}, u32[]{:S(2)}, u32[]{:S(2)}) collective-permute-start(bf16[10,96,256]{2,1,0:T(8,128)(2,1)} %collective-permute-done.10.refs_2_), channel_id=1, source_target_pairs={{0,1},{1,2},{2,3},{3,4},{4,5},{5,6},{6,7},{7,0},{8,9},{9,10},{10,1... | collective-permute-start | bytes 1474568 | tf_op jit(solution)/shard_map/ppermute | solution.py:514
  321.0 70.9 %collective-permute-start.15 = (bf16[10,96,256]{2,1,0:T(8,128)(2,1)}, bf16[10,96,256]{2,1,0:T(8,128)(2,1)}, u32[]{:S(2)}, u32[]{:S(2)}) collective-permute-start(bf16[10,96,256]{2,1,0:T(8,128)(2,1)} %collective-permute-done.14.refs_4_), channel_id=1, source_target_pairs={{0,7},{1,0},{2,1},{3,2},{4,3},{5,4},{6,5},{7,6},{8,15},{9,8},{10,9... | collective-permute-start | bytes 1474568 | tf_op jit(solution)/shard_map/ppermute | solution.py:514
  330.7 67.1 %collective-permute-start.3 = (bf16[10,96,256]{2,1,0:T(8,128)(2,1)}, bf16[10,96,256]{2,1,0:T(8,128)(2,1)}, u32[]{:S(2)}, u32[]{:S(2)}) collective-permute-start(bf16[10,96,256]{2,1,0:T(8,128)(2,1)} %collective-permute-done.2.refs_3_), channel_id=1, source_target_pairs={{0,1},{1,2},{2,3},{3,4},{4,5},{5,6},{6,7},{7,0},{8,9},{9,10},{10,1... | collective-permute-start | bytes 1474568 | tf_op jit(solution)/shard_map/ppermute | solution.py:514
  331.6 66.3 %collective-permute-start.7 = (bf16[10,96,256]{2,1,0:T(8,128)(2,1)}, bf16[10,96,256]{2,1,0:T(8,128)(2,1)}, u32[]{:S(2)}, u32[]{:S(2)}) collective-permute-start(bf16[10,96,256]{2,1,0:T(8,128)(2,1)} %collective-permute-done.6.refs_5_), channel_id=1, source_target_pairs={{0,7},{1,0},{2,1},{3,2},{4,3},{5,4},{6,5},{7,6},{8,15},{9,8},{10,9... | collective-permute-start | bytes 1474568 | tf_op jit(solution)/shard_map/ppermute | solution.py:514

commit v6 on v4

--- a/solution.py
+++ b/solution.py
@@ -34,7 +34,7 @@
     lax.fori_loop(0, n, lambda i, c: (body(i), c)[1], 0)
 
 
-def train_kernel(n, rounds, x, dy, wg_h, wu_h, wd_h, G, L0, L1, sq_out, A0, A1, AT, H, DY, DYT, ACC, HID, DGU, WGU, WD, PART, RECV, SQ, SQA,
+def train_kernel(n, rounds, x, dy, wg_h, wu_h, wd_h, G, L0, L1, sq_out, A0, A1, AT, H, DY, DYT, ACC, HID, DGU, WGU, WD, PART, RECV, SQ, SQA, SQO,
                  in_sem, w_sem, rs_s, rs_r, ag_s, ag_r, own_sem, sq_sem):
     _, tokens, d = x.shape
     layers, _, ff = wg_h.shape
@@ -287,7 +287,8 @@
     total = SQA[0]
     for k in range(1, n):
         total = total + SQA[k]
-    sq_out[...] = jnp.broadcast_to(jnp.sum(total, keepdims=True), sq_out.shape)
+    SQO[...] = jnp.broadcast_to(jnp.sum(total, keepdims=True), SQO.shape)
+    sq_copy_out = pltpu.make_async_copy(SQO, sq_out, own_sem.at[1])
 
     def finish(u):
         whole(RECV.at[u], rs_s.at[u]).wait()
@@ -296,8 +297,10 @@
         ag_wait(g, rounds - 1)
         whole(RECV.at[0:JOINT, 0:rounds], ag_s.at[g]).wait()
 
+    loop(units, finish)
+    sq_copy_out.start()
     loop(groups, finish_ag)
-    loop(units, finish)
+    sq_copy_out.wait()
     whole(RECV.at[:, 0], own_sem.at[0]).wait()
     whole(SQA.at[1:n], sq_sem.at[0]).wait()
 
@@ -317,7 +320,7 @@
         name="train",
         out_shape=(jax.ShapeDtypeStruct((2, rounds, units) + part, bf16), got, got, jax.ShapeDtypeStruct((8, 128), f32)),
         in_specs=[any_] * 5,
-        out_specs=(any_, any_, any_, pl.BlockSpec(memory_space=pltpu.VMEM)),
+        out_specs=(any_,) * 4,
         scratch_shapes=[
             act, act, act_t, act, act, act_t,
             pltpu.VMEM((tokens, d), f32),
@@ -329,17 +332,72 @@
             pltpu.VMEM((units, n - 1, 2) + part, bf16),
             pltpu.VMEM(part, f32),
             pltpu.VMEM((n, 8, 128), f32),
+            pltpu.VMEM((8, 128), f32),
             dma((5,)), dma((SLOTS, 3)),
-            dma((units,)), dma((units, n - 1)), dma((units // JOINT,)), dma((units // JOINT, rounds)), dma((1,)), dma((2,)),
+            dma((units,)), dma((units, n - 1)), dma((units // JOINT,)), dma((units // JOINT, rounds)), dma((2,)), dma((2,)),
         ],
         compiler_params=pltpu.CompilerParams(collective_id=0, has_side_effects=True, vmem_limit_bytes=67043328),
         cost_estimate=pl.CostEstimate(flops=17 * 2 * tokens * d * ff, bytes_accessed=8 * units * n * rows * FC, transcendentals=0),
     )(x, dy, w_gate, w_up, w_down)
 
 
-def adam_kernel(n, count, sources, n_src, aliased, sq, *refs):
+def place_of(k, me, n, layers, first):
+    t = first + k // layers
+    h, j = lax.rem(t, 2), t // 2
+    return lax.rem(k, layers), 2 * lax.rem(me + (2 * h - 1) * j + n, n) + h
+
+
+def stage_kernel(n, first, *refs):
+    arrays, wide, tall, sem = refs[:9], refs[9:12], refs[12:15], refs[15]
+    layers, steps = arrays[0].shape[0], wide[0].shape[0]
+    me = lax.axis_index("dp")
+
+    def copies(k):
+        ly, p = place_of(k, me, n, layers, first)
+        for q in range(3):
+            for x in range(3):
+                here = tall[q].at[k] if x == 2 else wide[q].at[k, x]
+                there = arrays[3 * q + x].at[ly, :, p] if x == 2 else arrays[3 * q + x].at[ly, p]
+                yield pltpu.make_async_copy(there, here, sem.at[q, x])
+
+    def start(k):
+        for c in copies(k):
+            c.start()
+
+    loop(steps, start)
+    for q in range(3):
+        for x in range(2):
+            both = wide[q].at[:, x]
+            pltpu.make_async_copy(both, both, sem.at[q, x]).wait()
+        pltpu.make_async_copy(tall[q], tall[q], sem.at[q, 2]).wait()
+
+
+def stage(views, first, steps, n):
+    w, m, v = views
+    _, _, rows_p, ff = w[0].shape
+    _, chunks, _, rows_d, d = w[2].shape
+    types = (bf16, f32, f32)
+    shapes = [jax.ShapeDtypeStruct((steps, 2, rows_p, ff), t) for t in types] + [jax.ShapeDtypeStruct((steps, chunks, rows_d, d), t) for t in types]
+    return pl.pallas_call(
+        functools.partial(stage_kernel, n, first),
+        name="stage",
+        in_specs=[pl.BlockSpec(memory_space=pltpu.HBM)] * 9,
+        out_specs=[pl.BlockSpec(memory_space=pltpu.VMEM)] * 6,
+        out_shape=shapes,
+        scratch_shapes=[pltpu.SemaphoreType.DMA((3, 3))],
+        compiler_params=pltpu.CompilerParams(vmem_limit_bytes=44 << 20),
+        cost_estimate=pl.CostEstimate(flops=3000000000, bytes_accessed=10000000, transcendentals=0),
+    )(*w, *m, *v)
+
+
+def adam_kernel(n, count, sources, n_src, aliased, staged, sq, *refs):
     gs, w, m, v = refs[:n_src], refs[n_src : n_src + 3], refs[n_src + 3 : n_src + 6], refs[n_src + 6 : n_src + 9]
-    refs = refs[n_src + 9 + (9 if aliased else 0) :]
+    if staged:
+        old_wide, old_tall = refs[n_src : n_src + 3], refs[n_src + 3 : n_src + 6]
+        refs = refs[n_src + 6 + (9 if aliased else 0) :]
+        w = refs[:3]
+    else:
+        refs = refs[n_src + 9 + (9 if aliased else 0) :]
     outs, g_in, wide, tall, in_sem, out_sem = refs[:9], refs[9], refs[10:13], refs[13:16], refs[16], refs[17]
     layers, _, rows_p, _ = w[0].shape
     _, chunks, _, rows_d, d = w[2].shape
@@ -349,9 +407,7 @@
     _, h0, j0 = sources[0]
 
     def place(k):
-        t = 2 * j0 + h0 + k // layers
-        h, j = lax.rem(t, 2), t // 2
-        return lax.rem(k, layers), 2 * lax.rem(me + (2 * h - 1) * j + n, n) + h
+        return place_of(k, me, n, layers, 2 * j0 + h0)
 
     def state(k, arrays, sem, out):
         ly, p = place(k)
@@ -384,8 +440,9 @@
     spans = [[t for t, src in enumerate(sources) if src[0] == x] for x in range(n_src)]
 
     def start(k):
-        for c in taken(k):
-            c.start()
+        if not staged:
+            for c in taken(k):
+                c.start()
         for x, span in enumerate(spans):
 
             @pl.when((k >= layers * span[0]) & (k < layers * (span[-1] + 1)))
@@ -395,27 +452,28 @@
     loop(min(depth - 2, steps), start)
     factor = jnp.minimum(1.0, 0.5 * lax.rsqrt(sq[0:1, 0:1] / count + 1e-30))
 
-    def update(g, rows):
+    def update(g, arrays, old_arrays, at):
         g = g.astype(f32) * factor
-        w, m, v = rows
-        new_m = 0.9 * m[...] + 0.1 * g
-        new_v = 0.95 * v[...] + 0.05 * g * g
-        old = w[...].astype(f32)
+        w, m, v = (a.at[at] for a in arrays)
+        old_w, old_m, old_v = (a.at[at] for a in old_arrays)
+        new_m = 0.9 * old_m[...] + 0.1 * g
+        new_v = 0.95 * old_v[...] + 0.05 * g * g
+        old = old_w[...].astype(f32)
         m[...] = new_m
         v[...] = new_v
         w[...] = (old - 0.02 * (new_m * lax.rsqrt(new_v + 1e-8) + 0.1 * old)).astype(bf16)
 
     def step(k):
         slot = lax.rem(k, depth)
-        arrived(k, in_sem, 6)
+        arrived(k, in_sem, 1 if staged else 6)
 
         def chunk(c):
             cols = pl.ds(pl.multiple_of(c * FC, FC), FC)
             for x in range(2):
-                update(g_in[slot, c, x * rows_p : (x + 1) * rows_p], [a.at[slot, x, :, cols] for a in wide])
+                update(g_in[slot, c, x * rows_p : (x + 1) * rows_p], wide, old_wide if staged else wide, (slot, x, slice(None), cols))
             for x in range(d // FC):
                 at = 2 * rows_p + x * rows_d
-                update(g_in[slot, c, at : at + rows_d], [a.at[slot, c, :, x * FC : (x + 1) * FC] for a in tall])
+                update(g_in[slot, c, at : at + rows_d], tall, old_tall if staged else tall, (slot, c, slice(None), slice(x * FC, (x + 1) * FC)))
 
         loop(chunks, chunk)
         for c in given(k):
@@ -437,12 +495,12 @@
     loop(2, finish)
 
 
-def adam(views, prev, sq, gs, sources, n, count):
+def adam(views, prev, sq, gs, sources, n, count, staged=None):
     w, m, v = views
     _, parts, rows_p, ff = w[0].shape
     _, chunks, _, rows_d, d = w[2].shape
-    any_ = pl.BlockSpec(memory_space=pl.ANY)
-    args = [*gs, *w, *m, *v]
+    any_, vmem = pl.BlockSpec(memory_space=pl.ANY), pl.BlockSpec(memory_space=pltpu.VMEM)
+    args = [*gs, *(staged or (*w, *m, *v))]
     aliases = {}
     if prev is not None:
         aliases = {1 + len(args) + k: k for k in range(9)}
@@ -450,9 +508,9 @@
     moved = 2 * len(sources) * sum(a.size * a.dtype.itemsize for a in (*w, *m, *v)) // parts
     types = (bf16, f32, f32)
     return pl.pallas_call(
-        functools.partial(adam_kernel, n, count, sources, len(gs), prev is not None),
+        functools.partial(adam_kernel, n, count, sources, len(gs), prev is not None, bool(staged)),
         name="adam",
-        in_specs=[pl.BlockSpec(memory_space=pltpu.VMEM)] + [any_] * len(args),
+        in_specs=[vmem] + [any_] * len(gs) + [vmem if staged else any_] * (6 if staged else 9) + [any_] * (0 if prev is None else 9),
         out_specs=[any_] * 9,
         out_shape=[jax.ShapeDtypeStruct(a.shape, a.dtype) for a in (*w, *m, *v)],
         input_output_aliases=aliases,
@@ -460,7 +518,7 @@
         + [pltpu.VMEM((DEPTH, 2, rows_p, ff), t) for t in types]
         + [pltpu.VMEM((DEPTH, chunks, rows_d, d), t) for t in types]
         + [pltpu.SemaphoreType.DMA((DEPTH,)), pltpu.SemaphoreType.DMA((DEPTH,))],
-        compiler_params=pltpu.CompilerParams(vmem_limit_bytes=67043328),
+        compiler_params=pltpu.CompilerParams(vmem_limit_bytes=(44 << 20) if staged else 67043328),
         cost_estimate=pl.CostEstimate(flops=30 * moved, bytes_accessed=moved, transcendentals=0),
     )(sq, *args)
 
@@ -503,7 +561,9 @@
                     gs.append(g)
                 sources.append((len(gs) - 1, h, j))
             at += len(sources)
-            out = adam(views, out, sq, gs, sources, n, count)
+            out = adam(views, out, sq, gs, sources, n, count, staged if k == hops else None)
+            if k == hops - 1:
+                staged = stage(views, at, 2 * layers, n)
         return tuple(o.reshape(a.shape) for o, a in zip(out, arrays, strict=True))
 
     return jax.shard_map(

time: 407 us -> 423 us (1.039)
  local copies, waits for them, and re-layouts: 1.06 us -> 15.6 us
    unnamed x8 -> x32, local copies, waits for them, and re-layouts: 1.06 us -> 15.6 us
where the time goes in v6:
time: 423 us; the launch traced here: 418 us
  Pallas kernels  334 us (79%)
  waiting for transfers between devices  54.7 us (13%)
  local copies, waits for them, and re-layouts  15.6 us (4%)
  starting transfers between devices  12.3 us (3%)
    pallas_call x1, Pallas kernels, train(): pl.pallas_call(functools.partial(train_kernel, n, rounds), name='train',...  264 us
    pallas_call x5, Pallas kernels, adam(): pl.pallas_call(functools.partial(adam_kernel, n, count, sources, len(gs),...  66.3 us
    ppermute x4, waiting for transfers between devices, whole(): r = lax.ppermute(came[k][0], 'dp', right)  54.7 us
    unnamed x32, local copies, waits for them, and re-layouts  15.6 us
    ppermute x4, starting transfers between devices, whole(): came.append([r, lax.ppermute(came[k][1], 'dp', left)])  8.79 us
  transfers between devices with their start and end apart: 8, of which 3 were waited for; matrix products, arithmetic and copies ran while one was open for 0% of the time, Pallas kernels for 15%

profile of v6, /device:TPU:21, one launch (start us, length us, event | category | flops | bytes accessed | tf_op | source)
XLA Modules:
  0.0 417.8 jit_solution(4683797043324162172)
XLA Ops:
  0.6 263.9 %train.1 = (bf16[2,3,20,96,256]{4,3,2,1,0:T(8,128)(2,1)}, bf16[20,96,256]{2,1,0:T(8,128)(2,1)}, bf16[20,96,256]{2,1,0:T(8,128)(2,1)}, f32[8,128]{1,0:T(8,128)}) custom-call(bf16[1,2048,512]{2,1,0:T(8,128)(2,1)} %x.1, bf16[1,2048,512]{2,1,0:T(8,128)(2,1)} %dy.1, bf16[2,512,2560]{2,1,0:T(8,128)(2,1)} %wg_h.1, bf16[2,512,2560]{2,1,0:T(8,128)(2,1)} %wu_h.1, ...), custom_call_target="tpu_custom_call" | custom-call | flops 91268055040 | bytes 31457280 | tf_op jit(solution)/shard_map/train/pallas_call | solution.py:318
  264.6 2.2 collective-permute-start
  266.8 1.4 collective-permute-start.4
  268.2 19.5 %collective-permute-done.refs_0_ = bf16[20,96,256]{2,1,0:T(8,128)(2,1)S(1)} collective-permute-done((bf16[20,96,256]{2,1,0:T(8,128)(2,1)}, bf16[20,96,256]{2,1,0:T(8,128)(2,1)S(1)}, u32[]{:S(2)}, u32[]{:S(2)}) %collective-permute-start) | collective-permute-done | bytes 983072 | tf_op jit(solution)/shard_map/ppermute | solution.py:554
  287.6 0.8 collective-permute-start.1
  288.5 0.0 collective-permute-done.4.refs_1_
  288.5 1.8 collective-permute-start.5
  290.3 18.5 %collective-permute-done.1.refs_2_ = bf16[20,96,256]{2,1,0:T(8,128)(2,1)S(1)} collective-permute-done((bf16[20,96,256]{2,1,0:T(8,128)(2,1)S(1)}, bf16[20,96,256]{2,1,0:T(8,128)(2,1)S(1)}, u32[]{:S(2)}, u32[]{:S(2)}) %collective-permute-start.1) | collective-permute-done | bytes 983072 | tf_op jit(solution)/shard_map/ppermute | solution.py:554
  308.8 0.3 collective-permute-start.2
  309.1 1.0 copy-done.12
  310.1 2.4 collective-permute-start.6
  312.4 16.8 %collective-permute-done.2.refs_1_ = bf16[20,96,256]{2,1,0:T(8,128)(2,1)} collective-permute-done((bf16[20,96,256]{2,1,0:T(8,128)(2,1)S(1)}, bf16[20,96,256]{2,1,0:T(8,128)(2,1)}, u32[]{:S(2)}, u32[]{:S(2)}) %collective-permute-start.2) | collective-permute-done | bytes 983072 | tf_op jit(solution)/shard_map/ppermute | solution.py:554
  329.2 0.2 collective-permute-start.3
  329.4 3.2 collective-permute-start.7
  332.6 16.3 %adam.5 = (bf16[2,16,32,2560]{3,2,1,0:T(8,128)(2,1)}, bf16[2,16,32,2560]{3,2,1,0:T(8,128)(2,1)}, bf16[2,10,16,16,512]{4,3,2,1,0:T(8,128)(2,1)}, f32[2,16,32,2560...) custom-call(f32[8,128]{1,0:T(8,128)} %get-tuple-element.64.sq, ...), custom_call_target="tpu_custom_call" | custom-call | flops 1179648000 | bytes 39321600 | tf_op jit(solution)/shard_map/adam/pallas_call | solution.py:510
  348.9 16.4 %adam.6 = (bf16[2,16,32,2560]{3,2,1,0:T(8,128)(2,1)}, bf16[2,16,32,2560]{3,2,1,0:T(8,128)(2,1)}, bf16[2,10,16,16,512]{4,3,2,1,0:T(8,128)(2,1)}, f32[2,16,32,2560...) custom-call(f32[8,128]{1,0:T(8,128)} %get-tuple-element.64.sq, ...), custom_call_target="tpu_custom_call", output_to_operand_aliasing={{0}: (13, {}), {1}: (14, {}), {2}: (15, {}), {3}: (16, {}),... | custom-call | flops 1179648000 | bytes 39321600 | tf_op jit(solution)/shard_map/adam/pallas_call | solution.py:510
  365.3 4.0 stage.1
  369.4 1.5 copy-done
  370.9 1.5 copy-done.2
  372.4 1.1 copy-done.3
  373.5 1.1 copy-done.5
  374.6 1.2 copy-done.7
  375.7 0.9 copy-done.9
  376.6 12.7 %adam.7 = (bf16[2,16,32,2560]{3,2,1,0:T(8,128)(2,1)}, bf16[2,16,32,2560]{3,2,1,0:T(8,128)(2,1)}, bf16[2,10,16,16,512]{4,3,2,1,0:T(8,128)(2,1)}, f32[2,16,32,2560...) custom-call(f32[8,128]{1,0:T(8,128)} %get-tuple-element.64.sq, ...), custom_call_target="tpu_custom_call", output_to_operand_aliasing={{0}: (13, {}), {1}: (14, {}), {2}: (15, {}), {3}: (16, {}),... | custom-call | flops 884736000 | bytes 29491200 | tf_op jit(solution)/shard_map/adam/pallas_call | solution.py:510
  389.3 12.8 %adam.8 = (bf16[2,16,32,2560]{3,2,1,0:T(8,128)(2,1)}, bf16[2,16,32,2560]{3,2,1,0:T(8,128)(2,1)}, bf16[2,10,16,16,512]{4,3,2,1,0:T(8,128)(2,1)}, f32[2,16,32,2560...) custom-call(f32[8,128]{1,0:T(8,128)} %get-tuple-element.64.sq, ...), custom_call_target="tpu_custom_call", output_to_operand_aliasing={{0}: (13, {}), {1}: (14, {}), {2}: (15, {}), {3}: (16, {}),... | custom-call | flops 884736000 | bytes 29491200 | tf_op jit(solution)/shard_map/adam/pallas_call | solution.py:510
  402.1 1.7 copy-done.1
  403.8 1.3 copy-done.4
  405.2 1.3 copy-done.6
  406.5 1.3 copy-done.8
  407.8 1.1 copy-done.10
  408.9 0.7 copy-done.11
  409.6 8.1 %adam.9 = (bf16[2,16,32,2560]{3,2,1,0:T(8,128)(2,1)}, bf16[2,16,32,2560]{3,2,1,0:T(8,128)(2,1)}, bf16[2,10,16,16,512]{4,3,2,1,0:T(8,128)(2,1)}, f32[2,16,32,2560...) custom-call(f32[8,128]{1,0:T(8,128)S(1)} %copy-done.11, ...), custom_call_target="tpu_custom_call", output_to_operand_aliasing={{0}: (9, {}), {1}: (10, {}), {2}: (11, {}), {3}: (12, {}), ... | custom-call | flops 589824000 | bytes 19660800 | tf_op jit(solution)/shard_map/adam/pallas_call | solution.py:510
  (23 shorter events, 0.0 us)
Async XLA Ops:
  264.6 23.1 %collective-permute-start = (bf16[20,96,256]{2,1,0:T(8,128)(2,1)}, bf16[20,96,256]{2,1,0:T(8,128)(2,1)S(1)}, u32[]{:S(2)}, u32[]{:S(2)}) collective-permute-start(bf16[20,96,256]{2,1,0:T(8,128)(2,1)} %get-tuple-element.65.refs_1_), channel_id=1, source_target_pairs={{0,1},{1,2},{2,3},{3,4},{4,5},{5,6},{6,7},{7,0},{8,9},{9,10},{10,1... | collective-permute-start | bytes 2949128 | tf_op jit(solution)/shard_map/ppermute | solution.py:554
  266.8 21.7 %collective-permute-start.4 = (bf16[20,96,256]{2,1,0:T(8,128)(2,1)}, bf16[20,96,256]{2,1,0:T(8,128)(2,1)S(1)}, u32[]{:S(2)}, u32[]{:S(2)}) collective-permute-start(bf16[20,96,256]{2,1,0:T(8,128)(2,1)} %get-tuple-element.66.refs_2_), channel_id=1, source_target_pairs={{0,7},{1,0},{2,1},{3,2},{4,3},{5,4},{6,5},{7,6},{8,15},{9,8},{10,9... | collective-permute-start | bytes 2949128 | tf_op jit(solution)/shard_map/ppermute | solution.py:555
  287.6 41.8 %copy-start.13 = (bf16[20,96,256]{2,1,0:T(8,128)(2,1)}, bf16[20,96,256]{2,1,0:T(8,128)(2,1)S(1)}, u32[]{:S(2)}) copy-start(bf16[20,96,256]{2,1,0:T(8,128)(2,1)S(1)} %collective-permute-done.refs_0_) | copy-start | bytes 2949124
  287.6 21.2 %collective-permute-start.1 = (bf16[20,96,256]{2,1,0:T(8,128)(2,1)S(1)}, bf16[20,96,256]{2,1,0:T(8,128)(2,1)S(1)}, u32[]{:S(2)}, u32[]{:S(2)}) collective-permute-start(bf16[20,96,256]{2,1,0:T(8,128)(2,1)S(1)} %collective-permute-done.refs_0_), channel_id=1, source_target_pairs={{0,1},{1,2},{2,3},{3,4},{4,5},{5,6},{6,7},{7,0},{8,9},{9,10},{10,1... | collective-permute-start | bytes 2949128 | tf_op jit(solution)/shard_map/ppermute | solution.py:554
  288.5 44.1 %copy-start.14 = (bf16[20,96,256]{2,1,0:T(8,128)(2,1)}, bf16[20,96,256]{2,1,0:T(8,128)(2,1)S(1)}, u32[]{:S(2)}) copy-start(bf16[20,96,256]{2,1,0:T(8,128)(2,1)S(1)} %collective-permute-done.4.refs_1_) | copy-start | bytes 2949124
  288.5 20.6 %collective-permute-start.5 = (bf16[20,96,256]{2,1,0:T(8,128)(2,1)S(1)}, bf16[20,96,256]{2,1,0:T(8,128)(2,1)S(1)}, u32[]{:S(2)}, u32[]{:S(2)}) collective-permute-start(bf16[20,96,256]{2,1,0:T(8,128)(2,1)S(1)} %collective-permute-done.4.refs_1_), channel_id=1, source_target_pairs={{0,7},{1,0},{2,1},{3,2},{4,3},{5,4},{6,5},{7,6},{8,15},{9,8},{10,9... | collective-permute-start | bytes 2949128 | tf_op jit(solution)/shard_map/ppermute | solution.py:555
  308.8 23.8 %copy-start.15 = (bf16[20,96,256]{2,1,0:T(8,128)(2,1)}, bf16[20,96,256]{2,1,0:T(8,128)(2,1)S(1)}, u32[]{:S(2)}) copy-start(bf16[20,96,256]{2,1,0:T(8,128)(2,1)S(1)} %collective-permute-done.1.refs_2_) | copy-start | bytes 2949124
  308.8 20.4 %collective-permute-start.2 = (bf16[20,96,256]{2,1,0:T(8,128)(2,1)S(1)}, bf16[20,96,256]{2,1,0:T(8,128)(2,1)}, u32[]{:S(2)}, u32[]{:S(2)}) collective-permute-start(bf16[20,96,256]{2,1,0:T(8,128)(2,1)S(1)} %collective-permute-done.1.refs_2_), channel_id=1, source_target_pairs={{0,1},{1,2},{2,3},{3,4},{4,5},{5,6},{6,7},{7,0},{8,9},{9,10},{10,1... | collective-permute-start | bytes 2949128 | tf_op jit(solution)/shard_map/ppermute | solution.py:554
  309.1 1.0 copy-start.12
  310.1 19.3 %collective-permute-start.6 = (bf16[20,96,256]{2,1,0:T(8,128)(2,1)S(1)}, bf16[20,96,256]{2,1,0:T(8,128)(2,1)}, u32[]{:S(2)}, u32[]{:S(2)}) collective-permute-start(bf16[20,96,256]{2,1,0:T(8,128)(2,1)S(1)} %collective-permute-done.5.refs_0_), channel_id=1, source_target_pairs={{0,7},{1,0},{2,1},{3,2},{4,3},{5,4},{6,5},{7,6},{8,15},{9,8},{10,9... | collective-permute-start | bytes 2949128 | tf_op jit(solution)/shard_map/ppermute | solution.py:555
  329.2 72.9 %collective-permute-start.3 = (bf16[20,96,256]{2,1,0:T(8,128)(2,1)}, bf16[20,96,256]{2,1,0:T(8,128)(2,1)}, u32[]{:S(2)}, u32[]{:S(2)}) collective-permute-start(bf16[20,96,256]{2,1,0:T(8,128)(2,1)} %collective-permute-done.2.refs_1_), channel_id=1, source_target_pairs={{0,1},{1,2},{2,3},{3,4},{4,5},{5,6},{6,7},{7,0},{8,9},{9,10},{10,1... | collective-permute-start | bytes 2949128 | tf_op jit(solution)/shard_map/ppermute | solution.py:554
  329.4 72.7 %collective-permute-start.7 = (bf16[20,96,256]{2,1,0:T(8,128)(2,1)}, bf16[20,96,256]{2,1,0:T(8,128)(2,1)}, u32[]{:S(2)}, u32[]{:S(2)}) collective-permute-start(bf16[20,96,256]{2,1,0:T(8,128)(2,1)} %collective-permute-done.6.refs_2_), channel_id=1, source_target_pairs={{0,7},{1,0},{2,1},{3,2},{4,3},{5,4},{6,5},{7,6},{8,15},{9,8},{10,9... | collective-permute-start | bytes 2949128 | tf_op jit(solution)/shard_map/ppermute | solution.py:555
  369.4 1.5 copy-start
  370.9 1.5 copy-start.2
  372.4 1.1 copy-start.3
  373.5 1.1 copy-start.5
  374.6 1.2 copy-start.7
  375.7 0.9 copy-start.9
  402.1 1.7 copy-start.1
  403.8 1.3 copy-start.4
  405.2 1.3 copy-start.6
  406.5 1.3 copy-start.8
  407.8 1.1 copy-start.10
  408.9 0.7 copy-start.11

commit v7 on v6

--- a/solution.py
+++ b/solution.py
@@ -14,6 +14,7 @@
 SLOTS = 4
 JOINT = 2
 HELD = 3
+LIMITS = {1: 61 << 20, 0: 24 << 20}
 DEPTH = 6
 TILE = 1024
 
@@ -385,7 +386,7 @@
         out_specs=[pl.BlockSpec(memory_space=pltpu.VMEM)] * 6,
         out_shape=shapes,
         scratch_shapes=[pltpu.SemaphoreType.DMA((3, 3))],
-        compiler_params=pltpu.CompilerParams(vmem_limit_bytes=44 << 20),
+        compiler_params=pltpu.CompilerParams(vmem_limit_bytes=40 << 20),
         cost_estimate=pl.CostEstimate(flops=3000000000, bytes_accessed=10000000, transcendentals=0),
     )(*w, *m, *v)
 
@@ -398,7 +399,7 @@
         w = refs[:3]
     else:
         refs = refs[n_src + 9 + (9 if aliased else 0) :]
-    outs, g_in, wide, tall, in_sem, out_sem = refs[:9], refs[9], refs[10:13], refs[13:16], refs[16], refs[17]
+    outs, g_in, wide, tall, in_sem, out_sem = refs[:9], refs[9], refs[10:13], refs[13:16], *refs[16:18]
     layers, _, rows_p, _ = w[0].shape
     _, chunks, _, rows_d, d = w[2].shape
     depth = g_in.shape[0]
@@ -440,16 +441,16 @@
     spans = [[t for t, src in enumerate(sources) if src[0] == x] for x in range(n_src)]
 
     def start(k):
-        if not staged:
-            for c in taken(k):
-                c.start()
+        for c in taken(k):
+            c.start()
         for x, span in enumerate(spans):
 
             @pl.when((k >= layers * span[0]) & (k < layers * (span[-1] + 1)))
             def _():
                 gradient(k, x, span[0]).start()
 
-    loop(min(depth - 2, steps), start)
+    if not staged:
+        loop(min(depth - 2, steps), start)
     factor = jnp.minimum(1.0, 0.5 * lax.rsqrt(sq[0:1, 0:1] / count + 1e-30))
 
     def update(g, arrays, old_arrays, at):
@@ -465,17 +466,26 @@
 
     def step(k):
         slot = lax.rem(k, depth)
-        arrived(k, in_sem, 1 if staged else 6)
-
-        def chunk(c):
-            cols = pl.ds(pl.multiple_of(c * FC, FC), FC)
-            for x in range(2):
-                update(g_in[slot, c, x * rows_p : (x + 1) * rows_p], wide, old_wide if staged else wide, (slot, x, slice(None), cols))
-            for x in range(d // FC):
-                at = 2 * rows_p + x * rows_d
-                update(g_in[slot, c, at : at + rows_d], tall, old_tall if staged else tall, (slot, c, slice(None), slice(x * FC, (x + 1) * FC)))
-
-        loop(chunks, chunk)
+        back = layers - 1 - place(k)[0]
+        if not staged:
+            arrived(k, in_sem, 6)
+
+        def run(g, first):
+            def chunk(c):
+                cols = pl.ds(pl.multiple_of(c * FC, FC), FC)
+                for x in range(2):
+                    update(g[first + c, x * rows_p : (x + 1) * rows_p], wide, old_wide if staged else wide, (slot, x, slice(None), cols))
+                for x in range(d // FC):
+                    at = 2 * rows_p + x * rows_d
+                    update(g[first + c, at : at + rows_d], tall, old_tall if staged else tall, (slot, c, slice(None), slice(x * FC, (x + 1) * FC)))
+
+            lax.fori_loop(0, chunks, lambda c, x: (chunk(c), x)[1], 0, unroll=5 if staged else 1)
+
+        if staged:
+            for x, span in enumerate(spans):
+                pl.when((k >= layers * span[0]) & (k < layers * (span[-1] + 1)))(functools.partial(run, gs[x], back * chunks))
+        else:
+            run(g_in.at[slot], 0)
         for c in given(k):
             c.start()
 
@@ -483,9 +493,11 @@
         def _():
             arrived(k - 2, out_sem, 5)
 
-        @pl.when(k + depth - 2 < steps)
-        def _():
-            start(k + depth - 2)
+        if not staged:
+
+            @pl.when(k + depth - 2 < steps)
+            def _():
+                start(k + depth - 2)
 
     loop(steps, step)
 
@@ -495,7 +507,7 @@
     loop(2, finish)
 
 
-def adam(views, prev, sq, gs, sources, n, count, staged=None):
+def adam(views, prev, sq, gs, sources, n, count, staged=None, limit=67043328):
     w, m, v = views
     _, parts, rows_p, ff = w[0].shape
     _, chunks, _, rows_d, d = w[2].shape
@@ -510,7 +522,7 @@
     return pl.pallas_call(
         functools.partial(adam_kernel, n, count, sources, len(gs), prev is not None, bool(staged)),
         name="adam",
-        in_specs=[vmem] + [any_] * len(gs) + [vmem if staged else any_] * (6 if staged else 9) + [any_] * (0 if prev is None else 9),
+        in_specs=[vmem] + [vmem if staged else any_] * len(gs) + [vmem if staged else any_] * (6 if staged else 9) + [any_] * (0 if prev is None else 9),
         out_specs=[any_] * 9,
         out_shape=[jax.ShapeDtypeStruct(a.shape, a.dtype) for a in (*w, *m, *v)],
         input_output_aliases=aliases,
@@ -518,7 +530,7 @@
         + [pltpu.VMEM((DEPTH, 2, rows_p, ff), t) for t in types]
         + [pltpu.VMEM((DEPTH, chunks, rows_d, d), t) for t in types]
         + [pltpu.SemaphoreType.DMA((DEPTH,)), pltpu.SemaphoreType.DMA((DEPTH,))],
-        compiler_params=pltpu.CompilerParams(vmem_limit_bytes=(44 << 20) if staged else 67043328),
+        compiler_params=pltpu.CompilerParams(vmem_limit_bytes=limit),
         cost_estimate=pl.CostEstimate(flops=30 * moved, bytes_accessed=moved, transcendentals=0),
     )(sq, *args)
 
@@ -561,7 +573,7 @@
                     gs.append(g)
                 sources.append((len(gs) - 1, h, j))
             at += len(sources)
-            out = adam(views, out, sq, gs, sources, n, count, staged if k == hops else None)
+            out = adam(views, out, sq, gs, sources, n, count, staged if k == hops else None, LIMITS.get(hops - k, 67043328))
             if k == hops - 1:
                 staged = stage(views, at, 2 * layers, n)
         return tuple(o.reshape(a.shape) for o, a in zip(out, arrays, strict=True))

time: 423 us -> 421 us (level)
    unnamed x32 -> x34, local copies, waits for them, and re-layouts: 15.6 us -> 14.9 us
where the time goes in v7:
time: 421 us; the launch traced here: 415 us
  Pallas kernels  332 us (79%)
  waiting for transfers between devices  54.7 us (13%)
  local copies, waits for them, and re-layouts  14.9 us (4%)
  starting transfers between devices  12.3 us (3%)
    pallas_call x1, Pallas kernels, train(): pl.pallas_call(functools.partial(train_kernel, n, rounds), name='train',...  264 us
    pallas_call x5, Pallas kernels, adam(): pl.pallas_call(functools.partial(adam_kernel, n, count, sources, len(gs),...  64.4 us
    ppermute x4, waiting for transfers between devices, whole(): r = lax.ppermute(came[k][0], 'dp', right)  54.7 us
    unnamed x34, local copies, waits for them, and re-layouts  14.9 us
    ppermute x4, starting transfers between devices, whole(): came.append([r, lax.ppermute(came[k][1], 'dp', left)])  8.82 us
  transfers between devices with their start and end apart: 8, of which 3 were waited for; matrix products, arithmetic and copies ran while one was open for 0% of the time, Pallas kernels for 15%

profile of v7, /device:TPU:21, one launch (start us, length us, event | category | flops | bytes accessed | tf_op | source)
XLA Modules:
  0.0 415.2 jit_solution(17189949154080109610)
XLA Ops:
  0.6 263.9 %train.1 = (bf16[2,3,20,96,256]{4,3,2,1,0:T(8,128)(2,1)}, bf16[20,96,256]{2,1,0:T(8,128)(2,1)}, bf16[20,96,256]{2,1,0:T(8,128)(2,1)}, f32[8,128]{1,0:T(8,128)}) custom-call(bf16[1,2048,512]{2,1,0:T(8,128)(2,1)} %x.1, bf16[1,2048,512]{2,1,0:T(8,128)(2,1)} %dy.1, bf16[2,512,2560]{2,1,0:T(8,128)(2,1)} %wg_h.1, bf16[2,512,2560]{2,1,0:T(8,128)(2,1)} %wu_h.1, ...), custom_call_target="tpu_custom_call" | custom-call | flops 91268055040 | bytes 31457280 | tf_op jit(solution)/shard_map/train/pallas_call | solution.py:319
  264.6 2.2 collective-permute-start
  266.8 1.4 collective-permute-start.4
  268.2 19.5 %collective-permute-done.refs_0_ = bf16[20,96,256]{2,1,0:T(8,128)(2,1)S(1)} collective-permute-done((bf16[20,96,256]{2,1,0:T(8,128)(2,1)}, bf16[20,96,256]{2,1,0:T(8,128)(2,1)S(1)}, u32[]{:S(2)}, u32[]{:S(2)}) %collective-permute-start) | collective-permute-done | bytes 983072 | tf_op jit(solution)/shard_map/ppermute | solution.py:566
  287.6 0.8 collective-permute-start.1
  288.5 0.0 collective-permute-done.4.refs_1_
  288.5 1.8 collective-permute-start.5
  290.3 18.5 %collective-permute-done.1.refs_2_ = bf16[20,96,256]{2,1,0:T(8,128)(2,1)S(1)} collective-permute-done((bf16[20,96,256]{2,1,0:T(8,128)(2,1)S(1)}, bf16[20,96,256]{2,1,0:T(8,128)(2,1)S(1)}, u32[]{:S(2)}, u32[]{:S(2)}) %collective-permute-start.1) | collective-permute-done | bytes 983072 | tf_op jit(solution)/shard_map/ppermute | solution.py:566
  308.8 0.3 collective-permute-start.2
  309.1 0.0 collective-permute-done.5.refs_0_
  309.1 1.0 copy-done.13
  310.1 2.4 collective-permute-start.6
  312.5 16.8 %collective-permute-done.2.refs_1_ = bf16[20,96,256]{2,1,0:T(8,128)(2,1)} collective-permute-done((bf16[20,96,256]{2,1,0:T(8,128)(2,1)S(1)}, bf16[20,96,256]{2,1,0:T(8,128)(2,1)}, u32[]{:S(2)}, u32[]{:S(2)}) %collective-permute-start.2) | collective-permute-done | bytes 983072 | tf_op jit(solution)/shard_map/ppermute | solution.py:566
  329.2 0.2 collective-permute-start.3
  329.4 3.2 collective-permute-start.7
  332.6 16.3 %adam.5 = (bf16[2,16,32,2560]{3,2,1,0:T(8,128)(2,1)}, bf16[2,16,32,2560]{3,2,1,0:T(8,128)(2,1)}, bf16[2,10,16,16,512]{4,3,2,1,0:T(8,128)(2,1)}, f32[2,16,32,2560...) custom-call(f32[8,128]{1,0:T(8,128)} %get-tuple-element.64.sq, ...), custom_call_target="tpu_custom_call" | custom-call | flops 1179648000 | bytes 39321600 | tf_op jit(solution)/shard_map/adam/pallas_call | solution.py:522
  348.9 16.4 %adam.6 = (bf16[2,16,32,2560]{3,2,1,0:T(8,128)(2,1)}, bf16[2,16,32,2560]{3,2,1,0:T(8,128)(2,1)}, bf16[2,10,16,16,512]{4,3,2,1,0:T(8,128)(2,1)}, f32[2,16,32,2560...) custom-call(f32[8,128]{1,0:T(8,128)} %get-tuple-element.64.sq, ...), custom_call_target="tpu_custom_call", output_to_operand_aliasing={{0}: (13, {}), {1}: (14, {}), {2}: (15, {}), {3}: (16, {}),... | custom-call | flops 1179648000 | bytes 39321600 | tf_op jit(solution)/shard_map/adam/pallas_call | solution.py:522
  365.4 4.0 stage.1
  369.4 1.5 copy-done
  370.9 1.5 copy-done.2
  372.4 1.1 copy-done.4
  373.5 1.1 copy-done.6
  374.6 1.2 copy-done.8
  375.7 0.8 copy-done.10
  376.6 12.7 %adam.7 = (bf16[2,16,32,2560]{3,2,1,0:T(8,128)(2,1)}, bf16[2,16,32,2560]{3,2,1,0:T(8,128)(2,1)}, bf16[2,10,16,16,512]{4,3,2,1,0:T(8,128)(2,1)}, f32[2,16,32,2560...) custom-call(f32[8,128]{1,0:T(8,128)} %get-tuple-element.64.sq, ...), custom_call_target="tpu_custom_call", output_to_operand_aliasing={{0}: (13, {}), {1}: (14, {}), {2}: (15, {}), {3}: (16, {}),... | custom-call | flops 884736000 | bytes 29491200 | tf_op jit(solution)/shard_map/adam/pallas_call | solution.py:522
  389.3 12.9 %adam.8 = (bf16[2,16,32,2560]{3,2,1,0:T(8,128)(2,1)}, bf16[2,16,32,2560]{3,2,1,0:T(8,128)(2,1)}, bf16[2,10,16,16,512]{4,3,2,1,0:T(8,128)(2,1)}, f32[2,16,32,2560...) custom-call(f32[8,128]{1,0:T(8,128)} %get-tuple-element.64.sq, ...), custom_call_target="tpu_custom_call", output_to_operand_aliasing={{0}: (13, {}), {1}: (14, {}), {2}: (15, {}), {3}: (16, {}),... | custom-call | flops 884736000 | bytes 29491200 | tf_op jit(solution)/shard_map/adam/pallas_call | solution.py:522
  402.3 1.7 copy-done.3
  404.0 1.3 copy-done.5
  405.4 1.3 copy-done.7
  406.7 1.3 copy-done.9
  408.0 1.1 copy-done.11
  409.1 6.0 %adam.9 = (bf16[2,16,32,2560]{3,2,1,0:T(8,128)(2,1)}, bf16[2,16,32,2560]{3,2,1,0:T(8,128)(2,1)}, bf16[2,10,16,16,512]{4,3,2,1,0:T(8,128)(2,1)}, f32[2,16,32,2560...) custom-call(f32[8,128]{1,0:T(8,128)S(1)} %copy-done.12, ...), custom_call_target="tpu_custom_call", output_to_operand_aliasing={{0}: (9, {}), {1}: (10, {}), {2}: (11, {}), {3}: (12, {}), ... | custom-call | flops 589824000 | bytes 19660800 | tf_op jit(solution)/shard_map/adam/pallas_call | solution.py:522
  (25 shorter events, 0.0 us)
Async XLA Ops:
  264.6 23.1 %collective-permute-start = (bf16[20,96,256]{2,1,0:T(8,128)(2,1)}, bf16[20,96,256]{2,1,0:T(8,128)(2,1)S(1)}, u32[]{:S(2)}, u32[]{:S(2)}) collective-permute-start(bf16[20,96,256]{2,1,0:T(8,128)(2,1)} %get-tuple-element.65.refs_1_), channel_id=1, source_target_pairs={{0,1},{1,2},{2,3},{3,4},{4,5},{5,6},{6,7},{7,0},{8,9},{9,10},{10,1... | collective-permute-start | bytes 2949128 | tf_op jit(solution)/shard_map/ppermute | solution.py:566
  266.8 21.7 %collective-permute-start.4 = (bf16[20,96,256]{2,1,0:T(8,128)(2,1)}, bf16[20,96,256]{2,1,0:T(8,128)(2,1)S(1)}, u32[]{:S(2)}, u32[]{:S(2)}) collective-permute-start(bf16[20,96,256]{2,1,0:T(8,128)(2,1)} %get-tuple-element.66.refs_2_), channel_id=1, source_target_pairs={{0,7},{1,0},{2,1},{3,2},{4,3},{5,4},{6,5},{7,6},{8,15},{9,8},{10,9... | collective-permute-start | bytes 2949128 | tf_op jit(solution)/shard_map/ppermute | solution.py:567
  287.6 41.8 %copy-start.14 = (bf16[20,96,256]{2,1,0:T(8,128)(2,1)}, bf16[20,96,256]{2,1,0:T(8,128)(2,1)S(1)}, u32[]{:S(2)}) copy-start(bf16[20,96,256]{2,1,0:T(8,128)(2,1)S(1)} %collective-permute-done.refs_0_) | copy-start | bytes 2949124
  287.6 21.2 %collective-permute-start.1 = (bf16[20,96,256]{2,1,0:T(8,128)(2,1)S(1)}, bf16[20,96,256]{2,1,0:T(8,128)(2,1)S(1)}, u32[]{:S(2)}, u32[]{:S(2)}) collective-permute-start(bf16[20,96,256]{2,1,0:T(8,128)(2,1)S(1)} %collective-permute-done.refs_0_), channel_id=1, source_target_pairs={{0,1},{1,2},{2,3},{3,4},{4,5},{5,6},{6,7},{7,0},{8,9},{9,10},{10,1... | collective-permute-start | bytes 2949128 | tf_op jit(solution)/shard_map/ppermute | solution.py:566
  288.5 44.1 %copy-start.15 = (bf16[20,96,256]{2,1,0:T(8,128)(2,1)}, bf16[20,96,256]{2,1,0:T(8,128)(2,1)S(1)}, u32[]{:S(2)}) copy-start(bf16[20,96,256]{2,1,0:T(8,128)(2,1)S(1)} %collective-permute-done.4.refs_1_) | copy-start | bytes 2949124
  288.5 20.6 %collective-permute-start.5 = (bf16[20,96,256]{2,1,0:T(8,128)(2,1)S(1)}, bf16[20,96,256]{2,1,0:T(8,128)(2,1)S(1)}, u32[]{:S(2)}, u32[]{:S(2)}) collective-permute-start(bf16[20,96,256]{2,1,0:T(8,128)(2,1)S(1)} %collective-permute-done.4.refs_1_), channel_id=1, source_target_pairs={{0,7},{1,0},{2,1},{3,2},{4,3},{5,4},{6,5},{7,6},{8,15},{9,8},{10,9... | collective-permute-start | bytes 2949128 | tf_op jit(solution)/shard_map/ppermute | solution.py:567
  308.8 23.8 %copy-start.16 = (bf16[20,96,256]{2,1,0:T(8,128)(2,1)}, bf16[20,96,256]{2,1,0:T(8,128)(2,1)S(1)}, u32[]{:S(2)}) copy-start(bf16[20,96,256]{2,1,0:T(8,128)(2,1)S(1)} %collective-permute-done.1.refs_2_) | copy-start | bytes 2949124
  308.8 20.4 %collective-permute-start.2 = (bf16[20,96,256]{2,1,0:T(8,128)(2,1)S(1)}, bf16[20,96,256]{2,1,0:T(8,128)(2,1)}, u32[]{:S(2)}, u32[]{:S(2)}) collective-permute-start(bf16[20,96,256]{2,1,0:T(8,128)(2,1)S(1)} %collective-permute-done.1.refs_2_), channel_id=1, source_target_pairs={{0,1},{1,2},{2,3},{3,4},{4,5},{5,6},{6,7},{7,0},{8,9},{9,10},{10,1... | collective-permute-start | bytes 2949128 | tf_op jit(solution)/shard_map/ppermute | solution.py:566
  309.1 1.0 copy-start.13
  310.1 19.3 %collective-permute-start.6 = (bf16[20,96,256]{2,1,0:T(8,128)(2,1)S(1)}, bf16[20,96,256]{2,1,0:T(8,128)(2,1)}, u32[]{:S(2)}, u32[]{:S(2)}) collective-permute-start(bf16[20,96,256]{2,1,0:T(8,128)(2,1)S(1)} %collective-permute-done.5.refs_0_), channel_id=1, source_target_pairs={{0,7},{1,0},{2,1},{3,2},{4,3},{5,4},{6,5},{7,6},{8,15},{9,8},{10,9... | collective-permute-start | bytes 2949128 | tf_op jit(solution)/shard_map/ppermute | solution.py:567
  329.2 73.0 %collective-permute-start.3 = (bf16[20,96,256]{2,1,0:T(8,128)(2,1)}, bf16[20,96,256]{2,1,0:T(8,128)(2,1)}, u32[]{:S(2)}, u32[]{:S(2)}) collective-permute-start(bf16[20,96,256]{2,1,0:T(8,128)(2,1)} %collective-permute-done.2.refs_1_), channel_id=1, source_target_pairs={{0,1},{1,2},{2,3},{3,4},{4,5},{5,6},{6,7},{7,0},{8,9},{9,10},{10,1... | collective-permute-start | bytes 2949128 | tf_op jit(solution)/shard_map/ppermute | solution.py:566
  329.4 72.9 %collective-permute-start.7 = (bf16[20,96,256]{2,1,0:T(8,128)(2,1)}, bf16[20,96,256]{2,1,0:T(8,128)(2,1)}, u32[]{:S(2)}, u32[]{:S(2)}) collective-permute-start(bf16[20,96,256]{2,1,0:T(8,128)(2,1)} %collective-permute-done.6.refs_2_), channel_id=1, source_target_pairs={{0,7},{1,0},{2,1},{3,2},{4,3},{5,4},{6,5},{7,6},{8,15},{9,8},{10,9... | collective-permute-start | bytes 2949128 | tf_op jit(solution)/shard_map/ppermute | solution.py:567
  369.4 1.5 copy-start
  370.9 1.5 copy-start.2
  372.4 1.1 copy-start.4
  373.5 1.1 copy-start.6
  374.6 1.2 copy-start.8
  375.7 0.8 copy-start.10
  389.3 13.0 %copy-start.1 = (f32[4,2,32,2560]{3,2,1,0:T(8,128)S(1)}, f32[4,2,32,2560]{3,2,1,0:T(8,128)}, u32[]{:S(2)}) copy-start(f32[4,2,32,2560]{3,2,1,0:T(8,128)} %copy-done) | copy-start | bytes 7864324
  389.3 13.0 %copy-start.12 = (f32[8,128]{1,0:T(8,128)S(1)}, f32[8,128]{1,0:T(8,128)}, u32[]{:S(2)}) copy-start(f32[8,128]{1,0:T(8,128)} %get-tuple-element.64.sq) | copy-start | bytes 12292
  402.3 1.7 copy-start.3
  404.0 1.3 copy-start.5
  405.4 1.3 copy-start.7
  406.7 1.3 copy-start.9
  408.0 1.1 copy-start.11

commit v8 on v7

--- a/solution.py
+++ b/solution.py
@@ -97,7 +97,7 @@
     loop(4, norm_x)
     ACC[...] = jnp.zeros_like(ACC)
 
-    def forward(i):
+    def forward(i, turn):
         w_wait(2 * i)
         w_wait(2 * i + 1)
         w_start(2 * i + 2)
@@ -107,11 +107,14 @@
         g = dot(a, WGU[pair, :, 0 : 2 * FC])
         u = dot(a, WGU[pair, :, 2 * FC : 4 * FC])
         ACC[...] += dot((g * sigmoid(g) * u).astype(bf16), WD[pl.ds(2 * pair, 2)].reshape(2 * FC, d))
-        t = rows(lax.rem(i, 4))
-        DYT[:, t] = DY[t, :].T
-
+        if turn:
+            t = rows(lax.rem(i, 4))
+            DYT[:, t] = DY[t, :].T
+
+    forward(0, False)
     dy_in.wait()
-    loop(chunks // 2, forward)
+    loop(chunks // 2 - 1, lambda i: forward(i + 1, True))
+    assert chunks // 2 > 4
 
     def between(t):
         r = rows(t)
@@ -130,7 +133,7 @@
         return 2 * lax.rem(me + sign[h] * (1 + s) + 2 * n, n) + h
 
     def rs_copy(u, s, h):
-        return pltpu.make_async_remote_copy(PART.at[u, piece(s, h)], RECV.at[u, s, h], rs_s.at[u], rs_r.at[u, s],
+        return pltpu.make_async_remote_copy(PART.at[u, piece(s, h)], RECV.at[lax.rem(u, n), s, h], rs_s.at[u], rs_r.at[lax.rem(u, n), s],
                                             device_id=(rep, to[h]), device_id_type=MESH)
 
     def whole(ref, sem):
@@ -138,12 +141,12 @@
 
     def rs_take(u, s, h):
         p = piece(s + 1, h)
-        total = (PART[u, p].astype(f32) + RECV[u, s, h].astype(f32)).astype(bf16)
+        total = (PART[u, p].astype(f32) + RECV[lax.rem(u, n), s, h].astype(f32)).astype(bf16)
         PART[u, p] = total
         return total
 
     def rs_event(u, s):
-        whole(RECV.at[u, s - 1], rs_r.at[u, s - 1]).wait()
+        whole(RECV.at[0, 0], rs_r.at[lax.rem(u, n), s - 1]).wait()
 
         @pl.when(s < n - 1)
         def _():
@@ -292,7 +295,7 @@
     sq_copy_out = pltpu.make_async_copy(SQO, sq_out, own_sem.at[1])
 
     def finish(u):
-        whole(RECV.at[u], rs_s.at[u]).wait()
+        whole(RECV.at[0], rs_s.at[u]).wait()
 
     def finish_ag(g):
         ag_wait(g, rounds - 1)
@@ -302,7 +305,7 @@
     sq_copy_out.start()
     loop(groups, finish_ag)
     sq_copy_out.wait()
-    whole(RECV.at[:, 0], own_sem.at[0]).wait()
+    whole(PART.at[:, 0:2], own_sem.at[0]).wait()
     whole(SQA.at[1:n], sq_sem.at[0]).wait()
 
 
@@ -330,12 +333,12 @@
             pltpu.VMEM((SLOTS // 2, d, 4 * FC), bf16),
             pltpu.VMEM((SLOTS, FC, d), bf16),
             pltpu.VMEM((units, 2 * n) + part, bf16),
-            pltpu.VMEM((units, n - 1, 2) + part, bf16),
+            pltpu.VMEM((n, n - 1, 2) + part, bf16),
             pltpu.VMEM(part, f32),
             pltpu.VMEM((n, 8, 128), f32),
             pltpu.VMEM((8, 128), f32),
             dma((5,)), dma((SLOTS, 3)),
-            dma((units,)), dma((units, n - 1)), dma((units // JOINT,)), dma((units // JOINT, rounds)), dma((2,)), dma((2,)),
+            dma((units,)), dma((n, n - 1)), dma((units // JOINT,)), dma((units // JOINT, rounds)), dma((2,)), dma((2,)),
         ],
         compiler_params=pltpu.CompilerParams(collective_id=0, has_side_effects=True, vmem_limit_bytes=67043328),
         cost_estimate=pl.CostEstimate(flops=17 * 2 * tokens * d * ff, bytes_accessed=8 * units * n * rows * FC, transcendentals=0),

time: 421 us -> 419 us (level)
  no operation moved by 1% of the time
where the time goes in v8:
time: 419 us; the launch traced here: 414 us
  Pallas kernels  331 us (79%)
  waiting for transfers between devices  54.7 us (13%)
  local copies, waits for them, and re-layouts  14.9 us (4%)
  starting transfers between devices  12.3 us (3%)
    pallas_call x1, Pallas kernels, train(): pl.pallas_call(functools.partial(train_kernel, n, rounds), name='train',...  263 us
    pallas_call x5, Pallas kernels, adam(): pl.pallas_call(functools.partial(adam_kernel, n, count, sources, len(gs),...  64.4 us
    ppermute x4, waiting for transfers between devices, whole(): r = lax.ppermute(came[k][0], 'dp', right)  54.7 us
    unnamed x34, local copies, waits for them, and re-layouts  14.9 us
    ppermute x4, starting transfers between devices, whole(): came.append([r, lax.ppermute(came[k][1], 'dp', left)])  9.49 us
  transfers between devices with their start and end apart: 8, of which 3 were waited for; matrix products, arithmetic and copies ran while one was open for 0% of the time, Pallas kernels for 15%

profile of v8, /device:TPU:21, one launch (start us, length us, event | category | flops | bytes accessed | tf_op | source)
XLA Modules:
  0.0 413.9 jit_solution(17732811745416080649)
XLA Ops:
  0.6 262.6 %train.1 = (bf16[2,3,20,96,256]{4,3,2,1,0:T(8,128)(2,1)}, bf16[20,96,256]{2,1,0:T(8,128)(2,1)}, bf16[20,96,256]{2,1,0:T(8,128)(2,1)}, f32[8,128]{1,0:T(8,128)}) custom-call(bf16[1,2048,512]{2,1,0:T(8,128)(2,1)} %x.1, bf16[1,2048,512]{2,1,0:T(8,128)(2,1)} %dy.1, bf16[2,512,2560]{2,1,0:T(8,128)(2,1)} %wg_h.1, bf16[2,512,2560]{2,1,0:T(8,128)(2,1)} %wu_h.1, ...), custom_call_target="tpu_custom_call" | custom-call | flops 91268055040 | bytes 31457280 | tf_op jit(solution)/shard_map/train/pallas_call | solution.py:322
  263.2 2.2 collective-permute-start
  265.4 1.5 collective-permute-start.4
  266.8 19.5 %collective-permute-done.refs_0_ = bf16[20,96,256]{2,1,0:T(8,128)(2,1)S(1)} collective-permute-done((bf16[20,96,256]{2,1,0:T(8,128)(2,1)}, bf16[20,96,256]{2,1,0:T(8,128)(2,1)S(1)}, u32[]{:S(2)}, u32[]{:S(2)}) %collective-permute-start) | collective-permute-done | bytes 983072 | tf_op jit(solution)/shard_map/ppermute | solution.py:569
  286.3 0.6 collective-permute-start.1
  286.9 2.0 collective-permute-start.5
  289.0 18.5 %collective-permute-done.1.refs_2_ = bf16[20,96,256]{2,1,0:T(8,128)(2,1)S(1)} collective-permute-done((bf16[20,96,256]{2,1,0:T(8,128)(2,1)S(1)}, bf16[20,96,256]{2,1,0:T(8,128)(2,1)S(1)}, u32[]{:S(2)}, u32[]{:S(2)}) %collective-permute-start.1) | collective-permute-done | bytes 983072 | tf_op jit(solution)/shard_map/ppermute | solution.py:569
  307.5 0.0 collective-permute-start.2
  307.5 0.0 collective-permute-done.5.refs_0_
  307.5 1.0 copy-done.13
  308.5 2.6 collective-permute-start.6
  311.1 16.8 %collective-permute-done.2.refs_1_ = bf16[20,96,256]{2,1,0:T(8,128)(2,1)} collective-permute-done((bf16[20,96,256]{2,1,0:T(8,128)(2,1)S(1)}, bf16[20,96,256]{2,1,0:T(8,128)(2,1)}, u32[]{:S(2)}, u32[]{:S(2)}) %collective-permute-start.2) | collective-permute-done | bytes 983072 | tf_op jit(solution)/shard_map/ppermute | solution.py:569
  327.9 0.0 collective-permute-start.3
  327.9 0.0 collective-permute-done.6.refs_2_
  327.9 3.4 collective-permute-start.7
  331.3 16.3 %adam.5 = (bf16[2,16,32,2560]{3,2,1,0:T(8,128)(2,1)}, bf16[2,16,32,2560]{3,2,1,0:T(8,128)(2,1)}, bf16[2,10,16,16,512]{4,3,2,1,0:T(8,128)(2,1)}, f32[2,16,32,2560...) custom-call(f32[8,128]{1,0:T(8,128)} %get-tuple-element.64.sq, ...), custom_call_target="tpu_custom_call" | custom-call | flops 1179648000 | bytes 39321600 | tf_op jit(solution)/shard_map/adam/pallas_call | solution.py:525
  347.6 16.4 %adam.6 = (bf16[2,16,32,2560]{3,2,1,0:T(8,128)(2,1)}, bf16[2,16,32,2560]{3,2,1,0:T(8,128)(2,1)}, bf16[2,10,16,16,512]{4,3,2,1,0:T(8,128)(2,1)}, f32[2,16,32,2560...) custom-call(f32[8,128]{1,0:T(8,128)} %get-tuple-element.64.sq, ...), custom_call_target="tpu_custom_call", output_to_operand_aliasing={{0}: (13, {}), {1}: (14, {}), {2}: (15, {}), {3}: (16, {}),... | custom-call | flops 1179648000 | bytes 39321600 | tf_op jit(solution)/shard_map/adam/pallas_call | solution.py:525
  364.0 4.0 stage.1
  368.1 1.5 copy-done
  369.6 1.5 copy-done.2
  371.1 1.1 copy-done.4
  372.2 1.1 copy-done.6
  373.3 1.2 copy-done.8
  374.4 0.8 copy-done.10
  375.2 12.7 %adam.7 = (bf16[2,16,32,2560]{3,2,1,0:T(8,128)(2,1)}, bf16[2,16,32,2560]{3,2,1,0:T(8,128)(2,1)}, bf16[2,10,16,16,512]{4,3,2,1,0:T(8,128)(2,1)}, f32[2,16,32,2560...) custom-call(f32[8,128]{1,0:T(8,128)} %get-tuple-element.64.sq, ...), custom_call_target="tpu_custom_call", output_to_operand_aliasing={{0}: (13, {}), {1}: (14, {}), {2}: (15, {}), {3}: (16, {}),... | custom-call | flops 884736000 | bytes 29491200 | tf_op jit(solution)/shard_map/adam/pallas_call | solution.py:525
  388.0 12.9 %adam.8 = (bf16[2,16,32,2560]{3,2,1,0:T(8,128)(2,1)}, bf16[2,16,32,2560]{3,2,1,0:T(8,128)(2,1)}, bf16[2,10,16,16,512]{4,3,2,1,0:T(8,128)(2,1)}, f32[2,16,32,2560...) custom-call(f32[8,128]{1,0:T(8,128)} %get-tuple-element.64.sq, ...), custom_call_target="tpu_custom_call", output_to_operand_aliasing={{0}: (13, {}), {1}: (14, {}), {2}: (15, {}), {3}: (16, {}),... | custom-call | flops 884736000 | bytes 29491200 | tf_op jit(solution)/shard_map/adam/pallas_call | solution.py:525
  401.0 1.7 copy-done.3
  402.7 1.3 copy-done.5
  404.0 1.3 copy-done.7
  405.3 1.3 copy-done.9
  406.7 1.1 copy-done.11
  407.7 6.0 %adam.9 = (bf16[2,16,32,2560]{3,2,1,0:T(8,128)(2,1)}, bf16[2,16,32,2560]{3,2,1,0:T(8,128)(2,1)}, bf16[2,10,16,16,512]{4,3,2,1,0:T(8,128)(2,1)}, f32[2,16,32,2560...) custom-call(f32[8,128]{1,0:T(8,128)S(1)} %copy-done.12, ...), custom_call_target="tpu_custom_call", output_to_operand_aliasing={{0}: (9, {}), {1}: (10, {}), {2}: (11, {}), {3}: (12, {}), ... | custom-call | flops 589824000 | bytes 19660800 | tf_op jit(solution)/shard_map/adam/pallas_call | solution.py:525
  (25 shorter events, 0.0 us)
Async XLA Ops:
  263.2 23.1 %collective-permute-start = (bf16[20,96,256]{2,1,0:T(8,128)(2,1)}, bf16[20,96,256]{2,1,0:T(8,128)(2,1)S(1)}, u32[]{:S(2)}, u32[]{:S(2)}) collective-permute-start(bf16[20,96,256]{2,1,0:T(8,128)(2,1)} %get-tuple-element.65.refs_1_), channel_id=1, source_target_pairs={{0,1},{1,2},{2,3},{3,4},{4,5},{5,6},{6,7},{7,0},{8,9},{9,10},{10,1... | collective-permute-start | bytes 2949128 | tf_op jit(solution)/shard_map/ppermute | solution.py:569
  265.4 21.5 %collective-permute-start.4 = (bf16[20,96,256]{2,1,0:T(8,128)(2,1)}, bf16[20,96,256]{2,1,0:T(8,128)(2,1)S(1)}, u32[]{:S(2)}, u32[]{:S(2)}) collective-permute-start(bf16[20,96,256]{2,1,0:T(8,128)(2,1)} %get-tuple-element.66.refs_2_), channel_id=1, source_target_pairs={{0,7},{1,0},{2,1},{3,2},{4,3},{5,4},{6,5},{7,6},{8,15},{9,8},{10,9... | collective-permute-start | bytes 2949128 | tf_op jit(solution)/shard_map/ppermute | solution.py:570
  286.3 41.6 %copy-start.14 = (bf16[20,96,256]{2,1,0:T(8,128)(2,1)}, bf16[20,96,256]{2,1,0:T(8,128)(2,1)S(1)}, u32[]{:S(2)}) copy-start(bf16[20,96,256]{2,1,0:T(8,128)(2,1)S(1)} %collective-permute-done.refs_0_) | copy-start | bytes 2949124
  286.3 21.2 %collective-permute-start.1 = (bf16[20,96,256]{2,1,0:T(8,128)(2,1)S(1)}, bf16[20,96,256]{2,1,0:T(8,128)(2,1)S(1)}, u32[]{:S(2)}, u32[]{:S(2)}) collective-permute-start(bf16[20,96,256]{2,1,0:T(8,128)(2,1)S(1)} %collective-permute-done.refs_0_), channel_id=1, source_target_pairs={{0,1},{1,2},{2,3},{3,4},{4,5},{5,6},{6,7},{7,0},{8,9},{9,10},{10,1... | collective-permute-start | bytes 2949128 | tf_op jit(solution)/shard_map/ppermute | solution.py:569
  286.9 44.3 %copy-start.15 = (bf16[20,96,256]{2,1,0:T(8,128)(2,1)}, bf16[20,96,256]{2,1,0:T(8,128)(2,1)S(1)}, u32[]{:S(2)}) copy-start(bf16[20,96,256]{2,1,0:T(8,128)(2,1)S(1)} %collective-permute-done.4.refs_1_) | copy-start | bytes 2949124
  286.9 20.5 %collective-permute-start.5 = (bf16[20,96,256]{2,1,0:T(8,128)(2,1)S(1)}, bf16[20,96,256]{2,1,0:T(8,128)(2,1)S(1)}, u32[]{:S(2)}, u32[]{:S(2)}) collective-permute-start(bf16[20,96,256]{2,1,0:T(8,128)(2,1)S(1)} %collective-permute-done.4.refs_1_), channel_id=1, source_target_pairs={{0,7},{1,0},{2,1},{3,2},{4,3},{5,4},{6,5},{7,6},{8,15},{9,8},{10,9... | collective-permute-start | bytes 2949128 | tf_op jit(solution)/shard_map/ppermute | solution.py:570
  307.5 23.8 %copy-start.16 = (bf16[20,96,256]{2,1,0:T(8,128)(2,1)}, bf16[20,96,256]{2,1,0:T(8,128)(2,1)S(1)}, u32[]{:S(2)}) copy-start(bf16[20,96,256]{2,1,0:T(8,128)(2,1)S(1)} %collective-permute-done.1.refs_2_) | copy-start | bytes 2949124
  307.5 20.4 %collective-permute-start.2 = (bf16[20,96,256]{2,1,0:T(8,128)(2,1)S(1)}, bf16[20,96,256]{2,1,0:T(8,128)(2,1)}, u32[]{:S(2)}, u32[]{:S(2)}) collective-permute-start(bf16[20,96,256]{2,1,0:T(8,128)(2,1)S(1)} %collective-permute-done.1.refs_2_), channel_id=1, source_target_pairs={{0,1},{1,2},{2,3},{3,4},{4,5},{5,6},{6,7},{7,0},{8,9},{9,10},{10,1... | collective-permute-start | bytes 2949128 | tf_op jit(solution)/shard_map/ppermute | solution.py:569
  307.5 1.0 copy-start.13
  308.5 19.4 %collective-permute-start.6 = (bf16[20,96,256]{2,1,0:T(8,128)(2,1)S(1)}, bf16[20,96,256]{2,1,0:T(8,128)(2,1)}, u32[]{:S(2)}, u32[]{:S(2)}) collective-permute-start(bf16[20,96,256]{2,1,0:T(8,128)(2,1)S(1)} %collective-permute-done.5.refs_0_), channel_id=1, source_target_pairs={{0,7},{1,0},{2,1},{3,2},{4,3},{5,4},{6,5},{7,6},{8,15},{9,8},{10,9... | collective-permute-start | bytes 2949128 | tf_op jit(solution)/shard_map/ppermute | solution.py:570
  327.9 73.0 %collective-permute-start.3 = (bf16[20,96,256]{2,1,0:T(8,128)(2,1)}, bf16[20,96,256]{2,1,0:T(8,128)(2,1)}, u32[]{:S(2)}, u32[]{:S(2)}) collective-permute-start(bf16[20,96,256]{2,1,0:T(8,128)(2,1)} %collective-permute-done.2.refs_1_), channel_id=1, source_target_pairs={{0,1},{1,2},{2,3},{3,4},{4,5},{5,6},{6,7},{7,0},{8,9},{9,10},{10,1... | collective-permute-start | bytes 2949128 | tf_op jit(solution)/shard_map/ppermute | solution.py:569
  327.9 73.0 %collective-permute-start.7 = (bf16[20,96,256]{2,1,0:T(8,128)(2,1)}, bf16[20,96,256]{2,1,0:T(8,128)(2,1)}, u32[]{:S(2)}, u32[]{:S(2)}) collective-permute-start(bf16[20,96,256]{2,1,0:T(8,128)(2,1)} %collective-permute-done.6.refs_2_), channel_id=1, source_target_pairs={{0,7},{1,0},{2,1},{3,2},{4,3},{5,4},{6,5},{7,6},{8,15},{9,8},{10,9... | collective-permute-start | bytes 2949128 | tf_op jit(solution)/shard_map/ppermute | solution.py:570
  368.1 1.5 copy-start
  369.6 1.5 copy-start.2
  371.1 1.1 copy-start.4
  372.2 1.1 copy-start.6
  373.2 1.2 copy-start.8
  374.4 0.8 copy-start.10
  388.0 13.0 %copy-start.1 = (f32[4,2,32,2560]{3,2,1,0:T(8,128)S(1)}, f32[4,2,32,2560]{3,2,1,0:T(8,128)}, u32[]{:S(2)}) copy-start(f32[4,2,32,2560]{3,2,1,0:T(8,128)} %copy-done) | copy-start | bytes 7864324
  388.0 13.0 %copy-start.12 = (f32[8,128]{1,0:T(8,128)S(1)}, f32[8,128]{1,0:T(8,128)}, u32[]{:S(2)}) copy-start(f32[8,128]{1,0:T(8,128)} %get-tuple-element.64.sq) | copy-start | bytes 12292
  401.0 1.7 copy-start.3
  402.7 1.3 copy-start.5
  404.0 1.3 copy-start.7
  405.3 1.3 copy-start.9
  406.7 1.1 copy-start.11
